TPU v7x, 256 devices: a 4x2x16 block of a 4x16x16 slice. The times are simulated.
256 devices in a mesh: rep: 2 (over y), seq: 128 (over z, x, core).
Axes of the slice: x: 4, y: 2, z: 16, core: 2. Of those that a mesh axis runs over, the one named last changes fastest.
The devices are a block of a 4x16x16 slice.
Arguments:
- latents: bfloat16 [16, 196608], P(None, ('rep', 'seq')), parts along dimension 1, may hold values from -6 to 6
- layout: int32 [256, 768], P('rep'), parts along dimension 0, may hold values from 0 to 98303, as said below
- assign: int32 [16], P('rep'), parts along dimension 0, may hold values from 0 to 7, as said below
- counts: int32 [16], P('rep'), parts along dimension 0, may hold values from 1 to 3
- latent_cache: bfloat16 [2, 1024, 1024], P(None, ('rep', 'seq')), parts along dimension 1, may hold values from -6 to 6
- feature_cache: bfloat16 [2, 1024, 64, 384], P(None, ('rep', 'seq')), parts along dimension 1, may hold values from -4 to 4
- first_weight: bfloat16 [3, 3, 3, 16, 384], replicated, may hold values from -0.3125 to 0.3125
- first_bias: float32 [384], replicated, may hold values from -3 to 3
- norm_gain: float32 [384], replicated, may hold values from 0.25 to 1.75
- second_weight: bfloat16 [3, 3, 3, 384, 192], replicated, may hold values from -0.0625 to 0.0625
- second_bias: float32 [192], replicated, may hold values from -3 to 3
Outputs:
- decoded_frames: bfloat16 [3, 2048, 128, 192], P(None, ('rep', 'seq')), parts along dimension 1
- latent_cache_next: bfloat16 [2, 1024, 1024], P(None, ('rep', 'seq')), parts along dimension 1
- feature_cache_next: bfloat16 [2, 1024, 64, 384], P(None, ('rep', 'seq')), parts along dimension 1
There are 2 independent parts, one for each index of `rep`. A program takes and returns all parts, laid end to end along the dimension named above; an argument that names none is the same for every part. Nothing has to cross between parts.
Inputs may be any that keep to these rules, and one draw needn't show every extreme that they name: assign is a permutation of 0 to 7. layout is a permutation of 0 to 98303. Call the cells of request assign[g], rows k * 4 to (k + 1) * 4 - 1, all frames and columns, the tile of seq index (g * 16 + k - 8) mod 128; every row of layout holds exactly 6 cells of every tile.
All inputs are finite; a program needn't handle non-finite values.
Results may differ from a plain program's by a relative error of at most 0.0034.
Values may be sent and summed in bfloat16 or wider, within the bound.
A program may use at most 128 MiB of HBM per device.

v0:
```python
import jax
import jax.numpy as jnp
from jax import lax
from jax.sharding import PartitionSpec as P

LAT_CH = 16
REQS = 8
FMAX = 3
ROWS_DEV = 4
W = 64


def padded_2(array, sides, width):
    for axis, dim in sides:
        devices, length = (lax.axis_size(axis), array.shape[dim])
        up = [(i, (i + 1) % devices) for i in range(devices)]
        down = [(j, i) for i, j in up]
        last = lax.slice_in_dim(array, length - width, length, axis=dim)
        first = lax.slice_in_dim(array, 0, width, axis=dim)
        before = lax.ppermute(last, axis, up)
        after = lax.ppermute(first, axis, down)
        array = jnp.concatenate([before, array, after], axis=dim)
    return array


def tile_numbers(layout, assign, per_group, devices):
    height = ROWS_DEV * per_group
    offset = per_group // 2
    tile_cells = FMAX * ROWS_DEV * W
    column = layout % W
    remain = layout // W
    image_row = remain % height
    remain = remain // height
    frame_index = remain % FMAX
    request = remain // FMAX
    group_ranks = jnp.arange(REQS, dtype=jnp.int32)
    group_index = jnp.sum(jnp.where(assign == request[..., None], group_ranks, 0), axis=-1)
    place = group_index * per_group + image_row // ROWS_DEV
    target = (place - offset + devices) % devices
    within = (frame_index * ROWS_DEV + image_row % ROWS_DEV) * W + column
    return target * tile_cells + within


def keep_rows(values, rim_width, position, height):
    row_index = position * ROWS_DEV - rim_width + jnp.arange(values.shape[1], dtype=jnp.int32)
    inside = (row_index >= 0) & (row_index < height)
    return jnp.where(inside[None, :, None, None], values, jnp.zeros((), values.dtype))


def causal_conv(values, weight, offset):
    result = lax.conv_general_dilated(
        values[None],
        weight,
        (1, 1, 1),
        ((0, 0), (0, 0), (1, 1)),
        dimension_numbers=("NDHWC", "DHWIO", "NDHWC"),
        preferred_element_type=jnp.float32,
    )
    return result[0] + offset


def activate(linear, norm_gain):
    inverse = lax.rsqrt(jnp.mean(linear * linear, axis=-1, keepdims=True) + 1e-06)
    return jax.nn.silu(linear * inverse * norm_gain).astype(jnp.bfloat16)


def body(
    latents,
    layout,
    assign,
    counts,
    latent_cache,
    feature_cache,
    first_weight,
    first_bias,
    norm_gain,
    second_weight,
    second_bias,
):
    devices = lax.axis_size("seq")
    myself = lax.axis_index("seq")
    per_group = devices // REQS
    offset = per_group // 2
    height = ROWS_DEV * per_group
    tile_cells = FMAX * ROWS_DEV * W
    per_peer = tile_cells // devices
    numbers = tile_numbers(layout, assign, per_group, devices)
    own_numbers = lax.dynamic_index_in_dim(numbers, myself, 0, keepdims=False)
    sending_order = jnp.argsort(own_numbers)
    outgoing = jnp.take(latents, sending_order, axis=1).reshape(LAT_CH, devices, per_peer)
    incoming = lax.all_to_all(outgoing, "seq", split_axis=1, concat_axis=1, tiled=True)
    arrived = lax.dynamic_slice_in_dim(jnp.sort(numbers, axis=1), myself * per_peer, per_peer, 1)
    placing = jnp.argsort((arrived - myself * tile_cells).reshape(-1))
    arranged = jnp.take(incoming.reshape(LAT_CH, tile_cells), placing, axis=1)
    window = jnp.transpose(arranged.reshape(LAT_CH, FMAX, ROWS_DEV, W), (1, 2, 3, 0))
    place = (myself + offset) % devices
    position = place % per_group
    request = jnp.take(assign, place // per_group)
    live_frames = jnp.take(counts, request)
    first_input = jnp.concatenate([latent_cache.reshape(2, ROWS_DEV, W, LAT_CH), window], axis=0)
    padded = keep_rows(padded_2(first_input, (("seq", 1),), 2), 2, position, height)
    widened = activate(causal_conv(padded, first_weight, first_bias), norm_gain)
    cached = padded_2(feature_cache, (("seq", 1),), 1)
    extended = keep_rows(jnp.concatenate([cached, widened], axis=0), 1, position, height)
    second_input = extended[:, 1:-1]
    doubled = jnp.repeat(jnp.repeat(extended, 2, axis=1)[:, 1:-1], 2, axis=2)
    decoded = causal_conv(doubled, second_weight, second_bias)
    frame_index = jnp.arange(FMAX, dtype=jnp.int32)[:, None, None, None]
    decoded_frames = jnp.where(frame_index < live_frames, decoded, 0.0).astype(jnp.bfloat16)
    latent_next = lax.dynamic_slice_in_dim(first_input, live_frames, 2, 0).reshape(
        2, ROWS_DEV, W * LAT_CH
    )
    feature_next = lax.dynamic_slice_in_dim(second_input, live_frames, 2, 0)
    return (decoded_frames, latent_next, feature_next)


def solution(mesh):
    return jax.shard_map(
        body,
        mesh=mesh,
        in_specs=(
            P(None, ("rep", "seq")),
            P("rep", None),
            P("rep"),
            P("rep"),
            P(None, ("rep", "seq"), None),
            P(None, ("rep", "seq"), None, None),
            P(),
            P(),
            P(),
            P(),
            P(),
        ),
        out_specs=(
            P(None, ("rep", "seq"), None, None),
            P(None, ("rep", "seq"), None),
            P(None, ("rep", "seq"), None, None),
        ),
        check_vma=False,
    )
```

profile of v0, /device:TPU:40, one launch (start us, length us, event | category | flops | bytes accessed | tf_op | source)
XLA Modules:
  0.0 162.3 jit_solution(7621123937541215728)
XLA Ops:
  7.2 0.0 copy-start
  7.2 0.1 sort.43.cloned.1.call-start
  7.3 1.8 %add_select_fusion.6 = s32[128,768]{1,0:T(8,128)S(1)} fusion(s32[128,768]{1,0:T(8,128)} %param.14), kind=kLoop, calls=%fused_computation.42 | loop fusion | flops 3735552 | bytes 786432 | tf_op jit(solution)/shard_map/jit(floor_divide)/jit(_where)/select_n | solution.py:35
  9.1 0.0 copy-start.10
  9.1 1.8 %select_reduce_fusion = s32[128,768]{1,0:T(8,128)S(1)} fusion(s32[128,768]{1,0:T(8,128)S(1)} %add_select_fusion.6, s32[8]{0:T(128)} %param.15), kind=kLoop, calls=%fused_computation.14 | loop fusion | flops 2260992 | bytes 786464 | tf_op jit(solution)/shard_map/reduce_sum | solution.py:37
  10.9 3.2 %fusion.28 = s32[128,768]{1,0:T(8,128)} fusion(s32[128,768]{1,0:T(8,128)S(1)} %select_reduce_fusion, s32[128,768]{1,0:T(8,128)} %param.14), kind=kLoop, calls=%fused_computation.56 | loop fusion | flops 8159232 | bytes 1179648 | tf_op jit(solution)/shard_map/add | solution.py:41
  14.1 0.1 sort.43.cloned.1.call-update
  14.1 0.8 dynamic-slice_reduce_fusion
  14.9 4.4 %sort.39 = (s32[768]{0:T(1024)}, s32[768]{0:T(1024)S(1)}) sort(s32[768]{0:T(1024)S(1)} %dynamic-slice_reduce_fusion, s32[768]{0:T(1024)S(1)} %iota.27), dimensions={0}, to_apply=%region_1.2 | sort | flops 7680 | bytes 12288 | tf_op jit(solution)/shard_map/jit(argsort)/sort | solution.py:89
  19.3 0.2 copy.86
  19.5 1.9 %gather_fusion = bf16[768,16]{1,0:T(8,128)(2,1)S(1)} fusion(bf16[16,768]{0,1:T(8,128)(2,1)S(1)} %copy.86, s32[1024]{0:T(1024)S(1)} %pad_clamp_fusion.1), kind=kCustom, calls=%fused_computation.clone | custom fusion | bytes 52224 | tf_op jit(solution)/shard_map/jit(_take)/gather | solution.py:90
  21.4 0.2 select_bitcast_fusion.1
  21.6 0.8 reshape.109
  22.3 32.2 %all-to-all-start = ((bf16[16,128,6]{0,2,1:T(8,128)(2,1)}), bf16[16,128,6]{0,2,1:T(8,128)(2,1)S(1)}, u32[]{:S(2)}, u32[]{:S(2)}) async-start(bf16[16,128,6]{0,2,1:T(8,128)(2,1)} %reshape.109), calls=%async_computation | async-start | bytes 524288 | tf_op jit(solution)/shard_map/all_to_all | solution.py:91
  54.5 0.3 copy.83
  54.8 1.0 fusion.49
  55.8 5.1 %collective-permute-start.1 = (bf16[2,1,64,384]{3,1,2,0:T(2,128)(2,1)}, bf16[2,1,64,384]{3,1,2,0:T(2,128)(2,1)}, u32[]{:S(2)}, u32[]{:S(2)}) collective-permute-start(bf16[2,1,64,384]{3,1,2,0:T(2,128)(2,1)} %get-tuple-element.46), channel_id=1, source_target_pairs={{1,0},{2,1},{3,2},{4,3},{5,4},{6,5},{7,6},{8,7},{9,8},{10,9},{11,1... | collective-permute-start | bytes 294920 | tf_op jit(solution)/shard_map/ppermute | solution.py:21
  60.9 0.7 dynamic-slice.4
  62.3 0.7 dynamic-slice.5
  63.7 0.1 reshape.108
  63.8 0.1 copy.88
  64.0 9.0 %all-to-all-done = bf16[16,128,6]{0,2,1:T(8,128)(2,1)S(1)} async-done(((bf16[16,128,6]{0,2,1:T(8,128)(2,1)}), bf16[16,128,6]{0,2,1:T(8,128)(2,1)S(1)}, u32[]{:S(2)}, u32[]{:S(2)}) %all-to-all-start) | async-done | bytes 24608 | tf_op jit(solution)/shard_map/all_to_all | solution.py:91
  73.0 0.1 reshape.110
  73.1 0.0 sort.43.cloned.1.call-done
  73.2 1.0 dynamic-slice_subtract_fusion
  74.2 0.1 reshape.111
  74.3 4.4 %sort.41 = (s32[768]{0:T(1024)}, s32[768]{0:T(1024)S(1)}) sort(s32[768]{0:T(1024)S(1)} %reshape.111, s32[768]{0:T(1024)S(1)} %iota.28), dimensions={0}, to_apply=%region_3.5 | sort | flops 7680 | bytes 12288 | tf_op jit(solution)/shard_map/jit(argsort)/sort | solution.py:93
  78.7 1.9 %gather_fusion.1 = bf16[768,16]{1,0:T(8,128)(2,1)S(1)} fusion(bf16[16,768]{0,1:T(8,128)(2,1)S(1)} %reshape.110, s32[1024]{0:T(1024)S(1)} %pad_clamp_fusion), kind=kCustom, calls=%fused_computation.1.clone | custom fusion | bytes 52224 | tf_op jit(solution)/shard_map/jit(_take)/gather | solution.py:94
  80.6 0.2 broadcast_select_fusion
  80.8 0.1 copy.87
  81.0 0.1 collective-permute-start.2
  81.1 5.0 %collective-permute-start.3 = (bf16[5,2,64,16]{2,3,1,0:T(8,128)(2,1)S(1)}, bf16[5,2,64,16]{2,3,1,0:T(8,128)(2,1)S(1)}, u32[]{:S(2)}, u32[]{:S(2)}) collective-permute-start(bf16[5,2,64,16]{2,3,1,0:T(8,128)(2,1)S(1)} %get-tuple-element.48), channel_id=1, source_target_pairs={{1,0},{2,1},{3,2},{4,3},{5,4},{6,5},{7,6},{8,7},{9,8},{10,9},{11,1... | collective-permute-start | bytes 61448 | tf_op jit(solution)/shard_map/ppermute | solution.py:21
  86.2 0.0 copy-start.12
  86.2 0.1 copy.99
  86.3 0.8 reshape.114
  87.1 0.7 collective-permute-done.2
  87.9 0.4 copy.89
  88.3 0.1 select_bitcast_fusion
  88.4 0.1 pad.4
  88.5 0.1 copy.91
  88.7 1.8 %convolution_select_fusion = f32[3,6,8,9,384]{4,2,3,1,0:T(8,128)S(1)} fusion(bf16[3,3,3,16,384]{4,3,2,1,0:T(8,128)(2,1)S(1)} %copy-done, pred[8,9]{0,1:T(8,128)(4,1)S(1)} %copy-done.12, bf16[5,8,1,7,2,16]{5,3,4,1,0,2:T(8,128)(2,1)S(1)} %slice.48, bf16[5,8,1,8,9,16]{5,3,4,1,0,2:T(8,128)(2,1)S(1)} %copy.91), kind=kOutput, calls=%fused_computation.24 | convolution fusion | flops 430817280 | bytes 2432584 | tf_op jit(solution)/shard_map/conv_general_dilated | solution.py:51
  90.6 0.5 copy.92
  91.1 0.2 copy-done.5
  91.2 0.4 multiply_reduce_fusion
  91.6 0.1 copy.93
  91.7 0.1 copy.94
  91.8 0.7 multiply_convert_fusion
  92.6 2.0 %maximum_select_fusion = bf16[5,6,64,384]{3,1,2,0:T(8,128)(2,1)S(1)} fusion(bf16[3,6,64,384]{3,1,2,0:T(8,128)(2,1)S(1)} %multiply_convert_fusion, bf16[2,1,64,384]{3,1,2,0:T(2,128)(2,1)} %collective-permute-done.1, bf16[2,4,64,384]{3,1,2,0:T(4,128)(2,1)S(1)} %copy.83, bf16[2,1,64,384]{3,1,2,0:T(2,128)(2,1)} %collective-permute-done, ...), kind=kLoop, calls=%fused_computation.20 | loop fusion | flops 6635520 | bytes 2949126 | tf_op jit(solution)/shard_map/jit(_where)/select_n | solution.py:47
  94.7 0.5 slice.53
  95.2 0.3 copy.95
  95.5 0.1 constant_dynamic-slice_fusion
  95.6 0.8 copy.101
  96.4 0.5 broadcast_in_dim.85
  96.9 0.3 slice.50
  97.2 4.4 %broadcast_in_dim.86 = bf16[5,10,64,2,384]{4,3,2,1,0:T(2,128)(2,1)} broadcast(bf16[5,10,64,384]{3,2,1,0:T(8,128)(2,1)S(1)} %slice.50), dimensions={0,1,2,4} | broadcast | bytes 7372800 | tf_op jit(solution)/shard_map/broadcast_in_dim | solution.py:106
  101.6 11.0 %reshape.191 = bf16[5,10,1,128,384]{4,3,1,0,2:T(8,128)(2,1)} reshape(bf16[5,10,64,2,384]{4,3,2,1,0:T(2,128)(2,1)} %broadcast_in_dim.86) | data formatting | bytes 9830400 | tf_op jit(solution)/shard_map/broadcast_in_dim;reshape | solution.py:52
  112.6 7.3 %pad.6 = bf16[5,10,1,136,384]{4,3,1,0,2:T(8,128)(2,1)} pad(bf16[5,10,1,128,384]{4,3,1,0,2:T(8,128)(2,1)} %reshape.191, bf16[]{:T(256)} %constant.179.clone.1), padding=0_0x0_0x0_0x1_7x0_0 | pad | bytes 10137602 | tf_op jit(solution)/shard_map/broadcast_in_dim;reshape | solution.py:52
  119.9 8.9 %reshape.166 = bf16[5,10,1,8,17,384]{5,4,3,1,0,2:T(8,128)(2,1)} reshape(bf16[5,10,1,136,384]{4,3,1,0,2:T(8,128)(2,1)} %pad.6) | data formatting | bytes 10444800 | tf_op jit(solution)/shard_map/conv_general_dilated | solution.py:51
  128.8 4.1 %copy.97 = bf16[5,10,1,8,17,384]{5,3,4,1,0,2:T(8,128)(2,1)S(1)} copy(bf16[5,10,1,8,17,384]{5,4,3,1,0,2:T(8,128)(2,1)} %reshape.166) | data formatting | bytes 10444800 | tf_op jit(solution)/shard_map/conv_general_dilated | solution.py:51
  133.0 0.2 slice.51
  133.2 18.6 %fusion.13 = f32[3,8,8,17,192]{4,2,3,1,0:T(8,128)S(1)} fusion(bf16[3,3,3,384,192]{3,4,2,1,0:T(8,128)(2,1)S(1)} %copy-done.9, bf16[5,10,1,7,2,384]{5,3,4,1,0,2:T(8,128)(2,1)S(1)} %slice.51, bf16[5,10,1,8,17,384]{5,3,4,1,0,2:T(8,128)(2,1)S(1)} %copy.97, pred[8,17]{0,1:T(8,128)(4,1)S(1)} %copy-done.11), kind=kOutput, calls=%fused_computation.21 | convolution fusion | flops 13013139456 | bytes 12248200 | tf_op jit(solution)/shard_map/conv_general_dilated | solution.py:51
  151.8 1.1 copy.98
  152.9 0.6 fusion.10
  153.6 1.8 %copy.100 = bf16[3,8,128,192]{2,3,1,0:T(8,128)(2,1)} copy(bf16[3,8,128,192]{3,1,2,0:T(8,128)(2,1)S(1)} %fusion.10) | data formatting | bytes 2359296
  (43 shorter events, 0.3 us)
Async XLA Ops:
  7.2 81.5 %copy-start = (bf16[3,3,3,16,384]{4,3,2,1,0:T(8,128)(2,1)S(1)}, bf16[3,3,3,16,384]{4,3,2,1,0:T(8,128)(2,1)}, u32[]{:S(2)}) copy-start(bf16[3,3,3,16,384]{4,3,2,1,0:T(8,128)(2,1)} %param.19) | copy-start | bytes 995332
  7.2 12.1 %copy-start.3 = (bf16[16,768]{1,0:T(8,128)(2,1)S(1)}, bf16[16,768]{1,0:T(8,128)(2,1)}, u32[]{:S(2)}) copy-start(bf16[16,768]{1,0:T(8,128)(2,1)} %param.13) | copy-start | bytes 73732
  7.2 47.3 %copy-start.2 = (bf16[2,4,64,384]{3,2,1,0:T(8,128)(2,1)S(1)}, bf16[2,4,64,384]{3,2,1,0:T(8,128)(2,1)}, u32[]{:S(2)}) copy-start(bf16[2,4,64,384]{3,2,1,0:T(8,128)(2,1)} %param.18) | copy-start | bytes 1179652
  7.2 65.9 %sort.43.cloned.1.call-start = ((), (), s32[]{:S(2)}) async-start(), calls=%async_computation.1 | async-start | bytes 1179680 | tf_op jit(solution)/shard_map/jit(sort)/sort | solution.py:92
  9.1 51.9 %copy-start.8 = (s32[8]{0:T(128)S(1)}, s32[8]{0:T(128)}, u32[]{:S(2)}) copy-start(s32[8]{0:T(128)} %param.15) | copy-start | bytes 100
  9.1 53.2 %copy-start.10 = (s32[8]{0:T(128)S(1)}, s32[8]{0:T(128)}, u32[]{:S(2)}) copy-start(s32[8]{0:T(128)} %param.16) | copy-start | bytes 100
  9.1 54.6 %copy-start.4 = (bf16[2,4,1024]{2,1,0:T(4,128)(2,1)S(1)}, bf16[2,4,1024]{2,1,0:T(4,128)(2,1)}, u32[]{:S(2)}) copy-start(bf16[2,4,1024]{2,1,0:T(4,128)(2,1)} %param.17) | copy-start | bytes 49156
  22.3 50.7 %all-to-all-start = ((bf16[16,128,6]{0,2,1:T(8,128)(2,1)}), bf16[16,128,6]{0,2,1:T(8,128)(2,1)S(1)}, u32[]{:S(2)}, u32[]{:S(2)}) async-start(bf16[16,128,6]{0,2,1:T(8,128)(2,1)} %reshape.109), calls=%async_computation | async-start | bytes 524288 | tf_op jit(solution)/shard_map/all_to_all | solution.py:91
  55.8 36.8 %collective-permute-start = (bf16[2,1,64,384]{3,1,2,0:T(2,128)(2,1)}, bf16[2,1,64,384]{3,1,2,0:T(2,128)(2,1)}, u32[]{:S(2)}, u32[]{:S(2)}) collective-permute-start(bf16[2,1,64,384]{3,1,2,0:T(2,128)(2,1)} %get-tuple-element.45), channel_id=1, source_target_pairs={{0,1},{1,2},{2,3},{3,4},{4,5},{5,6},{6,7},{7,8},{8,9},{9,10},{10,1... | collective-permute-start | bytes 294920 | tf_op jit(solution)/shard_map/ppermute | solution.py:20
  55.8 36.8 %collective-permute-start.1 = (bf16[2,1,64,384]{3,1,2,0:T(2,128)(2,1)}, bf16[2,1,64,384]{3,1,2,0:T(2,128)(2,1)}, u32[]{:S(2)}, u32[]{:S(2)}) collective-permute-start(bf16[2,1,64,384]{3,1,2,0:T(2,128)(2,1)} %get-tuple-element.46), channel_id=1, source_target_pairs={{1,0},{2,1},{3,2},{4,3},{5,4},{6,5},{7,6},{8,7},{9,8},{10,9},{11,1... | collective-permute-start | bytes 294920 | tf_op jit(solution)/shard_map/ppermute | solution.py:21
  81.0 6.9 %collective-permute-start.2 = (bf16[5,2,64,16]{2,3,1,0:T(8,128)(2,1)S(1)}, bf16[5,2,64,16]{2,3,1,0:T(8,128)(2,1)S(1)}, u32[]{:S(2)}, u32[]{:S(2)}) collective-permute-start(bf16[5,2,64,16]{2,3,1,0:T(8,128)(2,1)S(1)} %get-tuple-element.47), channel_id=1, source_target_pairs={{0,1},{1,2},{2,3},{3,4},{4,5},{5,6},{6,7},{7,8},{8,9},{9,10},{10,1... | collective-permute-start | bytes 61448 | tf_op jit(solution)/shard_map/ppermute | solution.py:20
  81.1 6.7 %collective-permute-start.3 = (bf16[5,2,64,16]{2,3,1,0:T(8,128)(2,1)S(1)}, bf16[5,2,64,16]{2,3,1,0:T(8,128)(2,1)S(1)}, u32[]{:S(2)}, u32[]{:S(2)}) collective-permute-start(bf16[5,2,64,16]{2,3,1,0:T(8,128)(2,1)S(1)} %get-tuple-element.48), channel_id=1, source_target_pairs={{1,0},{2,1},{3,2},{4,3},{5,4},{6,5},{7,6},{8,7},{9,8},{10,9},{11,1... | collective-permute-start | bytes 61448 | tf_op jit(solution)/shard_map/ppermute | solution.py:21
  86.2 2.5 %copy-start.12 = (pred[8,9]{0,1:T(8,128)(4,1)S(1)}, pred[8,9]{0,1:T(8,128)(4,1)}, u32[]{:S(2)}) copy-start(pred[8,9]{0,1:T(8,128)(4,1)} %constant.232) | copy-start | bytes 220
  90.5 0.7 copy-start.5
  90.6 1.3 copy-start.6
  128.8 4.3 %copy-start.9 = (bf16[3,3,3,384,192]{3,4,2,1,0:T(8,128)(2,1)S(1)}, bf16[3,3,3,384,192]{3,4,2,1,0:T(8,128)(2,1)}, u32[]{:S(2)}) copy-start(bf16[3,3,3,384,192]{3,4,2,1,0:T(8,128)(2,1)} %param.22) | copy-start | bytes 11943940
  128.8 4.3 %copy-start.11 = (pred[8,17]{0,1:T(8,128)(4,1)S(1)}, pred[8,17]{0,1:T(8,128)(4,1)}, u32[]{:S(2)}) copy-start(pred[8,17]{0,1:T(8,128)(4,1)} %constant.231) | copy-start | bytes 412
  151.8 1.1 copy-start.7
  152.9 2.5 %copy-start.1 = (bf16[3,3,3,16,384]{4,3,2,1,0:T(8,128)(2,1)S(1)}, bf16[3,3,3,16,384]{4,3,2,1,0:T(8,128)(2,1)}, u32[]{:S(2)}) copy-start(bf16[3,3,3,16,384]{4,3,2,1,0:T(8,128)(2,1)} %param.19) | copy-start | bytes 995332
Sparse Core Ops, SparseCore 0:
  14.3 15.0 sort.45.cloned.1.call-done
  (1 shorter events, 0.0 us)
where the time goes:
time: 164 us; the launch traced here: 162 us
  local copies, waits for them, and re-layouts  52.7 us (32%)
  starting transfers between devices  42.4 us (26%)
  other arithmetic  20.9 us (13%)
  matrix products  20.5 us (12%)
  between operations  16 us (10%)
  waiting for transfers between devices  9.77 us (6%)
    all_to_all x1, starting transfers between devices, body(): lax.all_to_all(outgoing, 'seq', split_axis=1, concat_axis=1, tiled=True)  32.2 us
    conv_general_dilated x2, matrix products, causal_conv(): lax.conv_general_dilated(values[None], weight, (1, 1, 1), ((0, 0), (0, 0)...  20.5 us
    another operation x2, local copies, waits for them, and re-layouts, causal_conv(): values[None]  18.3 us
    conv_general_dilated x7, local copies, waits for them, and re-layouts, causal_conv(): lax.conv_general_dilated(values[None], weight, (1, 1, 1), ((0, 0), (0, 0)...  14.9 us
    ppermute x2, starting transfers between devices, padded_2(): after = lax.ppermute(first, axis, down)  10.1 us
    all_to_all x1, waiting for transfers between devices, body(): lax.all_to_all(outgoing, 'seq', split_axis=1, concat_axis=1, tiled=True)  9.04 us
    broadcast_in_dim x2, local copies, waits for them, and re-layouts, body(): doubled = jnp.repeat(jnp.repeat(extended, 2, axis=1)[:, 1:-1], 2, axis=2)  4.91 us
    sort x1, other arithmetic, body(): sending_order = jnp.argsort(own_numbers)  4.37 us
  transfers between devices with their start and end apart: 5, of which 2 were waited for; matrix products, arithmetic and copies ran while one was open for 10% of the time, Pallas kernels for 0%

commit v1 on v0

--- a/solution.py
+++ b/solution.py
@@ -1,6 +1,8 @@
 import jax
 import jax.numpy as jnp
 from jax import lax
+from jax.experimental import pallas as pl
+from jax.experimental.pallas import tpu as pltpu
 from jax.sharding import PartitionSpec as P
 
 LAT_CH = 16
@@ -8,6 +10,8 @@
 FMAX = 3
 ROWS_DEV = 4
 W = 64
+MID_CH = 384
+OUT_CH = 192
 
 
 def padded_2(array, sides, width):
@@ -47,21 +51,151 @@
     return jnp.where(inside[None, :, None, None], values, jnp.zeros((), values.dtype))
 
 
-def causal_conv(values, weight, offset):
-    result = lax.conv_general_dilated(
-        values[None],
-        weight,
-        (1, 1, 1),
-        ((0, 0), (0, 0), (1, 1)),
-        dimension_numbers=("NDHWC", "DHWIO", "NDHWC"),
-        preferred_element_type=jnp.float32,
-    )
-    return result[0] + offset
-
-
-def activate(linear, norm_gain):
-    inverse = lax.rsqrt(jnp.mean(linear * linear, axis=-1, keepdims=True) + 1e-06)
-    return jax.nn.silu(linear * inverse * norm_gain).astype(jnp.bfloat16)
+def decode_kernel(
+    live_ref, place_ref, xt_ref, w1_ref, b1_ref, gain_ref, fc_ref, top_ref, bot_ref, w2_hbm, b2_ref,
+    out_ref, fn_ref, w2_ref, wc_ref, xs_ref, h_ref, ob_ref, sem,
+):
+    live = live_ref[0]
+    place = place_ref[0]
+    last = place_ref[1]
+    load = pltpu.make_async_copy(w2_hbm, w2_ref, sem)
+    load.start()
+    f32, bf16 = jnp.float32, jnp.bfloat16
+    rows, mid = ROWS_DEV + 2, MID_CH
+    xt = xt_ref[...].astype(f32)
+    lanes = xt.shape[1]
+    column = lax.broadcasted_iota(jnp.int32, xt.shape, 1) % W
+    shifted = (
+        jnp.where(column == 0, 0.0, pltpu.roll(xt, 1, 1)),
+        xt,
+        jnp.where(column == W - 1, 0.0, pltpu.roll(xt, lanes - 1, 1)),
+    )
+    per_frame = (ROWS_DEV + 4) * W
+    for e in range(3):
+        odd = pltpu.roll(shifted[e], lanes - W, 1).astype(bf16)
+        even = shifted[e].astype(bf16)
+        for b in range(3):
+            source, start = ((even, 0), (odd, 0), (even, 2 * W))[b]
+            for a in range(3):
+                k = ((a * 3 + b) * 3 + e) * LAT_CH
+                for t in range(FMAX):
+                    at = (t + a) * per_frame + start
+                    xs_ref[k : k + LAT_CH, t * rows * W : (t + 1) * rows * W] = source[:, at : at + rows * W]
+    cells = rows * W
+    row = lax.broadcasted_iota(jnp.int32, (cells, mid), 0)
+    first_column = (row % W) == 0
+    last_column = (row % W) == W - 1
+    outside = jnp.logical_or(
+        jnp.logical_and(row < W, place == 0),
+        jnp.logical_and(row >= cells - W, place == last),
+    )
+
+    def spread(frame, values):
+        before = jnp.where(first_column, 0.0, pltpu.roll(values, 1, 0)).astype(bf16)
+        after = jnp.where(last_column, 0.0, pltpu.roll(values, cells - 1, 0)).astype(bf16)
+        here = values.astype(bf16)
+        h_ref[0, frame, :, 0:mid] = before
+        h_ref[0, frame, :, mid : 2 * mid] = here
+        h_ref[1, frame, :, 0:mid] = here
+        h_ref[1, frame, :, mid : 2 * mid] = after
+
+    for frame in range(2):
+        values = jnp.concatenate(
+            [top_ref[frame], fc_ref[frame], bot_ref[frame]], axis=0
+        ).astype(f32)
+        spread(frame, jnp.where(outside, 0.0, values))
+    bias = b1_ref[...]
+    gain = gain_ref[...]
+    for t in range(FMAX):
+        pre = lax.dot_general(
+            xs_ref[:, t * cells : (t + 1) * cells],
+            w1_ref[...],
+            (((0,), (0,)), ((), ())),
+            preferred_element_type=f32,
+        ) + bias
+        inverse = lax.rsqrt(jnp.mean(pre * pre, axis=1, keepdims=True) + 1e-06)
+        v = pre * inverse * gain
+        half = 0.5 * v
+        spread(2 + t, jnp.where(outside, 0.0, half + half * jnp.tanh(half)))
+    own = slice(W, W + ROWS_DEV * W)
+    for j in range(2):
+        one = h_ref[1, 1 + j, own, 0:mid]
+        two = h_ref[1, 2 + j, own, 0:mid]
+        three = h_ref[1, 3 + j, own, 0:mid]
+        fn_ref[j] = jnp.where(live == 1, one.astype(f32), jnp.where(live == 2, two.astype(f32), three.astype(f32))).astype(bf16)
+    load.wait()
+    near = (((0,), (1, 2)), ((0, 1), (2,)))
+
+    @pl.loop(0, 3)
+    def _(a):
+        base = a * 9
+        tap = [[w2_ref[base + b * 3 + e].astype(f32) for e in range(3)] for b in range(3)]
+        for py in range(2):
+            for dy in range(2):
+                taps = [sum(tap[b][e] for b in near[py][dy]) for e in range(3)]
+                for px in range(2):
+                    for dx in range(2):
+                        total = sum(taps[e] for e in near[px][dx])
+                        wc_ref[py * 2 + px, a * 2 + dy, dx * mid : (dx + 1) * mid, 0:OUT_CH] = total.astype(bf16)
+
+    bias2 = b2_ref[...]
+    block = ROWS_DEV * W
+    for py in range(2):
+        for px in range(2):
+            total = None
+            for a in range(3):
+                for dy in range(2):
+                    at = (py + dy) * W
+                    left = h_ref[px, a : a + FMAX, at : at + block, :].reshape(FMAX * block, 2 * mid)
+                    part = jnp.dot(left, wc_ref[py * 2 + px, a * 2 + dy], preferred_element_type=f32)
+                    total = part if total is None else total + part
+            total = (total + bias2).reshape(FMAX, ROWS_DEV, W, 256)
+            for t in range(FMAX):
+                kept = jnp.where(t < live, total[t], 0.0)
+                for part in range(2):
+                    ob_ref[part, t, :, pl.ds(px, W, stride=2), :] = kept[:, :, part * 128 : (part + 1) * 128]
+        for t in range(FMAX):
+            for y in range(ROWS_DEV):
+                out_ref[t, 2 * y + py, :, 0:128] = ob_ref[0, t, y].astype(bf16)
+                out_ref[t, 2 * y + py, :, 128:OUT_CH] = ob_ref[1, t, y, :, 0 : OUT_CH - 128].astype(bf16)
+
+
+def decode(live, place, last, window, first_weight, first_bias, norm_gain, feature_cache, above, below, second_weight, second_bias):
+    rows = ROWS_DEV + 2
+    vm = pl.BlockSpec(memory_space=pltpu.VMEM)
+    sm = pl.BlockSpec(memory_space=pltpu.SMEM)
+    f32, bf16 = jnp.float32, jnp.bfloat16
+    return pl.pallas_call(
+        decode_kernel,
+        out_shape=(
+            jax.ShapeDtypeStruct((FMAX, 2 * ROWS_DEV, 2 * W, OUT_CH), bf16),
+            jax.ShapeDtypeStruct((2, ROWS_DEV * W, MID_CH), bf16),
+        ),
+        in_specs=[sm, sm, vm, vm, vm, vm, vm, vm, vm, pl.BlockSpec(memory_space=pl.ANY), vm],
+        out_specs=(vm, vm),
+        scratch_shapes=[
+            pltpu.VMEM((27, MID_CH, OUT_CH), bf16),
+            pltpu.VMEM((4, 6, 2 * MID_CH, 256), bf16),
+            pltpu.VMEM((27 * LAT_CH, FMAX * rows * W), bf16),
+            pltpu.VMEM((2, 5, rows * W, 2 * MID_CH), bf16),
+            pltpu.VMEM((2, FMAX, ROWS_DEV, 2 * W, 128), f32),
+            pltpu.SemaphoreType.DMA,
+        ],
+        compiler_params=pltpu.CompilerParams(vmem_limit_bytes=60 * 1024 * 1024),
+        cost_estimate=pl.CostEstimate(flops=6_200_000_000, bytes_accessed=7_000_000, transcendentals=442368),
+    )(
+        jnp.reshape(live, (1,)).astype(jnp.int32),
+        jnp.stack([place, last]).astype(jnp.int32),
+        window,
+        first_weight.reshape(27 * LAT_CH, MID_CH),
+        first_bias.reshape(1, MID_CH),
+        norm_gain.reshape(1, MID_CH),
+        feature_cache.reshape(2, ROWS_DEV * W, MID_CH),
+        above.reshape(2, W, MID_CH),
+        below.reshape(2, W, MID_CH),
+        second_weight.reshape(27, MID_CH, OUT_CH),
+        jnp.pad(second_bias, (0, 256 - OUT_CH)).reshape(1, 256),
+    )
 
 
 def body(
@@ -99,18 +233,19 @@
     live_frames = jnp.take(counts, request)
     first_input = jnp.concatenate([latent_cache.reshape(2, ROWS_DEV, W, LAT_CH), window], axis=0)
     padded = keep_rows(padded_2(first_input, (("seq", 1),), 2), 2, position, height)
-    widened = activate(causal_conv(padded, first_weight, first_bias), norm_gain)
-    cached = padded_2(feature_cache, (("seq", 1),), 1)
-    extended = keep_rows(jnp.concatenate([cached, widened], axis=0), 1, position, height)
-    second_input = extended[:, 1:-1]
-    doubled = jnp.repeat(jnp.repeat(extended, 2, axis=1)[:, 1:-1], 2, axis=2)
-    decoded = causal_conv(doubled, second_weight, second_bias)
-    frame_index = jnp.arange(FMAX, dtype=jnp.int32)[:, None, None, None]
-    decoded_frames = jnp.where(frame_index < live_frames, decoded, 0.0).astype(jnp.bfloat16)
+    ring = lax.axis_size("seq")
+    up = [(i, (i + 1) % ring) for i in range(ring)]
+    above = lax.ppermute(feature_cache[:, -1], "seq", up)
+    below = lax.ppermute(feature_cache[:, 0], "seq", [(j, i) for i, j in up])
+    cells = jnp.transpose(padded, (3, 0, 1, 2)).reshape(LAT_CH, -1)
+    decoded_frames, feature_next = decode(
+        live_frames, position, per_group - 1, cells, first_weight, first_bias, norm_gain,
+        feature_cache, above, below, second_weight, second_bias,
+    )
+    feature_next = feature_next.reshape(2, ROWS_DEV, W, MID_CH)
     latent_next = lax.dynamic_slice_in_dim(first_input, live_frames, 2, 0).reshape(
         2, ROWS_DEV, W * LAT_CH
     )
-    feature_next = lax.dynamic_slice_in_dim(second_input, live_frames, 2, 0)
     return (decoded_frames, latent_next, feature_next)
 
 

time: 164 us -> 120 us (0.73)
  local copies, waits for them, and re-layouts: 52.7 us -> 23.4 us
  matrix products: 20.5 us -> 0 us
  Pallas kernels: 0 us -> 14.8 us
  waiting for transfers between devices: 9.77 us -> 5.02 us
  other arithmetic: 20.9 us -> 17.5 us
    ppermute x0 -> x2, starting transfers between devices: none -> 24.6 us  [the longest x1 24.6 us: body(): below = lax.ppermute(feature_cache[:, 0], 'seq', [(j, i) for i, j in up])]
    conv_general_dilated x2 -> x0, matrix products: 20.5 us -> none  [causal_conv(): lax.conv_general_dilated(values[None], weight, (1, 1, 1), ((0, 0), (0, 0)...]
    all_to_all x1, starting transfers between devices: 32.2 us -> 12.1 us  [body(): lax.all_to_all(outgoing, 'seq', split_axis=1, concat_axis=1, tiled=True)]
    another operation x2 -> x0, local copies, waits for them, and re-layouts: 18.3 us -> none  [causal_conv(): values[None]]
    conv_general_dilated x7 -> x0, local copies, waits for them, and re-layouts: 14.9 us -> none  [causal_conv(): lax.conv_general_dilated(values[None], weight, (1, 1, 1), ((0, 0), (0, 0)...]
    pallas_call x0 -> x1, Pallas kernels: none -> 14.8 us  [decode(): pl.pallas_call(decode_kernel, out_shape=(jax.ShapeDtypeStruct((FMAX, 2 *...]
    unnamed x31 -> x22, local copies, waits for them, and re-layouts: 3.39 us -> 11.6 us
    ppermute x2 -> x1, starting transfers between devices: 10.1 us -> 5.04 us  [padded_2(): after = lax.ppermute(first, axis, down)]
  transfers between devices with their start and end apart: 5 -> 5, of which waited for: 2 -> 2; matrix products, arithmetic and copies ran while one was open for 10% -> 31% of each run, Pallas kernels for 0% -> 0%
where the time goes in v1:
time: 120 us; the launch traced here: 119 us
  starting transfers between devices  42.1 us (35%)
  local copies, waits for them, and re-layouts  23.4 us (20%)
  other arithmetic  17.5 us (15%)
  between operations  15.8 us (13%)
  Pallas kernels  14.8 us (12%)
  waiting for transfers between devices  5.02 us (4%)
    ppermute x1, starting transfers between devices, body(): below = lax.ppermute(feature_cache[:, 0], 'seq', [(j, i) for i, j in up])  24.6 us
    pallas_call x1, Pallas kernels, decode(): pl.pallas_call(decode_kernel, out_shape=(jax.ShapeDtypeStruct((FMAX, 2 *...  14.8 us
    all_to_all x1, starting transfers between devices, body(): lax.all_to_all(outgoing, 'seq', split_axis=1, concat_axis=1, tiled=True)  12.1 us
    unnamed x22, local copies, waits for them, and re-layouts  11.6 us
    ppermute x1, starting transfers between devices, padded_2(): after = lax.ppermute(first, axis, down)  5.04 us
    sort x1, other arithmetic, body(): sending_order = jnp.argsort(own_numbers)  4.37 us
    sort x1, other arithmetic, body(): placing = jnp.argsort((arrived - myself * tile_cells).reshape(-1))  4.37 us
    all_to_all x1, waiting for transfers between devices, body(): lax.all_to_all(outgoing, 'seq', split_axis=1, concat_axis=1, tiled=True)  4.28 us
  transfers between devices with their start and end apart: 5, of which 2 were waited for; matrix products, arithmetic and copies ran while one was open for 31% of the time, Pallas kernels for 0%

profile of v1, /device:TPU:40, one launch (start us, length us, event | category | flops | bytes accessed | tf_op | source)
XLA Modules:
  0.0 118.5 jit_solution(9585137365123194245)
XLA Ops:
  7.2 0.0 copy-start.5
  7.2 0.0 copy-start
  7.2 0.0 copy-start.8
  7.2 0.0 copy-start.2
  7.2 0.0 copy-start.3
  7.2 0.0 copy-start.1
  7.2 0.1 sort.43.cloned.1.call-start
  7.3 1.0 slice_bitcast_fusion
  8.3 24.6 %collective-permute-start.3 = (bf16[2,64,384]{2,1,0:T(8,128)(2,1)S(1)}, bf16[2,64,384]{2,1,0:T(8,128)(2,1)S(1)}, u32[]{:S(2)}, u32[]{:S(2)}) collective-permute-start(bf16[2,64,384]{2,1,0:T(8,128)(2,1)S(1)} %get-tuple-element.46), channel_id=1, source_target_pairs={{1,0},{2,1},{3,2},{4,3},{5,4},{6,5},{7,6},{8,7},{9,8},{10,9},{11,1... | collective-permute-start | bytes 294920 | tf_op jit(solution)/shard_map/ppermute | solution.py:239
  32.9 0.0 collective-permute-start.2
  32.9 1.7 %add_select_fusion.6 = s32[128,768]{1,0:T(8,128)S(1)} fusion(s32[128,768]{1,0:T(8,128)} %param.14), kind=kLoop, calls=%fused_computation.14 | loop fusion | flops 3735552 | bytes 786432 | tf_op jit(solution)/shard_map/jit(floor_divide)/jit(_where)/select_n | solution.py:39
  34.6 1.8 %select_reduce_fusion = s32[128,768]{1,0:T(8,128)S(1)} fusion(s32[128,768]{1,0:T(8,128)S(1)} %add_select_fusion.6, s32[8]{0:T(128)} %param.15), kind=kLoop, calls=%fused_computation.2 | loop fusion | flops 2260992 | bytes 786464 | tf_op jit(solution)/shard_map/reduce_sum | solution.py:41
  36.4 3.2 %fusion.4 = s32[128,768]{1,0:T(8,128)} fusion(s32[128,768]{1,0:T(8,128)S(1)} %select_reduce_fusion, s32[128,768]{1,0:T(8,128)} %param.14), kind=kLoop, calls=%fused_computation.27 | loop fusion | flops 8159232 | bytes 1179648 | tf_op jit(solution)/shard_map/add | solution.py:45
  39.6 0.1 sort.43.cloned.1.call-update
  39.6 0.8 dynamic-slice_reduce_fusion
  40.4 4.4 %sort.39 = (s32[768]{0:T(1024)}, s32[768]{0:T(1024)S(1)}) sort(s32[768]{0:T(1024)S(1)} %dynamic-slice_reduce_fusion, s32[768]{0:T(1024)S(1)} %iota.15), dimensions={0}, to_apply=%region_1.2 | sort | flops 7680 | bytes 12288 | tf_op jit(solution)/shard_map/jit(argsort)/sort | solution.py:223
  44.8 0.0 copy-done
  44.8 0.2 copy.37
  45.0 1.9 %gather_fusion = bf16[768,16]{1,0:T(8,128)(2,1)S(1)} fusion(bf16[16,768]{0,1:T(8,128)(2,1)S(1)} %copy.37, s32[1024]{0:T(1024)S(1)} %pad_clamp_fusion.1), kind=kCustom, calls=%fused_computation.clone | custom fusion | bytes 52224 | tf_op jit(solution)/shard_map/jit(_take)/gather | solution.py:224
  46.9 0.2 select_bitcast_fusion
  47.1 0.8 reshape.69
  47.8 12.1 %all-to-all-start = ((bf16[16,128,6]{0,2,1:T(8,128)(2,1)}), bf16[16,128,6]{0,2,1:T(8,128)(2,1)S(1)}, u32[]{:S(2)}, u32[]{:S(2)}) async-start(bf16[16,128,6]{0,2,1:T(8,128)(2,1)} %reshape.69), calls=%async_computation | async-start | bytes 524288 | tf_op jit(solution)/shard_map/all_to_all | solution.py:225
  60.0 0.0 copy-done.5
  60.0 0.7 dynamic-slice.4
  61.4 0.0 copy-done.8
  61.4 0.7 dynamic-slice.5
  62.8 0.0 copy-done.2
  62.8 0.6 reshape.75.b1_ref
  63.4 0.0 copy-done.3
  63.4 0.6 reshape.76.gain_ref
  64.0 0.0 copy-done.1
  64.0 0.1 reshape.68
  64.1 0.1 copy.39
  64.2 0.0 copy-start.4
  64.2 8.2 %copy.43 = bf16[3,3,3,384,192]{4,3,2,1,0:T(8,128)(2,1)} copy(bf16[3,3,3,384,192]{3,4,2,1,0:T(8,128)(2,1)} %param.22) | data formatting | bytes 7962624 | tf_op args[9]
  72.4 0.0 copy-done.4
  72.4 0.5 pad.4
  73.0 0.6 pad_add_fusion.place_ref
  73.5 4.3 %all-to-all-done = bf16[16,128,6]{0,2,1:T(8,128)(2,1)S(1)} async-done(((bf16[16,128,6]{0,2,1:T(8,128)(2,1)}), bf16[16,128,6]{0,2,1:T(8,128)(2,1)S(1)}, u32[]{:S(2)}, u32[]{:S(2)}) %all-to-all-start) | async-done | bytes 24608 | tf_op jit(solution)/shard_map/all_to_all | solution.py:225
  77.8 0.1 reshape.70
  77.9 0.0 sort.43.cloned.1.call-done
  78.0 1.0 dynamic-slice_subtract_fusion
  79.0 0.1 reshape.71
  79.1 4.4 %sort.41 = (s32[768]{0:T(1024)}, s32[768]{0:T(1024)S(1)}) sort(s32[768]{0:T(1024)S(1)} %reshape.71, s32[768]{0:T(1024)S(1)} %iota.16), dimensions={0}, to_apply=%region_3.5 | sort | flops 7680 | bytes 12288 | tf_op jit(solution)/shard_map/jit(argsort)/sort | solution.py:227
  83.5 1.9 %gather_fusion.1 = bf16[768,16]{1,0:T(8,128)(2,1)S(1)} fusion(bf16[16,768]{0,1:T(8,128)(2,1)S(1)} %reshape.70, s32[1024]{0:T(1024)S(1)} %pad_clamp_fusion), kind=kCustom, calls=%fused_computation.1.clone | custom fusion | bytes 52224 | tf_op jit(solution)/shard_map/jit(_take)/gather | solution.py:228
  85.4 0.2 broadcast_select_fusion
  85.6 0.1 copy.38
  85.7 0.3 collective-permute-start
  86.0 5.0 %collective-permute-start.1 = (bf16[5,2,64,16]{2,3,1,0:T(8,128)(2,1)S(1)}, bf16[5,2,64,16]{2,3,1,0:T(8,128)(2,1)S(1)}, u32[]{:S(2)}, u32[]{:S(2)}) collective-permute-start(bf16[5,2,64,16]{2,3,1,0:T(8,128)(2,1)S(1)} %get-tuple-element.49), channel_id=1, source_target_pairs={{1,0},{2,1},{3,2},{4,3},{5,4},{6,5},{7,6},{8,7},{9,8},{10,9},{11,1... | collective-permute-start | bytes 61448 | tf_op jit(solution)/shard_map/ppermute | solution.py:25
  91.1 0.1 copy.44
  91.2 0.8 reshape.80
  92.0 0.7 collective-permute-done
  92.8 0.0 collective-permute-done.1
  92.8 0.1 fusion.15
  92.9 0.8 reshape.73.xt_ref
  93.7 0.0 collective-permute-done.3.bot_ref
  93.7 0.0 copy-start.6
  93.7 0.0 collective-permute-done.2.top_ref
  93.7 0.0 copy-start.7
  93.7 0.6 copy-done.6
  94.3 0.0 copy-done.7
  94.4 14.8 %shard_map.130 = (bf16[3,8,128,192]{3,2,1,0:T(8,128)(2,1)}, bf16[2,256,384]{2,1,0:T(8,128)(2,1)}) custom-call(s32[1]{0:T(128)} %select_n.114.live_ref, s32[2]{0:T(128)} %pad_add_fusion.place_ref, bf16[16,2560]{1,0:T(8,128)(2,1)} %reshape.73.xt_ref, bf16[432,384]{1,0:T(8,128)(2,1)} %bitcast.41, f32[1,384]{1,0:T(1,128)} %reshape.75.b1_ref, ...), custom_call_target="tpu_custom_call" | custom-call | flops 6200000000 | bytes 7000000 | tf_op jit(solution)/shard_map/pallas_call | solution.py:168
  109.2 2.5 %copy.45 = bf16[3,8,128,192]{2,3,1,0:T(8,128)(2,1)} copy(bf16[3,8,128,192]{3,2,1,0:T(8,128)(2,1)} %get-tuple-element.43) | data formatting | bytes 2359296
  (12 shorter events, 0.1 us)
Async XLA Ops:
  7.2 52.8 %copy-start.5 = (s32[8]{0:T(128)S(1)}, s32[8]{0:T(128)}, u32[]{:S(2)}) copy-start(s32[8]{0:T(128)} %param.15) | copy-start | bytes 100
  7.2 37.6 %copy-start = (bf16[16,768]{1,0:T(8,128)(2,1)S(1)}, bf16[16,768]{1,0:T(8,128)(2,1)}, u32[]{:S(2)}) copy-start(bf16[16,768]{1,0:T(8,128)(2,1)} %param.13) | copy-start | bytes 73732
  7.2 54.2 %copy-start.8 = (s32[8]{0:T(128)S(1)}, s32[8]{0:T(128)}, u32[]{:S(2)}) copy-start(s32[8]{0:T(128)} %param.16) | copy-start | bytes 100
  7.2 55.5 %copy-start.2 = (f32[384]{0:T(512)S(1)}, f32[384]{0:T(512)}, u32[]{:S(2)}) copy-start(f32[384]{0:T(512)} %param.20) | copy-start | bytes 4612
  7.2 56.1 %copy-start.3 = (f32[384]{0:T(512)S(1)}, f32[384]{0:T(512)}, u32[]{:S(2)}) copy-start(f32[384]{0:T(512)} %param.21) | copy-start | bytes 4612
  7.2 56.7 %copy-start.1 = (bf16[2,4,1024]{2,1,0:T(4,128)(2,1)S(1)}, bf16[2,4,1024]{2,1,0:T(4,128)(2,1)}, u32[]{:S(2)}) copy-start(bf16[2,4,1024]{2,1,0:T(4,128)(2,1)} %param.17) | copy-start | bytes 49156
  7.2 70.7 %sort.43.cloned.1.call-start = ((), (), s32[]{:S(2)}) async-start(), calls=%async_computation.1 | async-start | bytes 1179680 | tf_op jit(solution)/shard_map/jit(sort)/sort | solution.py:226
  8.3 85.4 %collective-permute-start.3 = (bf16[2,64,384]{2,1,0:T(8,128)(2,1)S(1)}, bf16[2,64,384]{2,1,0:T(8,128)(2,1)S(1)}, u32[]{:S(2)}, u32[]{:S(2)}) collective-permute-start(bf16[2,64,384]{2,1,0:T(8,128)(2,1)S(1)} %get-tuple-element.46), channel_id=1, source_target_pairs={{1,0},{2,1},{3,2},{4,3},{5,4},{6,5},{7,6},{8,7},{9,8},{10,9},{11,1... | collective-permute-start | bytes 294920 | tf_op jit(solution)/shard_map/ppermute | solution.py:239
  32.9 60.8 %collective-permute-start.2 = (bf16[2,64,384]{2,1,0:T(8,128)(2,1)S(1)}, bf16[2,64,384]{2,1,0:T(8,128)(2,1)S(1)}, u32[]{:S(2)}, u32[]{:S(2)}) collective-permute-start(bf16[2,64,384]{2,1,0:T(8,128)(2,1)S(1)} %get-tuple-element.47), channel_id=1, source_target_pairs={{0,1},{1,2},{2,3},{3,4},{4,5},{5,6},{6,7},{7,8},{8,9},{9,10},{10,1... | collective-permute-start | bytes 294920 | tf_op jit(solution)/shard_map/ppermute | solution.py:238
  47.8 30.0 %all-to-all-start = ((bf16[16,128,6]{0,2,1:T(8,128)(2,1)}), bf16[16,128,6]{0,2,1:T(8,128)(2,1)S(1)}, u32[]{:S(2)}, u32[]{:S(2)}) async-start(bf16[16,128,6]{0,2,1:T(8,128)(2,1)} %reshape.69), calls=%async_computation | async-start | bytes 524288 | tf_op jit(solution)/shard_map/all_to_all | solution.py:225
  64.2 8.2 %copy-start.4 = (f32[192]{0:T(256)S(1)}, f32[192]{0:T(256)}, u32[]{:S(2)}) copy-start(f32[192]{0:T(256)} %param.23) | copy-start | bytes 2308
  85.7 7.0 %collective-permute-start = (bf16[5,2,64,16]{2,3,1,0:T(8,128)(2,1)S(1)}, bf16[5,2,64,16]{2,3,1,0:T(8,128)(2,1)S(1)}, u32[]{:S(2)}, u32[]{:S(2)}) collective-permute-start(bf16[5,2,64,16]{2,3,1,0:T(8,128)(2,1)S(1)} %get-tuple-element.48), channel_id=1, source_target_pairs={{0,1},{1,2},{2,3},{3,4},{4,5},{5,6},{6,7},{7,8},{8,9},{9,10},{10,1... | collective-permute-start | bytes 61448 | tf_op jit(solution)/shard_map/ppermute | solution.py:24
  86.0 6.7 %collective-permute-start.1 = (bf16[5,2,64,16]{2,3,1,0:T(8,128)(2,1)S(1)}, bf16[5,2,64,16]{2,3,1,0:T(8,128)(2,1)S(1)}, u32[]{:S(2)}, u32[]{:S(2)}) collective-permute-start(bf16[5,2,64,16]{2,3,1,0:T(8,128)(2,1)S(1)} %get-tuple-element.49), channel_id=1, source_target_pairs={{1,0},{2,1},{3,2},{4,3},{5,4},{6,5},{7,6},{8,7},{9,8},{10,9},{11,1... | collective-permute-start | bytes 61448 | tf_op jit(solution)/shard_map/ppermute | solution.py:25
  93.7 0.6 copy-start.6
  93.7 0.7 copy-start.7
Sparse Core Ops, SparseCore 0:
  39.8 15.0 sort.45.cloned.1.call-done
  (1 shorter events, 0.0 us)

commit v2 on v1

v2 whole, which is shorter than its diff:
```python
import functools

import jax
import jax.numpy as jnp
from jax import lax
from jax.experimental import pallas as pl
from jax.experimental.pallas import tpu as pltpu
from jax.sharding import PartitionSpec as P

LAT_CH = 16
MID_CH = 384
OUT_CH = 192
REQS = 8
FMAX = 3
ROWS_DEV = 4
W = 64


def counted_before(marks, earlier):
    size = earlier.shape[0]
    carry = jnp.zeros((marks.shape[0], 1), jnp.float32)
    parts = []
    for start in range(0, marks.shape[1], size):
        block = marks[:, start : start + size]
        parts.append(jnp.dot(block.astype(jnp.bfloat16), earlier, preferred_element_type=jnp.float32) + carry)
        carry = carry + jnp.sum(block, axis=1, keepdims=True)
    return jnp.concatenate(parts, axis=1)


def gather_kernel(
    devices, assign_ref, layout_ref, latents_ref, cache_ref, features_ref,
    window_ref, above_ref, below_ref,
    send1_ref, recv1_ref, send2_ref, recv2_ref, table_ref, rim_out_ref, rim_in_ref,
    plane_ok, far_ok, s1, r1, s2, r2, sf, rf, sh, rh,
):
    f32, bf16, i32 = jnp.float32, jnp.bfloat16, jnp.int32
    per_group = devices // REQS
    plane = per_group // 2
    planes = devices // plane
    tile = ROWS_DEV * W
    tile_cells = FMAX * tile
    per_peer = tile_cells // devices
    rep, me = lax.axis_index("rep"), lax.axis_index("seq")
    z, p = me // plane, me % plane
    even = p % 2 == 0
    ahead, behind = (me + 1) % devices, (me + devices - 1) % devices
    first, final = p == 0, p == plane - 1

    def signal(semaphore, device):
        pl.semaphore_signal(semaphore, inc=1, device_id=(rep, device), device_id_type=pl.DeviceIdType.MESH)

    barrier = pltpu.get_barrier_semaphore()
    for q in range(0, plane, 2):
        @pl.when(p != q)
        def _():
            signal(barrier, z * plane + q)
    for i in range(1, planes):
        signal(barrier, ((z + i) % planes) * plane + (p // 2) * 2 + 1)

    @pl.when(final)
    def _():
        signal(barrier, ahead)

    @pl.when(first)
    def _():
        signal(barrier, behind)

    row_of = lax.broadcasted_iota(i32, (tile_cells // 3, tile_cells // 3), 0)
    lane_of = lax.broadcasted_iota(i32, (tile_cells // 3, tile_cells // 3), 1)
    earlier = (row_of < lane_of).astype(bf16)
    own = layout_ref[pl.ds(me, 1), :]
    request = ((own // (ROWS_DEV * per_group * W)) * 43) // 128
    group = jnp.zeros_like(own)
    for g in range(REQS):
        group = group + jnp.where(assign_ref[g] == request, g, 0)
    place = group * per_group + (own // tile) % per_group
    target = (place + devices - per_group // 2) % devices
    line = (target % plane) * planes + target // plane
    hit = lax.broadcasted_iota(i32, (devices, tile_cells), 0) == line
    marks = hit.astype(f32)
    order = counted_before(marks, earlier)
    latents = latents_ref[...]
    rows = []
    for k in range(per_peer):
        chosen = jnp.where(order == k, marks, 0.0).astype(bf16)
        rows.append(lax.dot_general(latents, chosen, (((1,), (1,)), ((), ())), preferred_element_type=f32))
    rows.append(jnp.zeros((devices - per_peer * LAT_CH, devices), f32))
    send1_ref[...] = jnp.transpose(jnp.concatenate(rows, axis=0)).astype(bf16).reshape(plane, planes, devices)

    @pl.when(even)
    def _():
        pl.semaphore_wait(barrier, plane - 1 + jnp.where(first, 1, 0))
        signal(plane_ok, me + 1)

    @pl.when(jnp.logical_not(even))
    def _():
        pl.semaphore_wait(plane_ok, 1)

    near = []
    for i in range(1, plane):
        q = (p + i) % plane
        near.append(pltpu.make_async_remote_copy(
            src_ref=send1_ref.at[q], dst_ref=recv1_ref.at[p], send_sem=s1.at[i], recv_sem=r1.at[i],
            device_id=(rep, z * plane + q), device_id_type=pl.DeviceIdType.MESH))
        near[-1].start()
    recv1_ref[p] = send1_ref[p]

    my_place = (me + per_group // 2) % devices
    my_group, position = my_place // per_group, my_place % per_group
    frame = ROWS_DEV * per_group * W
    offset = layout_ref[...] - (assign_ref[my_group] * (FMAX * frame) + position * tile)
    inside = jnp.logical_and(jnp.logical_and(offset >= 0, offset < FMAX * frame), (offset & (frame - tile)) == 0)
    within = ((offset // frame) * tile + (offset & (tile - 1))).astype(f32)
    marks = inside.astype(f32)
    order = counted_before(marks, earlier)
    spot = lax.broadcasted_iota(i32, (devices, tile_cells), 1).astype(f32)
    for k in range(per_peer):
        chosen = jnp.logical_and(order == k, inside)
        home = jnp.sum(jnp.where(chosen, within, 0.0), axis=1, keepdims=True)
        table_ref[k * devices : (k + 1) * devices, :] = (home == spot).astype(bf16)

    for copy in near:
        copy.wait()
    to = lax.broadcasted_iota(i32, (devices, devices), 0)
    source = lax.broadcasted_iota(i32, (devices, devices), 1)
    turn = (source == (to % plane) * planes + to // plane).astype(bf16)
    turned = jnp.dot(turn, recv1_ref[...].reshape(devices, devices), preferred_element_type=f32)
    send2_ref[...] = turned.reshape(planes, plane, devices).astype(bf16)

    @pl.when(jnp.logical_not(even))
    def _():
        pl.semaphore_wait(barrier, 2 * (planes - 1) + jnp.where(final, 1, 0))
        signal(far_ok, me - 1)

    @pl.when(even)
    def _():
        pl.semaphore_wait(far_ok, 1)

    far = []
    for i in range(1, planes):
        q = (z + i) % planes
        far.append(pltpu.make_async_remote_copy(
            src_ref=send2_ref.at[q], dst_ref=recv2_ref.at[z], send_sem=s2.at[i], recv_sem=r2.at[i],
            device_id=(rep, q * plane + p), device_id_type=pl.DeviceIdType.MESH))
        far[-1].start()
    recv2_ref[z] = send2_ref[z]
    sides = []
    for side in range(2):
        sides.append(pltpu.make_async_remote_copy(
            src_ref=features_ref.at[:, pl.ds((ROWS_DEV - 1) * W * (1 - side), W)],
            dst_ref=(above_ref, below_ref)[side],
            send_sem=sf.at[side], recv_sem=rf.at[side],
            device_id=(rep, (ahead, behind)[side]), device_id_type=pl.DeviceIdType.MESH))
        sides[-1].start()
    for copy in far:
        copy.wait()
    arrived = jnp.transpose(recv2_ref[...].astype(f32).reshape(devices, devices))
    arrived = jnp.concatenate([arrived[k * LAT_CH : (k + 1) * LAT_CH] for k in range(per_peer)], axis=1)
    cells = jnp.dot(arrived.astype(bf16), table_ref[...], preferred_element_type=f32).astype(bf16)
    frames = [cache_ref[:, f * tile : (f + 1) * tile] for f in range(2)]
    frames = frames + [cells[:, f * tile : (f + 1) * tile] for f in range(FMAX)]
    rim = 2 * W
    for f in range(2 + FMAX):
        rim_out_ref[0, f] = frames[f][:, tile - rim :]
        rim_out_ref[1, f] = frames[f][:, 0:rim]
    edges = []
    for side in range(2):
        edges.append(pltpu.make_async_remote_copy(
            src_ref=rim_out_ref.at[side], dst_ref=rim_in_ref.at[side],
            send_sem=sh.at[side], recv_sem=rh.at[side],
            device_id=(rep, (ahead, behind)[side]), device_id_type=pl.DeviceIdType.MESH))
        edges[-1].start()
    for copy in sides + edges:
        copy.wait()
    nothing = jnp.zeros((LAT_CH, rim), f32)
    for f in range(2 + FMAX):
        top = jnp.where(position == 0, nothing, rim_in_ref[0, f].astype(f32)).astype(bf16)
        bottom = jnp.where(position == per_group - 1, nothing, rim_in_ref[1, f].astype(f32)).astype(bf16)
        at = f * (tile + 2 * rim)
        window_ref[:, at : at + rim] = top
        window_ref[:, at + rim : at + rim + tile] = frames[f]
        window_ref[:, at + rim + tile : at + 2 * rim + tile] = bottom


def gather(devices, assign, layout, latents, latent_cache, feature_cache):
    plane = devices // REQS // 2
    planes = devices // plane
    cells = FMAX * ROWS_DEV * W
    vm = pl.BlockSpec(memory_space=pltpu.VMEM)
    bf16, dma = jnp.bfloat16, pltpu.SemaphoreType.DMA
    return pl.pallas_call(
        functools.partial(gather_kernel, devices),
        out_shape=(
            jax.ShapeDtypeStruct((LAT_CH, (2 + FMAX) * (ROWS_DEV + 4) * W), bf16),
            jax.ShapeDtypeStruct((2, W, MID_CH), bf16),
            jax.ShapeDtypeStruct((2, W, MID_CH), bf16),
        ),
        in_specs=[pl.BlockSpec(memory_space=pltpu.SMEM), vm, vm, vm, vm],
        out_specs=(vm, vm, vm),
        scratch_shapes=[
            pltpu.VMEM((plane, planes, devices), bf16),
            pltpu.VMEM((plane, planes, devices), bf16),
            pltpu.VMEM((planes, plane, devices), bf16),
            pltpu.VMEM((planes, plane, devices), bf16),
            pltpu.VMEM((cells, cells), bf16),
            pltpu.VMEM((2, 2 + FMAX, LAT_CH, 2 * W), bf16),
            pltpu.VMEM((2, 2 + FMAX, LAT_CH, 2 * W), bf16),
            pltpu.SemaphoreType.REGULAR,
            pltpu.SemaphoreType.REGULAR,
            dma((plane,)), dma((plane,)), dma((planes,)), dma((planes,)),
            dma((2,)), dma((2,)), dma((2,)), dma((2,)),
        ],
        compiler_params=pltpu.CompilerParams(collective_id=0, has_side_effects=True, vmem_limit_bytes=40 * 1024 * 1024),
        cost_estimate=pl.CostEstimate(flops=1_000_000_000, bytes_accessed=1_500_000, transcendentals=0),
    )(
        assign,
        layout,
        latents,
        jnp.transpose(latent_cache.reshape(2, ROWS_DEV, W, LAT_CH), (3, 0, 1, 2)).reshape(LAT_CH, 2 * ROWS_DEV * W),
        feature_cache.reshape(2, ROWS_DEV * W, MID_CH),
    )


def decode_kernel(
    live_ref, place_ref, xt_ref, w1_ref, b1_ref, gain_ref, fc_ref, top_ref, bot_ref, w2_hbm, b2_ref,
    out_ref, fn_ref, w2_ref, wc_ref, xs_ref, h_ref, sem,
):
    live = live_ref[0]
    place = place_ref[0]
    last = place_ref[1]
    load = pltpu.make_async_copy(w2_hbm, w2_ref, sem)
    load.start()
    f32, bf16 = jnp.float32, jnp.bfloat16
    rows, mid = ROWS_DEV + 2, MID_CH
    xt = xt_ref[...].astype(f32)
    lanes = xt.shape[1]
    column = lax.broadcasted_iota(jnp.int32, xt.shape, 1) % W
    shifted = (
        jnp.where(column == 0, 0.0, pltpu.roll(xt, 1, 1)),
        xt,
        jnp.where(column == W - 1, 0.0, pltpu.roll(xt, lanes - 1, 1)),
    )
    per_frame = (ROWS_DEV + 4) * W
    for e in range(3):
        odd = pltpu.roll(shifted[e], lanes - W, 1).astype(bf16)
        even = shifted[e].astype(bf16)
        for b in range(3):
            source, start = ((even, 0), (odd, 0), (even, 2 * W))[b]
            for a in range(3):
                k = ((a * 3 + b) * 3 + e) * LAT_CH
                for t in range(FMAX):
                    at = (t + a) * per_frame + start
                    xs_ref[k : k + LAT_CH, t * rows * W : (t + 1) * rows * W] = source[:, at : at + rows * W]
    cells = rows * W
    row = lax.broadcasted_iota(jnp.int32, (cells, mid), 0)
    first_column = (row % W) == 0
    last_column = (row % W) == W - 1
    outside = jnp.logical_or(
        jnp.logical_and(row < W, place == 0),
        jnp.logical_and(row >= cells - W, place == last),
    )

    def spread(frame, values):
        before = jnp.where(first_column, 0.0, pltpu.roll(values, 1, 0)).astype(bf16)
        after = jnp.where(last_column, 0.0, pltpu.roll(values, cells - 1, 0)).astype(bf16)
        here = values.astype(bf16)
        h_ref[0, frame, :, 0:mid] = before
        h_ref[0, frame, :, mid : 2 * mid] = here
        h_ref[1, frame, :, 0:mid] = here
        h_ref[1, frame, :, mid : 2 * mid] = after

    for frame in range(2):
        values = jnp.concatenate(
            [top_ref[frame], fc_ref[frame], bot_ref[frame]], axis=0
        ).astype(f32)
        spread(frame, jnp.where(outside, 0.0, values))
    bias = b1_ref[...]
    gain = gain_ref[...]
    for t in range(FMAX):
        pre = lax.dot_general(
            xs_ref[:, t * cells : (t + 1) * cells],
            w1_ref[...],
            (((0,), (0,)), ((), ())),
            preferred_element_type=f32,
        ) + bias
        inverse = lax.rsqrt(jnp.mean(pre * pre, axis=1, keepdims=True) + 1e-06)
        v = pre * inverse * gain
        half = 0.5 * v
        spread(2 + t, jnp.where(outside, 0.0, half + half * jnp.tanh(half)))
    own = slice(W, W + ROWS_DEV * W)
    for j in range(2):
        one = h_ref[1, 1 + j, own, 0:mid]
        two = h_ref[1, 2 + j, own, 0:mid]
        three = h_ref[1, 3 + j, own, 0:mid]
        fn_ref[j] = jnp.where(live == 1, one.astype(f32), jnp.where(live == 2, two.astype(f32), three.astype(f32))).astype(bf16)
    load.wait()
    near = (((0,), (1, 2)), ((0, 1), (2,)))

    @pl.loop(0, 3)
    def _(a):
        base = a * 9
        tap = [[w2_ref[base + b * 3 + e].astype(f32) for e in range(3)] for b in range(3)]
        for slot, (py, dy) in enumerate(((0, 0), (0, 1), (1, 0), (1, 1))):
            taps = [sum(tap[b][e] for b in near[py][dy]) for e in range(3)]
            for px in range(2):
                for dx in range(2):
                    total = sum(taps[e] for e in near[px][dx])
                    wc_ref[px, a, slot * OUT_CH : (slot + 1) * OUT_CH, dx * mid : (dx + 1) * mid] = total.astype(bf16)

    bias2 = b2_ref[...]
    block = ROWS_DEV * W
    source = lax.broadcasted_iota(jnp.int32, (block, block), 0)
    target = lax.broadcasted_iota(jnp.int32, (block, block), 1)
    parity, line, cell = source // (2 * W), source // W % 2, source % W
    weave = (target == line * 2 * W + cell * 2 + parity).astype(bf16)

    @pl.loop(0, FMAX)
    def _(t):
        kept = []
        for px in range(2):
            both = [None, None]
            for a in range(3):
                for r in range(3):
                    right = h_ref[px, t + a, r * W : r * W + block, :]
                    first, count = ((0, 1), (1, 2), (3, 1))[r]
                    left = wc_ref[px, a, first * OUT_CH : (first + count) * OUT_CH, :]
                    part = lax.dot_general(left, right, (((1,), (1,)), ((), ())), preferred_element_type=f32)
                    for i in range(count):
                        py = (first + i) // 2
                        piece = part[i * OUT_CH : (i + 1) * OUT_CH]
                        both[py] = piece if both[py] is None else both[py] + piece
            kept.append([jnp.where(t < live, b + bias2, 0.0).astype(bf16) for b in both])
        for py in range(2):
            for pair in range(ROWS_DEV // 2):
                lanes = slice(pair * 2 * W, (pair + 1) * 2 * W)
                joined = jnp.concatenate([kept[0][py][:, lanes], kept[1][py][:, lanes]], axis=1)
                woven = jnp.dot(joined, weave, preferred_element_type=f32).astype(bf16)
                for line in range(2):
                    out_ref[t, 2 * (2 * pair + line) + py] = woven[:, line * 2 * W : (line + 1) * 2 * W]


def decode(live, place, last, window, first_weight, first_bias, norm_gain, feature_cache, above, below, second_weight, second_bias):
    rows = ROWS_DEV + 2
    vm = pl.BlockSpec(memory_space=pltpu.VMEM)
    sm = pl.BlockSpec(memory_space=pltpu.SMEM)
    f32, bf16 = jnp.float32, jnp.bfloat16
    frames, features = pl.pallas_call(
        decode_kernel,
        out_shape=(
            jax.ShapeDtypeStruct((FMAX, 2 * ROWS_DEV, OUT_CH, 2 * W), bf16),
            jax.ShapeDtypeStruct((2, ROWS_DEV * W, MID_CH), bf16),
        ),
        in_specs=[sm, sm, vm, vm, vm, vm, vm, vm, vm, pl.BlockSpec(memory_space=pl.ANY), vm],
        out_specs=(vm, vm),
        scratch_shapes=[
            pltpu.VMEM((27, OUT_CH, MID_CH), bf16),
            pltpu.VMEM((2, 3, 4 * OUT_CH, 2 * MID_CH), bf16),
            pltpu.VMEM((27 * LAT_CH, FMAX * rows * W), bf16),
            pltpu.VMEM((2, 5, rows * W, 2 * MID_CH), bf16),
            pltpu.SemaphoreType.DMA,
        ],
        compiler_params=pltpu.CompilerParams(vmem_limit_bytes=60 * 1024 * 1024),
        cost_estimate=pl.CostEstimate(flops=6_200_000_000, bytes_accessed=7_000_000, transcendentals=442368),
    )(
        jnp.reshape(live, (1,)).astype(jnp.int32),
        jnp.stack([place, last]).astype(jnp.int32),
        window,
        first_weight.reshape(27 * LAT_CH, MID_CH),
        first_bias.reshape(1, MID_CH),
        norm_gain.reshape(1, MID_CH),
        feature_cache.reshape(2, ROWS_DEV * W, MID_CH),
        above.reshape(2, W, MID_CH),
        below.reshape(2, W, MID_CH),
        jnp.swapaxes(second_weight, 3, 4).reshape(27, OUT_CH, MID_CH),
        second_bias.reshape(OUT_CH, 1),
    )
    return jnp.swapaxes(frames, 2, 3), features


def body(
    latents,
    layout,
    assign,
    counts,
    latent_cache,
    feature_cache,
    first_weight,
    first_bias,
    norm_gain,
    second_weight,
    second_bias,
):
    devices = lax.axis_size("seq")
    per_group = devices // REQS
    place = (lax.axis_index("seq") + per_group // 2) % devices
    live = counts[assign[place // per_group]]
    window, above, below = gather(devices, assign, layout, latents, latent_cache, feature_cache)
    decoded_frames, feature_next = decode(
        live, place % per_group, per_group - 1, window, first_weight, first_bias, norm_gain,
        feature_cache, above, below, second_weight, second_bias,
    )
    own = window.reshape(LAT_CH, 2 + FMAX, ROWS_DEV + 4, W)[:, :, 2 : 2 + ROWS_DEV]
    latent_next = lax.dynamic_slice_in_dim(own, live, 2, 1)
    latent_next = jnp.transpose(latent_next, (1, 2, 3, 0)).reshape(2, ROWS_DEV, W * LAT_CH)
    return (decoded_frames, latent_next, feature_next.reshape(2, ROWS_DEV, W, MID_CH))


def solution(mesh):
    return jax.shard_map(
        body,
        mesh=mesh,
        in_specs=(
            P(None, ("rep", "seq")),
            P("rep", None),
            P("rep"),
            P("rep"),
            P(None, ("rep", "seq"), None),
            P(None, ("rep", "seq"), None, None),
            P(),
            P(),
            P(),
            P(),
            P(),
        ),
        out_specs=(
            P(None, ("rep", "seq"), None, None),
            P(None, ("rep", "seq"), None),
            P(None, ("rep", "seq"), None, None),
        ),
        check_vma=False,
    )
```

time: 120 us -> 73.7 us (0.61)
  starting transfers between devices: 42.1 us -> 0 us
  Pallas kernels: 14.8 us -> 54.8 us
  other arithmetic: 17.5 us -> 0.62 us
  between operations: 15.8 us -> 4.59 us
  local copies, waits for them, and re-layouts: 23.4 us -> 13.3 us
  waiting for transfers between devices: 5.02 us -> 0 us
    pallas_call x0 -> x1, Pallas kernels: none -> 39.3 us  [gather(): pl.pallas_call(functools.partial(gather_kernel, devices), out_shape=(jax....]
    ppermute x4 -> x0, starting transfers between devices: 30 us -> none  [the longest x1 24.6 us: body(): below = lax.ppermute(feature_cache[:, 0], 'seq', [(j, i) for i, j in up])]
    all_to_all x1 -> x0, starting transfers between devices: 12.1 us -> none  [body(): lax.all_to_all(outgoing, 'seq', split_axis=1, concat_axis=1, tiled=True)]
    sort x2 -> x0, other arithmetic: 8.74 us -> none  [the longest x1 4.37 us: body(): sending_order = jnp.argsort(own_numbers)]
    unnamed x22 -> x14, local copies, waits for them, and re-layouts: 11.6 us -> 4.66 us
    all_to_all x1 -> x0, waiting for transfers between devices: 4.28 us -> none  [body(): lax.all_to_all(outgoing, 'seq', split_axis=1, concat_axis=1, tiled=True)]
    gather x2 -> x0, local copies, waits for them, and re-layouts: 3.76 us -> none  [the longest x1 1.88 us: body(): jnp.take(latents, sending_order, axis=1).reshape(LAT_CH, devices, per_peer)]
    add x1 -> x0, other arithmetic: 3.18 us -> none  [tile_numbers(): return target * tile_cells + within]
  transfers between devices with their start and end apart: 5 -> 0, of which waited for: 2 -> 0; matrix products, arithmetic and copies ran while one was open for 31% -> 0% of each run, Pallas kernels for 0% -> 0%
where the time goes in v2:
time: 73.7 us; the launch traced here: 73.2 us
  Pallas kernels  54.8 us (74%)
  local copies, waits for them, and re-layouts  13.3 us (18%)
  between operations  4.59 us (6%)
    pallas_call x1, Pallas kernels, gather(): pl.pallas_call(functools.partial(gather_kernel, devices), out_shape=(jax....  39.3 us
    pallas_call x1, Pallas kernels, decode(): pl.pallas_call(decode_kernel, out_shape=(jax.ShapeDtypeStruct((FMAX, 2 *...  15.4 us
    unnamed x14, local copies, waits for them, and re-layouts  4.66 us
    dynamic_slice x2, local copies, waits for them, and re-layouts, body(): live = counts[assign[place // per_group]]  2.55 us

profile of v2, /device:TPU:40, one launch (start us, length us, event | category | flops | bytes accessed | tf_op | source)
XLA Modules:
  0.0 73.2 jit_solution(235940111947150147)
XLA Ops:
  0.7 1.2 %dynamic_slice.9 = s32[1]{0:T(128)} dynamic-slice(s32[8]{0:T(128)} %assign_ref.1, s32[]{:T(128)S(6)} %select_n.26), dynamic_slice_sizes={1} | dynamic-slice | bytes 12 | tf_op jit(solution)/shard_map/dynamic_slice | solution.py:396
  3.9 0.6 pad_add_fusion.place_ref
  4.5 1.3 %dynamic_slice.10.live_ref = s32[1]{0:T(128)} dynamic-slice(s32[8]{0:T(128)} %param.14, s32[]{:T(128)S(6)} %select_n.27), dynamic_slice_sizes={1} | dynamic-slice | bytes 12 | tf_op jit(solution)/shard_map/dynamic_slice | solution.py:396
  7.7 1.3 %reshape.44.b1_ref = f32[1,384]{1,0:T(1,128)} reshape(f32[384]{0:T(512)} %param.18) | data formatting | bytes 3072 | tf_op jit(solution)/shard_map/reshape | solution.py:369
  9.0 1.3 %reshape.45.gain_ref = f32[1,384]{1,0:T(1,128)} reshape(f32[384]{0:T(512)} %param.19) | data formatting | bytes 3072 | tf_op jit(solution)/shard_map/reshape | solution.py:370
  10.2 1.4 %copy.17.b2_ref = f32[192,1]{1,0:T(8,128)} copy(f32[192,1]{0,1:T(1,128)} %bitcast.23) | data formatting | bytes 1536 | tf_op jit(solution)/shard_map/reshape | solution.py:375
  11.7 0.9 %reshape.40 = bf16[2,4,64,16]{3,2,1,0:T(8,128)(2,1)S(1)} reshape(bf16[2,4,1024]{2,1,0:T(4,128)(2,1)} %param.15) | data formatting | bytes 32768 | tf_op jit(solution)/shard_map/reshape | solution.py:219
  12.6 0.1 copy.19.cache_ref
  12.6 0.0 copy-start.1
  12.6 1.0 %copy-done.1 = s32[128,768]{1,0:T(8,128)S(1)} copy-done((s32[128,768]{1,0:T(8,128)S(1)}, s32[128,768]{1,0:T(8,128)}, u32[]{:S(2)}) %copy-start.1) | copy-done | bytes 393240
  13.6 0.0 copy-start.2
  13.7 1.0 %copy-done.2 = bf16[2,4,64,384]{3,2,1,0:T(8,128)(2,1)S(1)} copy-done((bf16[2,4,64,384]{3,2,1,0:T(8,128)(2,1)S(1)}, bf16[2,4,64,384]{3,2,1,0:T(8,128)(2,1)}, u32[]{:S(2)}) %copy-start.2) | copy-done | bytes 393240
  14.6 0.0 copy-start.3
  14.6 0.7 %copy-done.3 = bf16[16,768]{1,0:T(8,128)(2,1)S(1)} copy-done((bf16[16,768]{1,0:T(8,128)(2,1)S(1)}, bf16[16,768]{1,0:T(8,128)(2,1)}, u32[]{:S(2)}) %copy-start.3) | copy-done | bytes 24600
  15.4 0.0 copy-start.4
  15.4 0.7 copy-done.4
  16.0 39.3 %shard_map.130 = (bf16[16,2560]{1,0:T(8,128)(2,1)S(1)}, bf16[2,64,384]{2,1,0:T(8,128)(2,1)S(1)}, bf16[2,64,384]{2,1,0:T(8,128)(2,1)S(1)}) custom-call(s32[8]{0:T(128)S(1)} %copy-done.4, s32[128,768]{1,0:T(8,128)S(1)} %copy-done.1, bf16[16,768]{1,0:T(8,128)(2,1)S(1)} %copy-done.3, bf16[16,512]{1,0:T(8,128)(2,1)S(1)} %copy.19.cache_ref, ...), custom_call_target="tpu_custom_call" | custom-call | flops 1000000000 | bytes 1500000 | tf_op jit(solution)/shard_map/pallas_call | solution.py:191
  55.4 0.0 copy-start.5
  55.4 0.6 copy-done.5
  56.0 0.0 copy-start.6
  56.0 0.6 copy-done.6
  56.7 0.0 copy-start
  56.7 0.3 copy.20
  57.0 0.8 %reshape.49 = bf16[2,4,1024]{2,1,0:T(4,128)(2,1)} reshape(bf16[2,4,64,16]{3,2,1,0:T(8,128)(2,1)S(1)} %dynamic-slice_bitcast_fusion) | data formatting | bytes 32768 | tf_op jit(solution)/shard_map/reshape | solution.py:404
  57.8 0.0 copy-done
  57.8 15.4 %shard_map.131 = (bf16[3,8,192,128]{3,2,1,0:T(8,128)(2,1)}, bf16[2,256,384]{2,1,0:T(8,128)(2,1)}) custom-call(s32[1]{0:T(128)} %dynamic_slice.10.live_ref, s32[2]{0:T(128)} %pad_add_fusion.place_ref, bf16[16,2560]{1,0:T(8,128)(2,1)} %copy-done, bf16[432,384]{1,0:T(8,128)(2,1)} %bitcast.25, f32[1,384]{1,0:T(1,128)} %reshape.44.b1_ref, ...), custom_call_target="tpu_custom_call" | custom-call | flops 6200000000 | bytes 7000000 | tf_op jit(solution)/shard_map/pallas_call | solution.py:347
  (2 shorter events, 0.0 us)
Async XLA Ops:
  12.6 1.0 %copy-start.1 = (s32[128,768]{1,0:T(8,128)S(1)}, s32[128,768]{1,0:T(8,128)}, u32[]{:S(2)}) copy-start(s32[128,768]{1,0:T(8,128)} %layout_ref.1) | copy-start | bytes 1179652
  13.6 1.0 %copy-start.2 = (bf16[2,4,64,384]{3,2,1,0:T(8,128)(2,1)S(1)}, bf16[2,4,64,384]{3,2,1,0:T(8,128)(2,1)}, u32[]{:S(2)}) copy-start(bf16[2,4,64,384]{3,2,1,0:T(8,128)(2,1)} %param.16) | copy-start | bytes 1179652
  14.6 0.7 %copy-start.3 = (bf16[16,768]{1,0:T(8,128)(2,1)S(1)}, bf16[16,768]{1,0:T(8,128)(2,1)}, u32[]{:S(2)}) copy-start(bf16[16,768]{1,0:T(8,128)(2,1)} %latents_ref.1) | copy-start | bytes 73732
  15.4 0.7 copy-start.4
  55.4 0.6 copy-start.5
  56.0 0.6 copy-start.6
  56.7 1.2 %copy-start = (bf16[16,2560]{1,0:T(8,128)(2,1)}, bf16[16,2560]{1,0:T(8,128)(2,1)S(1)}, u32[]{:S(2)}) copy-start(bf16[16,2560]{1,0:T(8,128)(2,1)S(1)} %get-tuple-element.8.xt_ref) | copy-start | bytes 245764

commit v3 on v2

v3 whole, which is shorter than its diff:
```python
import functools

import jax
import jax.numpy as jnp
from jax import lax
from jax.experimental import pallas as pl
from jax.experimental.pallas import tpu as pltpu
from jax.sharding import PartitionSpec as P

LAT_CH = 16
MID_CH = 384
OUT_CH = 192
REQS = 8
FMAX = 3
ROWS_DEV = 4
W = 64


def spread_of_cells():
    lane = lax.broadcasted_iota(jnp.int32, (W * LAT_CH, W), 0)
    cell = lax.broadcasted_iota(jnp.int32, (W * LAT_CH, W), 1)
    fold = (lane // LAT_CH == cell).astype(jnp.bfloat16)
    channel = lax.broadcasted_iota(jnp.int32, (LAT_CH, W * LAT_CH), 0)
    member = lax.broadcasted_iota(jnp.int32, (LAT_CH, W * LAT_CH), 1) % LAT_CH == channel
    return fold, member


def rows_outside(position, last):
    cells = (ROWS_DEV + 2) * W
    row = lax.broadcasted_iota(jnp.int32, (cells, MID_CH), 0)
    above = jnp.logical_and(row < W, position == 0)
    return jnp.logical_or(above, jnp.logical_and(row >= cells - W, position == last))


def lay_out(target, frame, values):
    cells = values.shape[0]
    column = lax.broadcasted_iota(jnp.int32, values.shape, 0) % W
    before = jnp.where(column == 0, 0.0, pltpu.roll(values, 1, 0)).astype(jnp.bfloat16)
    after = jnp.where(column == W - 1, 0.0, pltpu.roll(values, cells - 1, 0)).astype(jnp.bfloat16)
    here = values.astype(jnp.bfloat16)
    target[0, frame, :, 0:MID_CH] = before
    target[0, frame, :, MID_CH : 2 * MID_CH] = here
    target[1, frame, :, 0:MID_CH] = here
    target[1, frame, :, MID_CH : 2 * MID_CH] = after


def combine_taps(weight, upper, middle, lower):
    near = (((0,), (1, 2)), ((0, 1), (2,)))

    @pl.loop(0, 3)
    def _(a):
        base = a * 9
        tap = [[weight[base + b * 3 + e].astype(jnp.float32) for e in range(3)] for b in range(3)]
        for target, start, py, dy in ((upper, 0, 0, 0), (middle, 0, 0, 1), (middle, OUT_CH, 1, 0), (lower, 0, 1, 1)):
            taps = [sum(tap[b][e] for b in near[py][dy]) for e in range(3)]
            for px in range(2):
                for dx in range(2):
                    total = sum(taps[e] for e in near[px][dx]).astype(jnp.bfloat16)
                    target[px, a, start : start + OUT_CH, dx * MID_CH : (dx + 1) * MID_CH] = total


def add_products(sums, features, upper, middle, lower, px, frame, a, count, times, started):
    block = ROWS_DEV * W
    begun = set()
    for r, weights in enumerate((middle, upper, lower)):
        row = (1, 0, 2)[r]
        right = features[px, frame, row * W : row * W + block, :]
        left = weights[px, a : a + count]
        height = left.shape[1]
        part = lax.dot_general(
            left.reshape(count * height, left.shape[2]), right, (((1,), (1,)), ((), ())), preferred_element_type=jnp.float32
        )
        for i, t in enumerate(times):
            for py in ((0, 1), (0,), (1,))[r]:
                at = i * height + (py * OUT_CH if r == 0 else 0)
                piece = part[at : at + OUT_CH]
                if r == 0 and t not in started:
                    sums[t, px, py] = piece
                else:
                    sums[t, px, py] = sums[t, px, py] + piece


def counted_before(marks, earlier):
    size = earlier.shape[0]
    carry = jnp.zeros((marks.shape[0], 1), jnp.float32)
    parts = []
    for start in range(0, marks.shape[1], size):
        block = marks[:, start : start + size]
        parts.append(jnp.dot(block.astype(jnp.bfloat16), earlier, preferred_element_type=jnp.float32) + carry)
        carry = carry + jnp.sum(block, axis=1, keepdims=True)
    return jnp.concatenate(parts, axis=1)


def gather_kernel(
    devices, assign_ref, layout_hbm, latents_hbm, cache_hbm, features_hbm, weight_hbm,
    window_ref, upper_hbm, middle_hbm, lower_hbm, part_hbm,
    layout_ref, latents_ref, cache_ref, features_ref, weight_ref, above_ref, below_ref,
    upper_ref, middle_ref, lower_ref, small_ref, part_ref, load_sem, store_sem,
    send1_ref, recv1_ref, send2_ref, recv2_ref, table_ref, rim_out_ref, rim_in_ref,
    plane_ok, far_ok, s1, r1, s2, r2, sf, rf, sh, rh,
):
    f32, bf16, i32 = jnp.float32, jnp.bfloat16, jnp.int32
    per_group = devices // REQS
    plane = per_group // 2
    planes = devices // plane
    tile = ROWS_DEV * W
    tile_cells = FMAX * tile
    per_peer = tile_cells // devices
    rep, me = lax.axis_index("rep"), lax.axis_index("seq")
    z, p = me // plane, me % plane
    even = p % 2 == 0
    ahead, behind = (me + 1) % devices, (me + devices - 1) % devices
    first, final = p == 0, p == plane - 1

    def signal(semaphore, device):
        pl.semaphore_signal(semaphore, inc=1, device_id=(rep, device), device_id_type=pl.DeviceIdType.MESH)

    loads = [
        pltpu.make_async_copy(source, target, load_sem.at[i])
        for i, (source, target) in enumerate((
            (layout_hbm, layout_ref), (latents_hbm, latents_ref), (cache_hbm, cache_ref), (features_hbm, features_ref),
        ))
    ]
    loads = loads + [
        pltpu.make_async_copy(weight_hbm.at[3 * i : 3 * i + 3], weight_ref.at[3 * i : 3 * i + 3], load_sem.at[4 + i])
        for i in range(9)
    ]
    for copy in loads:
        copy.start()

    barrier = pltpu.get_barrier_semaphore()
    for q in range(0, plane, 2):
        @pl.when(p != q)
        def _():
            signal(barrier, z * plane + q)
    for i in range(1, planes):
        signal(barrier, ((z + i) % planes) * plane + (p // 2) * 2 + 1)

    @pl.when(final)
    def _():
        signal(barrier, ahead)

    @pl.when(first)
    def _():
        signal(barrier, behind)

    row_of = lax.broadcasted_iota(i32, (tile_cells // 3, tile_cells // 3), 0)
    lane_of = lax.broadcasted_iota(i32, (tile_cells // 3, tile_cells // 3), 1)
    earlier = (row_of < lane_of).astype(bf16)
    loads[0].wait()
    own = layout_ref[pl.ds(me, 1), :]
    request = ((own // (ROWS_DEV * per_group * W)) * 43) // 128
    group = jnp.zeros_like(own)
    for g in range(REQS):
        group = group + jnp.where(assign_ref[g] == request, g, 0)
    place = group * per_group + (own // tile) % per_group
    target = (place + devices - per_group // 2) % devices
    line = (target % plane) * planes + target // plane
    hit = lax.broadcasted_iota(i32, (devices, tile_cells), 0) == line
    marks = hit.astype(f32)
    order = counted_before(marks, earlier)
    loads[1].wait()
    latents = latents_ref[...]
    rows = []
    for k in range(per_peer):
        chosen = jnp.where(order == k, marks, 0.0).astype(bf16)
        rows.append(lax.dot_general(latents, chosen, (((1,), (1,)), ((), ())), preferred_element_type=f32))
    rows.append(jnp.zeros((devices - per_peer * LAT_CH, devices), f32))
    send1_ref[...] = jnp.transpose(jnp.concatenate(rows, axis=0)).astype(bf16).reshape(plane, planes, devices)

    @pl.when(even)
    def _():
        pl.semaphore_wait(barrier, plane - 1 + jnp.where(first, 1, 0))
        signal(plane_ok, me + 1)

    @pl.when(jnp.logical_not(even))
    def _():
        pl.semaphore_wait(plane_ok, 1)

    near = []
    for i in range(1, plane):
        q = (p + i) % plane
        near.append(pltpu.make_async_remote_copy(
            src_ref=send1_ref.at[q], dst_ref=recv1_ref.at[p], send_sem=s1.at[i], recv_sem=r1.at[i],
            device_id=(rep, z * plane + q), device_id_type=pl.DeviceIdType.MESH))
        near[-1].start()
    recv1_ref[p] = send1_ref[p]

    my_place = (me + per_group // 2) % devices
    my_group, position = my_place // per_group, my_place % per_group
    frame = ROWS_DEV * per_group * W
    offset = layout_ref[...] - (assign_ref[my_group] * (FMAX * frame) + position * tile)
    inside = jnp.logical_and(jnp.logical_and(offset >= 0, offset < FMAX * frame), (offset & (frame - tile)) == 0)
    within = ((offset // frame) * tile + (offset & (tile - 1))).astype(f32)
    marks = inside.astype(f32)
    order = counted_before(marks, earlier)
    spot = lax.broadcasted_iota(i32, (devices, tile_cells), 1).astype(f32)
    for k in range(per_peer):
        chosen = jnp.logical_and(order == k, inside)
        home = jnp.sum(jnp.where(chosen, within, 0.0), axis=1, keepdims=True)
        table_ref[k * devices : (k + 1) * devices, :] = (home == spot).astype(bf16)

    for copy in near:
        copy.wait()
    to = lax.broadcasted_iota(i32, (devices, devices), 0)
    source = lax.broadcasted_iota(i32, (devices, devices), 1)
    turn = (source == (to % plane) * planes + to // plane).astype(bf16)
    turned = jnp.dot(turn, recv1_ref[...].reshape(devices, devices), preferred_element_type=f32)
    send2_ref[...] = turned.reshape(planes, plane, devices).astype(bf16)

    @pl.when(jnp.logical_not(even))
    def _():
        pl.semaphore_wait(barrier, 2 * (planes - 1) + jnp.where(final, 1, 0))
        signal(far_ok, me - 1)

    @pl.when(even)
    def _():
        pl.semaphore_wait(far_ok, 1)

    far = []
    for i in range(1, planes):
        q = (z + i) % planes
        far.append(pltpu.make_async_remote_copy(
            src_ref=send2_ref.at[q], dst_ref=recv2_ref.at[z], send_sem=s2.at[i], recv_sem=r2.at[i],
            device_id=(rep, q * plane + p), device_id_type=pl.DeviceIdType.MESH))
        far[-1].start()
    recv2_ref[z] = send2_ref[z]
    loads[3].wait()
    sides = []
    for side in range(2):
        sides.append(pltpu.make_async_remote_copy(
            src_ref=features_ref.at[:, pl.ds((ROWS_DEV - 1) * W * (1 - side), W)],
            dst_ref=(above_ref, below_ref)[side],
            send_sem=sf.at[side], recv_sem=rf.at[side],
            device_id=(rep, (ahead, behind)[side]), device_id_type=pl.DeviceIdType.MESH))
        sides[-1].start()

    loads[2].wait()
    wide = cache_ref[...].astype(f32).reshape(2 * ROWS_DEV, W * LAT_CH)
    fold, member = spread_of_cells()
    stacked = jnp.concatenate([
        jnp.where(member, jnp.broadcast_to(wide[i : i + 1], member.shape), 0.0) for i in range(2 * ROWS_DEV)
    ], axis=0).astype(bf16)
    folded = jnp.dot(stacked, fold, preferred_element_type=f32)
    cached = jnp.concatenate([folded[i * LAT_CH : (i + 1) * LAT_CH] for i in range(2 * ROWS_DEV)], axis=1).astype(bf16)

    for copy in loads[4:]:
        copy.wait()
    combine_taps(weight_ref, upper_ref, middle_ref, lower_ref)
    stores = [
        pltpu.make_async_copy(source.at[px, a], target.at[px, a], store_sem.at[i, px, a])
        for i, (source, target) in enumerate(((upper_ref, upper_hbm), (middle_ref, middle_hbm), (lower_ref, lower_hbm)))
        for px in range(2)
        for a in range(3)
    ]
    for copy in stores:
        copy.start()

    for copy in sides:
        copy.wait()
    outside = rows_outside(position, per_group - 1)
    for f in range(2):
        values = jnp.concatenate([above_ref[f], features_ref[f], below_ref[f]], axis=0).astype(f32)
        lay_out(small_ref, f, jnp.where(outside, 0.0, values))
    for px in range(2):
        add_products(part_ref, small_ref, upper_ref, middle_ref, lower_ref, px, 1, 0, 2, (1, 0), {})
        add_products(part_ref, small_ref, upper_ref, middle_ref, lower_ref, px, 0, 0, 1, (0,), {0})
    saved = [pltpu.make_async_copy(part_ref.at[t], part_hbm.at[t], store_sem.at[3, 0, t]) for t in range(2)]
    for copy in saved:
        copy.start()
    for copy in far:
        copy.wait()
    arrived = jnp.transpose(recv2_ref[...].astype(f32).reshape(devices, devices))
    arrived = jnp.concatenate([arrived[k * LAT_CH : (k + 1) * LAT_CH] for k in range(per_peer)], axis=1)
    cells = jnp.dot(arrived.astype(bf16), table_ref[...], preferred_element_type=f32).astype(bf16)
    frames = [cached[:, f * tile : (f + 1) * tile] for f in range(2)]
    frames = frames + [cells[:, f * tile : (f + 1) * tile] for f in range(FMAX)]
    rim = 2 * W
    for f in range(2 + FMAX):
        rim_out_ref[0, f] = frames[f][:, tile - rim :]
        rim_out_ref[1, f] = frames[f][:, 0:rim]
    edges = []
    for side in range(2):
        edges.append(pltpu.make_async_remote_copy(
            src_ref=rim_out_ref.at[side], dst_ref=rim_in_ref.at[side],
            send_sem=sh.at[side], recv_sem=rh.at[side],
            device_id=(rep, (ahead, behind)[side]), device_id_type=pl.DeviceIdType.MESH))
        edges[-1].start()
    for copy in edges:
        copy.wait()
    nothing = jnp.zeros((LAT_CH, rim), f32)
    for f in range(2 + FMAX):
        top = jnp.where(position == 0, nothing, rim_in_ref[0, f].astype(f32)).astype(bf16)
        bottom = jnp.where(position == per_group - 1, nothing, rim_in_ref[1, f].astype(f32)).astype(bf16)
        at = f * (tile + 2 * rim)
        window_ref[:, at : at + rim] = top
        window_ref[:, at + rim : at + rim + tile] = frames[f]
        window_ref[:, at + rim + tile : at + 2 * rim + tile] = bottom
    for copy in stores + saved:
        copy.wait()


def gather(devices, assign, layout, latents, latent_cache, feature_cache, second_weight):
    plane = devices // REQS // 2
    planes = devices // plane
    cells = FMAX * ROWS_DEV * W
    vm, hbm = pl.BlockSpec(memory_space=pltpu.VMEM), pl.BlockSpec(memory_space=pl.ANY)
    bf16, dma = jnp.bfloat16, pltpu.SemaphoreType.DMA
    return pl.pallas_call(
        functools.partial(gather_kernel, devices),
        out_shape=(
            jax.ShapeDtypeStruct((LAT_CH, (2 + FMAX) * (ROWS_DEV + 4) * W), bf16),
            jax.ShapeDtypeStruct((2, 3, OUT_CH, 2 * MID_CH), bf16),
            jax.ShapeDtypeStruct((2, 3, 2 * OUT_CH, 2 * MID_CH), bf16),
            jax.ShapeDtypeStruct((2, 3, OUT_CH, 2 * MID_CH), bf16),
            jax.ShapeDtypeStruct((2, 2, 2, OUT_CH, ROWS_DEV * W), jnp.float32),
        ),
        in_specs=[pl.BlockSpec(memory_space=pltpu.SMEM), hbm, hbm, hbm, hbm, hbm],
        out_specs=(vm, hbm, hbm, hbm, hbm),
        scratch_shapes=[
            pltpu.VMEM((devices, cells), jnp.int32),
            pltpu.VMEM((LAT_CH, cells), bf16),
            pltpu.VMEM((2, ROWS_DEV, W * LAT_CH), bf16),
            pltpu.VMEM((2, ROWS_DEV * W, MID_CH), bf16),
            pltpu.VMEM((27, OUT_CH, MID_CH), bf16),
            pltpu.VMEM((2, W, MID_CH), bf16),
            pltpu.VMEM((2, W, MID_CH), bf16),
            pltpu.VMEM((2, 3, OUT_CH, 2 * MID_CH), bf16),
            pltpu.VMEM((2, 3, 2 * OUT_CH, 2 * MID_CH), bf16),
            pltpu.VMEM((2, 3, OUT_CH, 2 * MID_CH), bf16),
            pltpu.VMEM((2, 2, (ROWS_DEV + 2) * W, 2 * MID_CH), bf16),
            pltpu.VMEM((2, 2, 2, OUT_CH, ROWS_DEV * W), jnp.float32),
            dma((13,)),
            dma((4, 2, 3)),
            pltpu.VMEM((plane, planes, devices), bf16),
            pltpu.VMEM((plane, planes, devices), bf16),
            pltpu.VMEM((planes, plane, devices), bf16),
            pltpu.VMEM((planes, plane, devices), bf16),
            pltpu.VMEM((cells, cells), bf16),
            pltpu.VMEM((2, 2 + FMAX, LAT_CH, 2 * W), bf16),
            pltpu.VMEM((2, 2 + FMAX, LAT_CH, 2 * W), bf16),
            pltpu.SemaphoreType.REGULAR,
            pltpu.SemaphoreType.REGULAR,
            dma((plane,)), dma((plane,)), dma((planes,)), dma((planes,)),
            dma((2,)), dma((2,)), dma((2,)), dma((2,)),
        ],
        compiler_params=pltpu.CompilerParams(collective_id=0, has_side_effects=True, vmem_limit_bytes=56 * 1024 * 1024),
        cost_estimate=pl.CostEstimate(flops=3_000_000_000, bytes_accessed=13_000_000, transcendentals=0),
    )(
        assign,
        layout,
        latents,
        latent_cache,
        feature_cache.reshape(2, ROWS_DEV * W, MID_CH),
        jnp.swapaxes(second_weight, 3, 4).reshape(27, OUT_CH, MID_CH),
    )


def decode_kernel(
    per_group, place_axis, assign_ref, counts_ref, window_ref, w1_hbm, b1_hbm, gain_hbm, fc_hbm, upper_hbm, middle_hbm, lower_hbm,
    part_hbm, b2_hbm,
    out_hbm, ln_ref, fn_ref,
    w1_ref, b1_ref, gain_ref, fc_ref, upper_ref, middle_ref, lower_ref, sums_ref, b2_ref, xs_ref, h_ref, frames_ref,
    load_sem, out_sem,
):
    f32, bf16 = jnp.float32, jnp.bfloat16
    place = (lax.axis_index(place_axis) + per_group // 2) % (per_group * REQS)
    position = place % per_group
    live = counts_ref[assign_ref[place // per_group]]
    small = [
        pltpu.make_async_copy(source, target, load_sem.at[i])
        for i, (source, target) in enumerate((
            (w1_hbm, w1_ref), (b1_hbm, b1_ref), (gain_hbm, gain_ref), (b2_hbm, b2_ref), (fc_hbm, fc_ref),
        ))
    ]
    large = [pltpu.make_async_copy(part_hbm.at[t], sums_ref.at[t], load_sem.at[5 + t]) for t in range(2)]
    for i, (source, target) in enumerate(((middle_hbm, middle_ref), (upper_hbm, upper_ref), (lower_hbm, lower_ref))):
        for px in range(2):
            for a in range(3):
                large.append(pltpu.make_async_copy(source.at[px, a], target.at[px, a], load_sem.at[7 + i * 6 + px * 3 + a]))
    for copy in small + large:
        copy.start()
    rows = ROWS_DEV + 2
    cells, tile = rows * W, ROWS_DEV * W
    per_frame = (ROWS_DEV + 4) * W
    xt = window_ref[...].astype(f32)
    lanes = xt.shape[1]
    column = lax.broadcasted_iota(jnp.int32, xt.shape, 1) % W
    shifted = (
        jnp.where(column == 0, 0.0, pltpu.roll(xt, 1, 1)),
        xt,
        jnp.where(column == W - 1, 0.0, pltpu.roll(xt, lanes - 1, 1)),
    )
    for e in range(3):
        odd = pltpu.roll(shifted[e], lanes - W, 1).astype(bf16)
        even = shifted[e].astype(bf16)
        for b in range(3):
            source, start = ((even, 0), (odd, 0), (even, 2 * W))[b]
            for a in range(3):
                k = ((a * 3 + b) * 3 + e) * LAT_CH
                for t in range(FMAX):
                    at = (t + a) * per_frame + start
                    xs_ref[k : k + LAT_CH, t * cells : (t + 1) * cells] = source[:, at : at + cells]
    outside = rows_outside(position, per_group - 1)
    for copy in small:
        copy.wait()
    bias = b1_ref[...].reshape(1, MID_CH)
    gain = gain_ref[...].reshape(1, MID_CH)
    for t in range(FMAX):
        pre = lax.dot_general(
            xs_ref[:, t * cells : (t + 1) * cells], w1_ref[...], (((0,), (0,)), ((), ())), preferred_element_type=f32
        ) + bias
        inverse = lax.rsqrt(jnp.mean(pre * pre, axis=1, keepdims=True) + 1e-06)
        half = 0.5 * (pre * inverse * gain)
        lay_out(h_ref, t, jnp.where(outside, 0.0, half + half * jnp.tanh(half)))
    own = slice(W, W + tile)
    kept = [fc_ref[1].astype(f32)] + [h_ref[1, t, own, 0:MID_CH].astype(f32) for t in range(FMAX)]
    for j in range(2):
        fn_ref[j] = jnp.where(live == 1, kept[j], jnp.where(live == 2, kept[j + 1], kept[j + 2])).astype(bf16)
    fold, member = spread_of_cells()
    latest = []
    for j in range(2):
        frames = [xt[:, f * per_frame + 2 * W : f * per_frame + 2 * W + tile] for f in range(j + 1, j + 4)]
        chosen = jnp.where(live == 1, frames[0], jnp.where(live == 2, frames[1], frames[2]))
        latest = latest + [chosen[:, y * W : (y + 1) * W] for y in range(ROWS_DEV)]
    wide = lax.dot_general(
        jnp.concatenate(latest, axis=0).astype(bf16), fold, (((1,), (1,)), ((), ())), preferred_element_type=f32
    ).reshape(2 * ROWS_DEV, LAT_CH, W * LAT_CH)
    ln_ref[...] = jnp.sum(jnp.where(member[None], wide, 0.0), axis=1).reshape(2, ROWS_DEV, W * LAT_CH).astype(bf16)
    block = tile
    source = lax.broadcasted_iota(jnp.int32, (block, block), 0)
    target = lax.broadcasted_iota(jnp.int32, (block, block), 1)
    parity, line, cell = source // (2 * W), source // W % 2, source % W
    weave = (target == line * 2 * W + cell * 2 + parity).astype(bf16)
    bias2 = jnp.transpose(jnp.broadcast_to(b2_ref[...].reshape(1, OUT_CH), (8, OUT_CH)))[:, 0:1]
    for copy in large:
        copy.wait()
    started = {0, 1}
    done = []
    for frame in range(FMAX):
        for px in range(2):
            times = tuple(range(2, frame - 1, -1))
            add_products(sums_ref, h_ref, upper_ref, middle_ref, lower_ref, px, frame, frame, 3 - frame, times, started)
        started = {0, 1, 2}
        t = frame
        ready = [[jnp.where(t < live, sums_ref[t, px, py] + bias2, 0.0).astype(bf16) for py in range(2)] for px in range(2)]
        for py in range(2):
            for pair in range(ROWS_DEV // 2):
                part = slice(pair * 2 * W, (pair + 1) * 2 * W)
                joined = jnp.concatenate([ready[0][py][:, part], ready[1][py][:, part]], axis=1)
                woven = jnp.dot(joined, weave, preferred_element_type=f32).astype(bf16)
                for line in range(2):
                    frames_ref[t, 2 * (2 * pair + line) + py] = woven[:, line * 2 * W : (line + 1) * 2 * W]
        done.append(pltpu.make_async_copy(frames_ref.at[t], out_hbm.at[t], out_sem.at[t]))
        done[-1].start()
    for copy in done:
        copy.wait()


def decode(devices, assign, counts, gathered, first_weight, first_bias, norm_gain, feature_cache, second_bias):
    per_group = devices // REQS
    cells = (ROWS_DEV + 2) * W
    vm, hbm = pl.BlockSpec(memory_space=pltpu.VMEM), pl.BlockSpec(memory_space=pl.ANY)
    sm = pl.BlockSpec(memory_space=pltpu.SMEM)
    f32, bf16 = jnp.float32, jnp.bfloat16
    frames, latents, features = pl.pallas_call(
        functools.partial(decode_kernel, per_group, "seq"),
        out_shape=(
            jax.ShapeDtypeStruct((FMAX, 2 * ROWS_DEV, OUT_CH, 2 * W), bf16),
            jax.ShapeDtypeStruct((2, ROWS_DEV, W * LAT_CH), bf16),
            jax.ShapeDtypeStruct((2, ROWS_DEV * W, MID_CH), bf16),
        ),
        in_specs=[sm, sm, vm] + [hbm] * 9,
        out_specs=(hbm, vm, vm),
        scratch_shapes=[
            pltpu.VMEM((27 * LAT_CH, MID_CH), bf16),
            pltpu.VMEM((MID_CH,), f32),
            pltpu.VMEM((MID_CH,), f32),
            pltpu.VMEM((2, ROWS_DEV * W, MID_CH), bf16),
            pltpu.VMEM((2, 3, OUT_CH, 2 * MID_CH), bf16),
            pltpu.VMEM((2, 3, 2 * OUT_CH, 2 * MID_CH), bf16),
            pltpu.VMEM((2, 3, OUT_CH, 2 * MID_CH), bf16),
            pltpu.VMEM((FMAX, 2, 2, OUT_CH, ROWS_DEV * W), f32),
            pltpu.VMEM((OUT_CH,), f32),
            pltpu.VMEM((27 * LAT_CH, FMAX * cells), bf16),
            pltpu.VMEM((2, FMAX, cells, 2 * MID_CH), bf16),
            pltpu.VMEM((FMAX, 2 * ROWS_DEV, OUT_CH, 2 * W), bf16),
            pltpu.SemaphoreType.DMA((25,)),
            pltpu.SemaphoreType.DMA((FMAX,)),
        ],
        compiler_params=pltpu.CompilerParams(vmem_limit_bytes=56 * 1024 * 1024),
        cost_estimate=pl.CostEstimate(flops=4_500_000_000, bytes_accessed=11_000_000, transcendentals=442368),
    )(
        assign, counts, gathered[0], first_weight.reshape(27 * LAT_CH, MID_CH), first_bias, norm_gain,
        feature_cache.reshape(2, ROWS_DEV * W, MID_CH), *gathered[1:], second_bias,
    )
    return jnp.swapaxes(frames, 2, 3), latents, features.reshape(2, ROWS_DEV, W, MID_CH)


def body(
    latents,
    layout,
    assign,
    counts,
    latent_cache,
    feature_cache,
    first_weight,
    first_bias,
    norm_gain,
    second_weight,
    second_bias,
):
    devices = lax.axis_size("seq")
    gathered = gather(devices, assign, layout, latents, latent_cache, feature_cache, second_weight)
    return decode(devices, assign, counts, gathered, first_weight, first_bias, norm_gain, feature_cache, second_bias)


def solution(mesh):
    return jax.shard_map(
        body,
        mesh=mesh,
        in_specs=(
            P(None, ("rep", "seq")),
            P("rep", None),
            P("rep"),
            P("rep"),
            P(None, ("rep", "seq"), None),
            P(None, ("rep", "seq"), None, None),
            P(),
            P(),
            P(),
            P(),
            P(),
        ),
        out_specs=(
            P(None, ("rep", "seq"), None, None),
            P(None, ("rep", "seq"), None),
            P(None, ("rep", "seq"), None, None),
        ),
        check_vma=False,
    )
```

time: 73.7 us -> 52.9 us (0.72)
  local copies, waits for them, and re-layouts: 13.3 us -> 0 us
  between operations: 4.59 us -> 0.64 us
  Pallas kernels: 54.8 us -> 52.1 us
    reshape x7 -> x0, local copies, waits for them, and re-layouts: 6.03 us -> none  [the longest x1 1.44 us: decode(): second_bias.reshape(OUT_CH, 1)]
    unnamed x14 -> x0, local copies, waits for them, and re-layouts: 4.66 us -> none
    pallas_call x1, Pallas kernels: 15.4 us -> 10.8 us  [decode(): pl.pallas_call(functools.partial(decode_kernel, per_group, 'seq'), out_sh...]
    dynamic_slice x2 -> x0, local copies, waits for them, and re-layouts: 2.55 us -> none  [body(): live = counts[assign[place // per_group]]]
    pallas_call x1, Pallas kernels: 39.3 us -> 41.2 us  [gather(): pl.pallas_call(functools.partial(gather_kernel, devices), out_shape=(jax....]
where the time goes in v3:
time: 52.9 us; the launch traced here: 52.7 us
  Pallas kernels  52.1 us (98%)
  between operations  0.64 us (1%)
    pallas_call x1, Pallas kernels, gather(): pl.pallas_call(functools.partial(gather_kernel, devices), out_shape=(jax....  41.2 us
    pallas_call x1, Pallas kernels, decode(): pl.pallas_call(functools.partial(decode_kernel, per_group, 'seq'), out_sh...  10.8 us

profile of v3, /device:TPU:40, one launch (start us, length us, event | category | flops | bytes accessed | tf_op | source)
XLA Modules:
  0.0 52.7 jit_solution(9430549255710218161)
XLA Ops:
  0.6 41.2 %shard_map.130 = (bf16[16,2560]{1,0:T(8,128)(2,1)}, bf16[2,3,192,768]{3,2,1,0:T(8,128)(2,1)}, bf16[2,3,384,768]{3,2,1,0:T(8,128)(2,1)}, bf16[2,3,192,768]{3,2,1,0:T(8,128)(2,1)}, f32[2,2,2,192,256]{4,3,2,1,0:T(8,128)}) custom-call(s32[8]{0:T(128)} %assign_ref.3, s32[128,768]{1,0:T(8,128)} %layout_hbm.1, bf16[16,768]{1,0:T(8,128)(2,1)} %latents_hbm.1, ...), custom_call_target="tpu_custom_call" | custom-call | flops 3000000000 | bytes 13000000 | tf_op jit(solution)/shard_map/pallas_call | solution.py:309
  41.9 10.8 %shard_map.131 = (bf16[3,8,192,128]{3,2,1,0:T(8,128)(2,1)}, bf16[2,4,1024]{2,1,0:T(4,128)(2,1)}, bf16[2,256,384]{2,1,0:T(8,128)(2,1)}) custom-call(s32[8]{0:T(128)} %assign_ref.3, s32[8]{0:T(128)} %counts_ref.1, bf16[16,2560]{1,0:T(8,128)(2,1)} %get-tuple-element.11.window_ref, bf16[432,384]{1,0:T(8,128)(2,1)} %bitcast.10, f32[384]{0:T(512)} %b1_hbm.1, ...), custom_call_target="tpu_custom_call" | custom-call | flops 4499999744 | bytes 11000000 | tf_op jit(solution)/shard_map/pallas_call | solution.py:466

commit v4 on v3

--- a/solution.py
+++ b/solution.py
@@ -93,10 +93,10 @@
 
 def gather_kernel(
     devices, assign_ref, layout_hbm, latents_hbm, cache_hbm, features_hbm, weight_hbm,
-    window_ref, upper_hbm, middle_hbm, lower_hbm, part_hbm,
+    window_ref, upper_ref, middle_ref, lower_ref, part_ref,
     layout_ref, latents_ref, cache_ref, features_ref, weight_ref, above_ref, below_ref,
-    upper_ref, middle_ref, lower_ref, small_ref, part_ref, load_sem, store_sem,
-    send1_ref, recv1_ref, send2_ref, recv2_ref, table_ref, rim_out_ref, rim_in_ref,
+    small_ref, load_sem,
+    send1_ref, recv1_ref, send2_ref, recv2_ref, upper_table, table_ref, lower_table, rim_out_ref, rim_in_ref,
     plane_ok, far_ok, s1, r1, s2, r2, sf, rf, sh, rh,
 ):
     f32, bf16, i32 = jnp.float32, jnp.bfloat16, jnp.int32
@@ -166,7 +166,11 @@
         chosen = jnp.where(order == k, marks, 0.0).astype(bf16)
         rows.append(lax.dot_general(latents, chosen, (((1,), (1,)), ((), ())), preferred_element_type=f32))
     rows.append(jnp.zeros((devices - per_peer * LAT_CH, devices), f32))
-    send1_ref[...] = jnp.transpose(jnp.concatenate(rows, axis=0)).astype(bf16).reshape(plane, planes, devices)
+    sent = jnp.transpose(jnp.concatenate(rows, axis=0)).reshape(plane, planes, devices)
+    for q in range(plane):
+        send1_ref[q, 0] = (sent[q - 1] if q > 0 else pltpu.roll(sent[plane - 1], 1, 0)).astype(bf16)
+        send1_ref[q, 1] = sent[q].astype(bf16)
+        send1_ref[q, 2] = (sent[q + 1] if q < plane - 1 else pltpu.roll(sent[0], planes - 1, 0)).astype(bf16)
 
     @pl.when(even)
     def _():
@@ -189,24 +193,35 @@
     my_place = (me + per_group // 2) % devices
     my_group, position = my_place // per_group, my_place % per_group
     frame = ROWS_DEV * per_group * W
-    offset = layout_ref[...] - (assign_ref[my_group] * (FMAX * frame) + position * tile)
-    inside = jnp.logical_and(jnp.logical_and(offset >= 0, offset < FMAX * frame), (offset & (frame - tile)) == 0)
-    within = ((offset // frame) * tile + (offset & (tile - 1))).astype(f32)
-    marks = inside.astype(f32)
-    order = counted_before(marks, earlier)
-    spot = lax.broadcasted_iota(i32, (devices, tile_cells), 1).astype(f32)
-    for k in range(per_peer):
-        chosen = jnp.logical_and(order == k, inside)
-        home = jnp.sum(jnp.where(chosen, within, 0.0), axis=1, keepdims=True)
-        table_ref[k * devices : (k + 1) * devices, :] = (home == spot).astype(bf16)
+    half = tile // 2
+    for side, table in enumerate((upper_table, table_ref, lower_table)):
+        other = (my_place + side - 1 + devices) % devices
+        start = assign_ref[other // per_group] * (FMAX * frame) + (other % per_group) * tile
+        offset = layout_ref[...] - start
+        inside = jnp.logical_and(jnp.logical_and(offset >= 0, offset < FMAX * frame), (offset & (frame - tile)) == 0)
+        inner = offset & (tile - 1)
+        if side == 0:
+            within = jnp.where(inner >= half, (offset // frame) * half + inner - half, -1)
+        elif side == 1:
+            within = (offset // frame) * tile + inner
+        else:
+            within = jnp.where(inner < half, (offset // frame) * half + inner, -1)
+        within = within.astype(f32)
+        order = counted_before(inside.astype(f32), earlier)
+        spot = lax.broadcasted_iota(i32, (devices, table.shape[1]), 1).astype(f32)
+        for k in range(per_peer):
+            chosen = jnp.logical_and(order == k, inside)
+            home = jnp.sum(jnp.where(chosen, within, 0.0), axis=1, keepdims=True)
+            table[k * devices : (k + 1) * devices, :] = (home == spot).astype(bf16)
 
     for copy in near:
         copy.wait()
     to = lax.broadcasted_iota(i32, (devices, devices), 0)
     source = lax.broadcasted_iota(i32, (devices, devices), 1)
     turn = (source == (to % plane) * planes + to // plane).astype(bf16)
-    turned = jnp.dot(turn, recv1_ref[...].reshape(devices, devices), preferred_element_type=f32)
-    send2_ref[...] = turned.reshape(planes, plane, devices).astype(bf16)
+    for side in range(3):
+        turned = jnp.dot(turn, recv1_ref[:, side].reshape(devices, devices), preferred_element_type=f32)
+        send2_ref[:, side] = turned.reshape(planes, plane, devices).astype(bf16)
 
     @pl.when(jnp.logical_not(even))
     def _():
@@ -244,20 +259,26 @@
     folded = jnp.dot(stacked, fold, preferred_element_type=f32)
     cached = jnp.concatenate([folded[i * LAT_CH : (i + 1) * LAT_CH] for i in range(2 * ROWS_DEV)], axis=1).astype(bf16)
 
+    rim = 2 * W
+    for f in range(2):
+        rim_out_ref[0, f] = cached[:, (f + 1) * tile - rim : (f + 1) * tile]
+        rim_out_ref[1, f] = cached[:, f * tile : f * tile + rim]
+    edges = []
+    for side in range(2):
+        edges.append(pltpu.make_async_remote_copy(
+            src_ref=rim_out_ref.at[side], dst_ref=rim_in_ref.at[side],
+            send_sem=sh.at[side], recv_sem=rh.at[side],
+            device_id=(rep, (ahead, behind)[side]), device_id_type=pl.DeviceIdType.MESH))
+        edges[-1].start()
+
     for copy in loads[4:]:
         copy.wait()
     combine_taps(weight_ref, upper_ref, middle_ref, lower_ref)
-    stores = [
-        pltpu.make_async_copy(source.at[px, a], target.at[px, a], store_sem.at[i, px, a])
-        for i, (source, target) in enumerate(((upper_ref, upper_hbm), (middle_ref, middle_hbm), (lower_ref, lower_hbm)))
-        for px in range(2)
-        for a in range(3)
-    ]
-    for copy in stores:
-        copy.start()
 
     for copy in sides:
         copy.wait()
+    for copy in edges:
+        copy.wait_recv()
     outside = rows_outside(position, per_group - 1)
     for f in range(2):
         values = jnp.concatenate([above_ref[f], features_ref[f], below_ref[f]], axis=0).astype(f32)
@@ -265,46 +286,34 @@
     for px in range(2):
         add_products(part_ref, small_ref, upper_ref, middle_ref, lower_ref, px, 1, 0, 2, (1, 0), {})
         add_products(part_ref, small_ref, upper_ref, middle_ref, lower_ref, px, 0, 0, 1, (0,), {0})
-    saved = [pltpu.make_async_copy(part_ref.at[t], part_hbm.at[t], store_sem.at[3, 0, t]) for t in range(2)]
-    for copy in saved:
-        copy.start()
     for copy in far:
         copy.wait()
-    arrived = jnp.transpose(recv2_ref[...].astype(f32).reshape(devices, devices))
-    arrived = jnp.concatenate([arrived[k * LAT_CH : (k + 1) * LAT_CH] for k in range(per_peer)], axis=1)
-    cells = jnp.dot(arrived.astype(bf16), table_ref[...], preferred_element_type=f32).astype(bf16)
-    frames = [cached[:, f * tile : (f + 1) * tile] for f in range(2)]
-    frames = frames + [cells[:, f * tile : (f + 1) * tile] for f in range(FMAX)]
-    rim = 2 * W
-    for f in range(2 + FMAX):
-        rim_out_ref[0, f] = frames[f][:, tile - rim :]
-        rim_out_ref[1, f] = frames[f][:, 0:rim]
-    edges = []
-    for side in range(2):
-        edges.append(pltpu.make_async_remote_copy(
-            src_ref=rim_out_ref.at[side], dst_ref=rim_in_ref.at[side],
-            send_sem=sh.at[side], recv_sem=rh.at[side],
-            device_id=(rep, (ahead, behind)[side]), device_id_type=pl.DeviceIdType.MESH))
-        edges[-1].start()
-    for copy in edges:
-        copy.wait()
+    found = []
+    for side, table in enumerate((upper_table, table_ref, lower_table)):
+        arrived = jnp.transpose(recv2_ref[:, side].astype(f32).reshape(devices, devices))
+        arrived = jnp.concatenate([arrived[k * LAT_CH : (k + 1) * LAT_CH] for k in range(per_peer)], axis=1)
+        found.append(jnp.dot(arrived.astype(bf16), table[...], preferred_element_type=f32))
     nothing = jnp.zeros((LAT_CH, rim), f32)
     for f in range(2 + FMAX):
-        top = jnp.where(position == 0, nothing, rim_in_ref[0, f].astype(f32)).astype(bf16)
-        bottom = jnp.where(position == per_group - 1, nothing, rim_in_ref[1, f].astype(f32)).astype(bf16)
+        if f < 2:
+            top, here, bottom = rim_in_ref[0, f].astype(f32), cached[:, f * tile : (f + 1) * tile], rim_in_ref[1, f].astype(f32)
+        else:
+            t = f - 2
+            top, bottom = (found[side][:, t * rim : (t + 1) * rim] for side in (0, 2))
+            here = found[1][:, t * tile : (t + 1) * tile].astype(bf16)
         at = f * (tile + 2 * rim)
-        window_ref[:, at : at + rim] = top
-        window_ref[:, at + rim : at + rim + tile] = frames[f]
-        window_ref[:, at + rim + tile : at + 2 * rim + tile] = bottom
-    for copy in stores + saved:
-        copy.wait()
+        window_ref[:, at : at + rim] = jnp.where(position == 0, nothing, top).astype(bf16)
+        window_ref[:, at + rim : at + rim + tile] = here
+        window_ref[:, at + rim + tile : at + 2 * rim + tile] = jnp.where(position == per_group - 1, nothing, bottom).astype(bf16)
+    for copy in edges:
+        copy.wait_send()
 
 
 def gather(devices, assign, layout, latents, latent_cache, feature_cache, second_weight):
     plane = devices // REQS // 2
     planes = devices // plane
     cells = FMAX * ROWS_DEV * W
-    vm, hbm = pl.BlockSpec(memory_space=pltpu.VMEM), pl.BlockSpec(memory_space=pl.ANY)
+    vm, hbm = pl.BlockSpec(memory_space=pltpu.VMEM), pl.BlockSpec(memory_space=pltpu.HBM)
     bf16, dma = jnp.bfloat16, pltpu.SemaphoreType.DMA
     return pl.pallas_call(
         functools.partial(gather_kernel, devices),
@@ -316,7 +325,7 @@
             jax.ShapeDtypeStruct((2, 2, 2, OUT_CH, ROWS_DEV * W), jnp.float32),
         ),
         in_specs=[pl.BlockSpec(memory_space=pltpu.SMEM), hbm, hbm, hbm, hbm, hbm],
-        out_specs=(vm, hbm, hbm, hbm, hbm),
+        out_specs=(vm, vm, vm, vm, vm),
         scratch_shapes=[
             pltpu.VMEM((devices, cells), jnp.int32),
             pltpu.VMEM((LAT_CH, cells), bf16),
@@ -325,42 +334,41 @@
             pltpu.VMEM((27, OUT_CH, MID_CH), bf16),
             pltpu.VMEM((2, W, MID_CH), bf16),
             pltpu.VMEM((2, W, MID_CH), bf16),
-            pltpu.VMEM((2, 3, OUT_CH, 2 * MID_CH), bf16),
-            pltpu.VMEM((2, 3, 2 * OUT_CH, 2 * MID_CH), bf16),
-            pltpu.VMEM((2, 3, OUT_CH, 2 * MID_CH), bf16),
             pltpu.VMEM((2, 2, (ROWS_DEV + 2) * W, 2 * MID_CH), bf16),
-            pltpu.VMEM((2, 2, 2, OUT_CH, ROWS_DEV * W), jnp.float32),
             dma((13,)),
-            dma((4, 2, 3)),
-            pltpu.VMEM((plane, planes, devices), bf16),
-            pltpu.VMEM((plane, planes, devices), bf16),
-            pltpu.VMEM((planes, plane, devices), bf16),
-            pltpu.VMEM((planes, plane, devices), bf16),
+            pltpu.VMEM((plane, 3, planes, devices), bf16),
+            pltpu.VMEM((plane, 3, planes, devices), bf16),
+            pltpu.VMEM((planes, 3, plane, devices), bf16),
+            pltpu.VMEM((planes, 3, plane, devices), bf16),
+            pltpu.VMEM((cells, cells // 2), bf16),
             pltpu.VMEM((cells, cells), bf16),
-            pltpu.VMEM((2, 2 + FMAX, LAT_CH, 2 * W), bf16),
-            pltpu.VMEM((2, 2 + FMAX, LAT_CH, 2 * W), bf16),
+            pltpu.VMEM((cells, cells // 2), bf16),
+            pltpu.VMEM((2, 2, LAT_CH, 2 * W), bf16),
+            pltpu.VMEM((2, 2, LAT_CH, 2 * W), bf16),
             pltpu.SemaphoreType.REGULAR,
             pltpu.SemaphoreType.REGULAR,
             dma((plane,)), dma((plane,)), dma((planes,)), dma((planes,)),
             dma((2,)), dma((2,)), dma((2,)), dma((2,)),
         ],
-        compiler_params=pltpu.CompilerParams(collective_id=0, has_side_effects=True, vmem_limit_bytes=56 * 1024 * 1024),
+        compiler_params=pltpu.CompilerParams(collective_id=0, has_side_effects=True, vmem_limit_bytes=28 * 1024 * 1024),
         cost_estimate=pl.CostEstimate(flops=3_000_000_000, bytes_accessed=13_000_000, transcendentals=0),
     )(
-        assign,
-        layout,
-        latents,
-        latent_cache,
-        feature_cache.reshape(2, ROWS_DEV * W, MID_CH),
-        jnp.swapaxes(second_weight, 3, 4).reshape(27, OUT_CH, MID_CH),
+        *(pltpu.with_memory_space_constraint(x, pltpu.HBM) for x in (
+            assign,
+            layout,
+            latents,
+            latent_cache,
+            feature_cache.reshape(2, ROWS_DEV * W, MID_CH),
+            jnp.swapaxes(second_weight, 3, 4).reshape(27, OUT_CH, MID_CH),
+        )),
     )
 
 
 def decode_kernel(
-    per_group, place_axis, assign_ref, counts_ref, window_ref, w1_hbm, b1_hbm, gain_hbm, fc_hbm, upper_hbm, middle_hbm, lower_hbm,
-    part_hbm, b2_hbm,
+    per_group, place_axis, assign_ref, counts_ref, window_ref, w1_hbm, b1_hbm, gain_hbm, fc_hbm, upper_ref, middle_ref, lower_ref,
+    part_ref, b2_hbm,
     out_hbm, ln_ref, fn_ref,
-    w1_ref, b1_ref, gain_ref, fc_ref, upper_ref, middle_ref, lower_ref, sums_ref, b2_ref, xs_ref, h_ref, frames_ref,
+    w1_ref, b1_ref, gain_ref, fc_ref, sums_ref, b2_ref, xs_ref, h_ref, frames_ref,
     load_sem, out_sem,
 ):
     f32, bf16 = jnp.float32, jnp.bfloat16
@@ -373,12 +381,7 @@
             (w1_hbm, w1_ref), (b1_hbm, b1_ref), (gain_hbm, gain_ref), (b2_hbm, b2_ref), (fc_hbm, fc_ref),
         ))
     ]
-    large = [pltpu.make_async_copy(part_hbm.at[t], sums_ref.at[t], load_sem.at[5 + t]) for t in range(2)]
-    for i, (source, target) in enumerate(((middle_hbm, middle_ref), (upper_hbm, upper_ref), (lower_hbm, lower_ref))):
-        for px in range(2):
-            for a in range(3):
-                large.append(pltpu.make_async_copy(source.at[px, a], target.at[px, a], load_sem.at[7 + i * 6 + px * 3 + a]))
-    for copy in small + large:
+    for copy in small:
         copy.start()
     rows = ROWS_DEV + 2
     cells, tile = rows * W, ROWS_DEV * W
@@ -433,9 +436,7 @@
     parity, line, cell = source // (2 * W), source // W % 2, source % W
     weave = (target == line * 2 * W + cell * 2 + parity).astype(bf16)
     bias2 = jnp.transpose(jnp.broadcast_to(b2_ref[...].reshape(1, OUT_CH), (8, OUT_CH)))[:, 0:1]
-    for copy in large:
-        copy.wait()
-    started = {0, 1}
+    started = set()
     done = []
     for frame in range(FMAX):
         for px in range(2):
@@ -443,7 +444,10 @@
             add_products(sums_ref, h_ref, upper_ref, middle_ref, lower_ref, px, frame, frame, 3 - frame, times, started)
         started = {0, 1, 2}
         t = frame
-        ready = [[jnp.where(t < live, sums_ref[t, px, py] + bias2, 0.0).astype(bf16) for py in range(2)] for px in range(2)]
+        ready = []
+        for px in range(2):
+            total = [sums_ref[t, px, py] + (part_ref[t, px, py] if t < 2 else 0.0) + bias2 for py in range(2)]
+            ready.append([jnp.where(t < live, one, 0.0).astype(bf16) for one in total])
         for py in range(2):
             for pair in range(ROWS_DEV // 2):
                 part = slice(pair * 2 * W, (pair + 1) * 2 * W)
@@ -460,7 +464,7 @@
 def decode(devices, assign, counts, gathered, first_weight, first_bias, norm_gain, feature_cache, second_bias):
     per_group = devices // REQS
     cells = (ROWS_DEV + 2) * W
-    vm, hbm = pl.BlockSpec(memory_space=pltpu.VMEM), pl.BlockSpec(memory_space=pl.ANY)
+    vm, hbm = pl.BlockSpec(memory_space=pltpu.VMEM), pl.BlockSpec(memory_space=pltpu.HBM)
     sm = pl.BlockSpec(memory_space=pltpu.SMEM)
     f32, bf16 = jnp.float32, jnp.bfloat16
     frames, latents, features = pl.pallas_call(
@@ -470,25 +474,22 @@
             jax.ShapeDtypeStruct((2, ROWS_DEV, W * LAT_CH), bf16),
             jax.ShapeDtypeStruct((2, ROWS_DEV * W, MID_CH), bf16),
         ),
-        in_specs=[sm, sm, vm] + [hbm] * 9,
+        in_specs=[sm, sm, vm] + [hbm] * 4 + [vm] * 4 + [hbm],
         out_specs=(hbm, vm, vm),
         scratch_shapes=[
             pltpu.VMEM((27 * LAT_CH, MID_CH), bf16),
             pltpu.VMEM((MID_CH,), f32),
             pltpu.VMEM((MID_CH,), f32),
             pltpu.VMEM((2, ROWS_DEV * W, MID_CH), bf16),
-            pltpu.VMEM((2, 3, OUT_CH, 2 * MID_CH), bf16),
-            pltpu.VMEM((2, 3, 2 * OUT_CH, 2 * MID_CH), bf16),
-            pltpu.VMEM((2, 3, OUT_CH, 2 * MID_CH), bf16),
             pltpu.VMEM((FMAX, 2, 2, OUT_CH, ROWS_DEV * W), f32),
             pltpu.VMEM((OUT_CH,), f32),
             pltpu.VMEM((27 * LAT_CH, FMAX * cells), bf16),
             pltpu.VMEM((2, FMAX, cells, 2 * MID_CH), bf16),
             pltpu.VMEM((FMAX, 2 * ROWS_DEV, OUT_CH, 2 * W), bf16),
-            pltpu.SemaphoreType.DMA((25,)),
+            pltpu.SemaphoreType.DMA((5,)),
             pltpu.SemaphoreType.DMA((FMAX,)),
         ],
-        compiler_params=pltpu.CompilerParams(vmem_limit_bytes=56 * 1024 * 1024),
+        compiler_params=pltpu.CompilerParams(vmem_limit_bytes=28 * 1024 * 1024),
         cost_estimate=pl.CostEstimate(flops=4_500_000_000, bytes_accessed=11_000_000, transcendentals=442368),
     )(
         assign, counts, gathered[0], first_weight.reshape(27 * LAT_CH, MID_CH), first_bias, norm_gain,

time: 52.9 us -> 51.1 us (0.966)
  Pallas kernels: 52.1 us -> 50 us
    pallas_call x1, Pallas kernels: 10.8 us -> 8.88 us  [decode(): pl.pallas_call(functools.partial(decode_kernel, per_group, 'seq'), out_sh...]
where the time goes in v4:
time: 51.1 us; the launch traced here: 51 us
  Pallas kernels  50 us (98%)
  between operations  0.91 us (2%)
    pallas_call x1, Pallas kernels, gather(): pl.pallas_call(functools.partial(gather_kernel, devices), out_shape=(jax....  41.2 us
    pallas_call x1, Pallas kernels, decode(): pl.pallas_call(functools.partial(decode_kernel, per_group, 'seq'), out_sh...  8.88 us

profile of v4, /device:TPU:40, one launch (start us, length us, event | category | flops | bytes accessed | tf_op | source)
XLA Modules:
  0.0 51.0 jit_solution(8786231698367569283)
XLA Ops:
  0.6 0.0 copy-start
  0.6 0.0 copy-start.1
  0.7 0.0 copy-start.2
  0.7 0.0 copy-start.3
  0.7 0.0 copy-start.4
  0.7 0.0 copy-start.5
  0.7 0.0 copy-start.6
  0.7 41.2 %shard_map.130 = (bf16[16,2560]{1,0:T(8,128)(2,1)S(1)}, bf16[2,3,192,768]{3,2,1,0:T(8,128)(2,1)S(1)}, bf16[2,3,384,768]{3,2,1,0:T(8,128)(2,1)S(1)}, bf16[2,3,192...) custom-call(s32[8]{0:T(128)} %assign_ref.3, s32[128,768]{1,0:T(8,128)} %layout_hbm.1, bf16[16,768]{1,0:T(8,128)(2,1)} %latents_hbm.1, ...), custom_call_target="tpu_custom_call" | custom-call | flops 3000000000 | bytes 13000000 | tf_op jit(solution)/shard_map/pallas_call | solution.py:318
  41.9 0.0 copy-done
  41.9 0.0 copy-done.1
  41.9 0.0 copy-done.2
  41.9 0.0 copy-done.3
  41.9 0.0 copy-done.4
  41.9 0.0 copy-done.5
  41.9 0.0 copy-done.6
  41.9 8.9 %shard_map.131 = (bf16[3,8,192,128]{3,2,1,0:T(8,128)(2,1)}, bf16[2,4,1024]{2,1,0:T(4,128)(2,1)}, bf16[2,256,384]{2,1,0:T(8,128)(2,1)}) custom-call(s32[8]{0:T(128)S(1)} %copy-done.5, s32[8]{0:T(128)S(1)} %copy-done.6, bf16[16,2560]{1,0:T(8,128)(2,1)S(1)} %get-tuple-element.11.window_ref, bf16[432,384]{1,0:T(8,128)(2,1)S(1)} %bitcast.9, f32[384]{0:T(512)S(1)} %copy-done.2, ...), custom_call_target="tpu_custom_call" | custom-call | flops 4499999744 | bytes 11000000 | tf_op jit(solution)/shard_map/pallas_call | solution.py:470
Async XLA Ops:
  0.6 41.2 %copy-start = (bf16[2,4,64,384]{3,2,1,0:T(8,128)(2,1)S(1)}, bf16[2,4,64,384]{3,2,1,0:T(8,128)(2,1)}, u32[]{:S(2)}) copy-start(bf16[2,4,64,384]{3,2,1,0:T(8,128)(2,1)} %param.16) | copy-start | bytes 1179652
  0.6 41.2 %copy-start.1 = (bf16[3,3,3,16,384]{4,3,2,1,0:T(8,128)(2,1)S(1)}, bf16[3,3,3,16,384]{4,3,2,1,0:T(8,128)(2,1)}, u32[]{:S(2)}) copy-start(bf16[3,3,3,16,384]{4,3,2,1,0:T(8,128)(2,1)} %param.17) | copy-start | bytes 995332
  0.7 41.2 %copy-start.2 = (f32[384]{0:T(512)S(1)}, f32[384]{0:T(512)}, u32[]{:S(2)}) copy-start(f32[384]{0:T(512)} %b1_hbm.1) | copy-start | bytes 4612
  0.7 41.2 %copy-start.3 = (f32[384]{0:T(512)S(1)}, f32[384]{0:T(512)}, u32[]{:S(2)}) copy-start(f32[384]{0:T(512)} %gain_hbm.1) | copy-start | bytes 4612
  0.7 41.2 %copy-start.4 = (f32[192]{0:T(256)S(1)}, f32[192]{0:T(256)}, u32[]{:S(2)}) copy-start(f32[192]{0:T(256)} %b2_hbm.1) | copy-start | bytes 2308
  0.7 41.2 %copy-start.5 = (s32[8]{0:T(128)S(1)}, s32[8]{0:T(128)}, u32[]{:S(2)}) copy-start(s32[8]{0:T(128)} %assign_ref.3) | copy-start | bytes 100
  0.7 41.2 %copy-start.6 = (s32[8]{0:T(128)S(1)}, s32[8]{0:T(128)}, u32[]{:S(2)}) copy-start(s32[8]{0:T(128)} %counts_ref.1) | copy-start | bytes 100

commit v5 on v4

--- a/solution.py
+++ b/solution.py
@@ -59,10 +59,10 @@
                     target[px, a, start : start + OUT_CH, dx * MID_CH : (dx + 1) * MID_CH] = total
 
 
-def add_products(sums, features, upper, middle, lower, px, frame, a, count, times, started):
+def add_products(sums, features, upper, middle, lower, px, frame, a, count, times, started, parts=(0, 1, 2)):
     block = ROWS_DEV * W
-    begun = set()
-    for r, weights in enumerate((middle, upper, lower)):
+    for r in parts:
+        weights = (middle, upper, lower)[r]
         row = (1, 0, 2)[r]
         right = features[px, frame, row * W : row * W + block, :]
         left = weights[px, a : a + count]
@@ -91,10 +91,14 @@
     return jnp.concatenate(parts, axis=1)
 
 
+def by_distance(ring):
+    return sorted(range(1, ring), key=lambda i: (-min(i, ring - i), i))
+
+
 def gather_kernel(
-    devices, assign_ref, layout_hbm, latents_hbm, cache_hbm, features_hbm, weight_hbm,
+    devices, assign_hbm, layout_hbm, latents_hbm, cache_hbm, features_hbm, weight_hbm,
     window_ref, upper_ref, middle_ref, lower_ref, part_ref,
-    layout_ref, latents_ref, cache_ref, features_ref, weight_ref, above_ref, below_ref,
+    assign_ref, layout_ref, latents_ref, cache_ref, features_ref, weight_ref, above_ref, below_ref,
     small_ref, load_sem,
     send1_ref, recv1_ref, send2_ref, recv2_ref, upper_table, table_ref, lower_table, rim_out_ref, rim_in_ref,
     plane_ok, far_ok, s1, r1, s2, r2, sf, rf, sh, rh,
@@ -118,23 +122,23 @@
     loads = [
         pltpu.make_async_copy(source, target, load_sem.at[i])
         for i, (source, target) in enumerate((
-            (layout_hbm, layout_ref), (latents_hbm, latents_ref), (cache_hbm, cache_ref), (features_hbm, features_ref),
+            (layout_hbm, layout_ref), (assign_hbm, assign_ref), (latents_hbm, latents_ref), (cache_hbm, cache_ref), (features_hbm, features_ref),
         ))
     ]
     loads = loads + [
-        pltpu.make_async_copy(weight_hbm.at[3 * i : 3 * i + 3], weight_ref.at[3 * i : 3 * i + 3], load_sem.at[4 + i])
+        pltpu.make_async_copy(weight_hbm.at[3 * i : 3 * i + 3], weight_ref.at[3 * i : 3 * i + 3], load_sem.at[5 + i])
         for i in range(9)
     ]
     for copy in loads:
         copy.start()
 
     barrier = pltpu.get_barrier_semaphore()
+    for i in by_distance(planes):
+        signal(barrier, ((z + i) % planes) * plane + (p // 2) * 2 + 1)
     for q in range(0, plane, 2):
         @pl.when(p != q)
         def _():
             signal(barrier, z * plane + q)
-    for i in range(1, planes):
-        signal(barrier, ((z + i) % planes) * plane + (p // 2) * 2 + 1)
 
     @pl.when(final)
     def _():
@@ -148,6 +152,7 @@
     lane_of = lax.broadcasted_iota(i32, (tile_cells // 3, tile_cells // 3), 1)
     earlier = (row_of < lane_of).astype(bf16)
     loads[0].wait()
+    loads[1].wait()
     own = layout_ref[pl.ds(me, 1), :]
     request = ((own // (ROWS_DEV * per_group * W)) * 43) // 128
     group = jnp.zeros_like(own)
@@ -159,7 +164,7 @@
     hit = lax.broadcasted_iota(i32, (devices, tile_cells), 0) == line
     marks = hit.astype(f32)
     order = counted_before(marks, earlier)
-    loads[1].wait()
+    loads[2].wait()
     latents = latents_ref[...]
     rows = []
     for k in range(per_peer):
@@ -233,14 +238,14 @@
         pl.semaphore_wait(far_ok, 1)
 
     far = []
-    for i in range(1, planes):
+    for i in by_distance(planes):
         q = (z + i) % planes
         far.append(pltpu.make_async_remote_copy(
             src_ref=send2_ref.at[q], dst_ref=recv2_ref.at[z], send_sem=s2.at[i], recv_sem=r2.at[i],
             device_id=(rep, q * plane + p), device_id_type=pl.DeviceIdType.MESH))
         far[-1].start()
     recv2_ref[z] = send2_ref[z]
-    loads[3].wait()
+    loads[4].wait()
     sides = []
     for side in range(2):
         sides.append(pltpu.make_async_remote_copy(
@@ -250,7 +255,7 @@
             device_id=(rep, (ahead, behind)[side]), device_id_type=pl.DeviceIdType.MESH))
         sides[-1].start()
 
-    loads[2].wait()
+    loads[3].wait()
     wide = cache_ref[...].astype(f32).reshape(2 * ROWS_DEV, W * LAT_CH)
     fold, member = spread_of_cells()
     stacked = jnp.concatenate([
@@ -271,7 +276,7 @@
             device_id=(rep, (ahead, behind)[side]), device_id_type=pl.DeviceIdType.MESH))
         edges[-1].start()
 
-    for copy in loads[4:]:
+    for copy in loads[5:]:
         copy.wait()
     combine_taps(weight_ref, upper_ref, middle_ref, lower_ref)
 
@@ -324,9 +329,10 @@
             jax.ShapeDtypeStruct((2, 3, OUT_CH, 2 * MID_CH), bf16),
             jax.ShapeDtypeStruct((2, 2, 2, OUT_CH, ROWS_DEV * W), jnp.float32),
         ),
-        in_specs=[pl.BlockSpec(memory_space=pltpu.SMEM), hbm, hbm, hbm, hbm, hbm],
+        in_specs=[hbm] * 6,
         out_specs=(vm, vm, vm, vm, vm),
         scratch_shapes=[
+            pltpu.SMEM((REQS,), jnp.int32),
             pltpu.VMEM((devices, cells), jnp.int32),
             pltpu.VMEM((LAT_CH, cells), bf16),
             pltpu.VMEM((2, ROWS_DEV, W * LAT_CH), bf16),
@@ -335,7 +341,7 @@
             pltpu.VMEM((2, W, MID_CH), bf16),
             pltpu.VMEM((2, W, MID_CH), bf16),
             pltpu.VMEM((2, 2, (ROWS_DEV + 2) * W, 2 * MID_CH), bf16),
-            dma((13,)),
+            dma((14,)),
             pltpu.VMEM((plane, 3, planes, devices), bf16),
             pltpu.VMEM((plane, 3, planes, devices), bf16),
             pltpu.VMEM((planes, 3, plane, devices), bf16),
@@ -365,20 +371,20 @@
 
 
 def decode_kernel(
-    per_group, place_axis, assign_ref, counts_ref, window_ref, w1_hbm, b1_hbm, gain_hbm, fc_hbm, upper_ref, middle_ref, lower_ref,
+    per_group, place_axis, assign_hbm, counts_hbm, window_ref, w1_hbm, b1_hbm, gain_hbm, fc_hbm, upper_ref, middle_ref, lower_ref,
     part_ref, b2_hbm,
     out_hbm, ln_ref, fn_ref,
-    w1_ref, b1_ref, gain_ref, fc_ref, sums_ref, b2_ref, xs_ref, h_ref, frames_ref,
+    assign_ref, counts_ref, w1_ref, b1_ref, gain_ref, fc_ref, sums_ref, b2_ref, xs_ref, pre_ref, h_ref, frames_ref,
     load_sem, out_sem,
 ):
     f32, bf16 = jnp.float32, jnp.bfloat16
     place = (lax.axis_index(place_axis) + per_group // 2) % (per_group * REQS)
     position = place % per_group
-    live = counts_ref[assign_ref[place // per_group]]
     small = [
         pltpu.make_async_copy(source, target, load_sem.at[i])
         for i, (source, target) in enumerate((
             (w1_hbm, w1_ref), (b1_hbm, b1_ref), (gain_hbm, gain_ref), (b2_hbm, b2_ref), (fc_hbm, fc_ref),
+            (assign_hbm, assign_ref), (counts_hbm, counts_ref),
         ))
     ]
     for copy in small:
@@ -404,59 +410,86 @@
                 for t in range(FMAX):
                     at = (t + a) * per_frame + start
                     xs_ref[k : k + LAT_CH, t * cells : (t + 1) * cells] = source[:, at : at + cells]
-    outside = rows_outside(position, per_group - 1)
     for copy in small:
         copy.wait()
+    live = counts_ref[assign_ref[place // per_group]]
     bias = b1_ref[...].reshape(1, MID_CH)
     gain = gain_ref[...].reshape(1, MID_CH)
-    for t in range(FMAX):
-        pre = lax.dot_general(
+    row = lax.broadcasted_iota(jnp.int32, (W, MID_CH), 0)
+
+    def linear(t):
+        pre_ref[t] = lax.dot_general(
             xs_ref[:, t * cells : (t + 1) * cells], w1_ref[...], (((0,), (0,)), ((), ())), preferred_element_type=f32
-        ) + bias
+        )
+
+    def activate(t, y):
+        at = pl.ds(pl.multiple_of(y * W, W), W)
+        pre = pre_ref[t, at, :] + bias
         inverse = lax.rsqrt(jnp.mean(pre * pre, axis=1, keepdims=True) + 1e-06)
         half = 0.5 * (pre * inverse * gain)
-        lay_out(h_ref, t, jnp.where(outside, 0.0, half + half * jnp.tanh(half)))
-    own = slice(W, W + tile)
-    kept = [fc_ref[1].astype(f32)] + [h_ref[1, t, own, 0:MID_CH].astype(f32) for t in range(FMAX)]
-    for j in range(2):
-        fn_ref[j] = jnp.where(live == 1, kept[j], jnp.where(live == 2, kept[j + 1], kept[j + 2])).astype(bf16)
-    fold, member = spread_of_cells()
-    latest = []
-    for j in range(2):
-        frames = [xt[:, f * per_frame + 2 * W : f * per_frame + 2 * W + tile] for f in range(j + 1, j + 4)]
-        chosen = jnp.where(live == 1, frames[0], jnp.where(live == 2, frames[1], frames[2]))
-        latest = latest + [chosen[:, y * W : (y + 1) * W] for y in range(ROWS_DEV)]
-    wide = lax.dot_general(
-        jnp.concatenate(latest, axis=0).astype(bf16), fold, (((1,), (1,)), ((), ())), preferred_element_type=f32
-    ).reshape(2 * ROWS_DEV, LAT_CH, W * LAT_CH)
-    ln_ref[...] = jnp.sum(jnp.where(member[None], wide, 0.0), axis=1).reshape(2, ROWS_DEV, W * LAT_CH).astype(bf16)
+        above = jnp.logical_and(y == 0, position == 0)
+        below = jnp.logical_and(y == rows - 1, position == per_group - 1)
+        values = jnp.where(jnp.logical_or(above, below), 0.0, half + half * jnp.tanh(half))
+        here = values.astype(bf16)
+        h_ref[0, t, at, 0:MID_CH] = jnp.where(row == 0, 0.0, pltpu.roll(values, 1, 0)).astype(bf16)
+        h_ref[0, t, at, MID_CH : 2 * MID_CH] = here
+        h_ref[1, t, at, 0:MID_CH] = here
+        h_ref[1, t, at, MID_CH : 2 * MID_CH] = jnp.where(row == W - 1, 0.0, pltpu.roll(values, W - 1, 0)).astype(bf16)
+
+    def keep_last(j):
+        own = slice(W, W + tile)
+        fresh = h_ref[1, jnp.maximum(j + live - 2, 0), own, 0:MID_CH].astype(f32)
+        fn_ref[j] = jnp.where(j + live == 1, fc_ref[1].astype(f32), fresh).astype(bf16)
+        latest = window_ref[:, pl.ds(pl.multiple_of((j + live) * per_frame + 2 * W, 2 * W), tile)].astype(f32)
+        latest = jnp.concatenate([latest[:, y * W : (y + 1) * W] for y in range(ROWS_DEV)], axis=0).astype(bf16)
+        wide = lax.dot_general(latest, fold, (((1,), (1,)), ((), ())), preferred_element_type=f32)
+        wide = jnp.where(member[None], wide.reshape(ROWS_DEV, LAT_CH, W * LAT_CH), 0.0)
+        ln_ref[j] = jnp.sum(wide, axis=1).astype(bf16)
+
+    def finish(t, py):
+        ready = []
+        for px in range(2):
+            total = sums_ref[t, px, py] + (part_ref[t, px, py] if t < 2 else 0.0) + bias2
+            ready.append(jnp.where(t < live, total, 0.0).astype(bf16))
+        for pair in range(ROWS_DEV // 2):
+            part = slice(pair * 2 * W, (pair + 1) * 2 * W)
+            joined = jnp.concatenate([ready[0][:, part], ready[1][:, part]], axis=1)
+            woven = jnp.dot(joined, weave, preferred_element_type=f32).astype(bf16)
+            for line in range(2):
+                frames_ref[t, 2 * (2 * pair + line) + py] = woven[:, line * 2 * W : (line + 1) * 2 * W]
+
+    for t in range(FMAX):
+        linear(t)
+    for y in range(rows):
+        activate(0, y)
     block = tile
     source = lax.broadcasted_iota(jnp.int32, (block, block), 0)
     target = lax.broadcasted_iota(jnp.int32, (block, block), 1)
     parity, line, cell = source // (2 * W), source // W % 2, source % W
     weave = (target == line * 2 * W + cell * 2 + parity).astype(bf16)
     bias2 = jnp.transpose(jnp.broadcast_to(b2_ref[...].reshape(1, OUT_CH), (8, OUT_CH)))[:, 0:1]
-    started = set()
-    done = []
+    fold, member = spread_of_cells()
+    done = [pltpu.make_async_copy(frames_ref.at[t], out_hbm.at[t], out_sem.at[t]) for t in range(FMAX)]
     for frame in range(FMAX):
-        for px in range(2):
-            times = tuple(range(2, frame - 1, -1))
-            add_products(sums_ref, h_ref, upper_ref, middle_ref, lower_ref, px, frame, frame, 3 - frame, times, started)
-        started = {0, 1, 2}
-        t = frame
-        ready = []
-        for px in range(2):
-            total = [sums_ref[t, px, py] + (part_ref[t, px, py] if t < 2 else 0.0) + bias2 for py in range(2)]
-            ready.append([jnp.where(t < live, one, 0.0).astype(bf16) for one in total])
-        for py in range(2):
-            for pair in range(ROWS_DEV // 2):
-                part = slice(pair * 2 * W, (pair + 1) * 2 * W)
-                joined = jnp.concatenate([ready[0][py][:, part], ready[1][py][:, part]], axis=1)
-                woven = jnp.dot(joined, weave, preferred_element_type=f32).astype(bf16)
-                for line in range(2):
-                    frames_ref[t, 2 * (2 * pair + line) + py] = woven[:, line * 2 * W : (line + 1) * 2 * W]
-        done.append(pltpu.make_async_copy(frames_ref.at[t], out_hbm.at[t], out_sem.at[t]))
-        done[-1].start()
+        times = tuple(range(2, frame - 1, -1))
+        started = set() if frame == 0 else {0, 1, 2}
+
+        @pl.loop(0, 2)
+        def _(i):
+            for r in range(3):
+                add_products(sums_ref, h_ref, upper_ref, middle_ref, lower_ref, i, frame, frame, 3 - frame, times, started, (r,))
+                if frame + 1 < FMAX:
+                    activate(frame + 1, i * 3 + r)
+            if frame > 0:
+                finish(frame - 1, i)
+            if frame == FMAX - 1:
+                keep_last(i)
+
+        if frame > 0:
+            done[frame - 1].start()
+    for py in range(2):
+        finish(FMAX - 1, py)
+    done[FMAX - 1].start()
     for copy in done:
         copy.wait()
 
@@ -465,7 +498,6 @@
     per_group = devices // REQS
     cells = (ROWS_DEV + 2) * W
     vm, hbm = pl.BlockSpec(memory_space=pltpu.VMEM), pl.BlockSpec(memory_space=pltpu.HBM)
-    sm = pl.BlockSpec(memory_space=pltpu.SMEM)
     f32, bf16 = jnp.float32, jnp.bfloat16
     frames, latents, features = pl.pallas_call(
         functools.partial(decode_kernel, per_group, "seq"),
@@ -474,9 +506,11 @@
             jax.ShapeDtypeStruct((2, ROWS_DEV, W * LAT_CH), bf16),
             jax.ShapeDtypeStruct((2, ROWS_DEV * W, MID_CH), bf16),
         ),
-        in_specs=[sm, sm, vm] + [hbm] * 4 + [vm] * 4 + [hbm],
+        in_specs=[hbm, hbm, vm] + [hbm] * 4 + [vm] * 4 + [hbm],
         out_specs=(hbm, vm, vm),
         scratch_shapes=[
+            pltpu.SMEM((REQS,), jnp.int32),
+            pltpu.SMEM((REQS,), jnp.int32),
             pltpu.VMEM((27 * LAT_CH, MID_CH), bf16),
             pltpu.VMEM((MID_CH,), f32),
             pltpu.VMEM((MID_CH,), f32),
@@ -484,9 +518,10 @@
             pltpu.VMEM((FMAX, 2, 2, OUT_CH, ROWS_DEV * W), f32),
             pltpu.VMEM((OUT_CH,), f32),
             pltpu.VMEM((27 * LAT_CH, FMAX * cells), bf16),
+            pltpu.VMEM((FMAX, cells, MID_CH), f32),
             pltpu.VMEM((2, FMAX, cells, 2 * MID_CH), bf16),
             pltpu.VMEM((FMAX, 2 * ROWS_DEV, OUT_CH, 2 * W), bf16),
-            pltpu.SemaphoreType.DMA((5,)),
+            pltpu.SemaphoreType.DMA((7,)),
             pltpu.SemaphoreType.DMA((FMAX,)),
         ],
         compiler_params=pltpu.CompilerParams(vmem_limit_bytes=28 * 1024 * 1024),

time: 51.1 us -> 52.3 us (1.023)
  Pallas kernels: 50 us -> 51.5 us
    pallas_call x1, Pallas kernels: 8.88 us -> 11.3 us  [decode(): pl.pallas_call(functools.partial(decode_kernel, per_group, 'seq'), out_sh...]
    pallas_call x1, Pallas kernels: 41.2 us -> 40.2 us  [gather(): pl.pallas_call(functools.partial(gather_kernel, devices), out_shape=(jax....]
where the time goes in v5:
time: 52.3 us; the launch traced here: 52.2 us
  Pallas kernels  51.5 us (98%)
  between operations  0.75 us (1%)
    pallas_call x1, Pallas kernels, gather(): pl.pallas_call(functools.partial(gather_kernel, devices), out_shape=(jax....  40.2 us
    pallas_call x1, Pallas kernels, decode(): pl.pallas_call(functools.partial(decode_kernel, per_group, 'seq'), out_sh...  11.3 us

profile of v5, /device:TPU:40, one launch (start us, length us, event | category | flops | bytes accessed | tf_op | source)
XLA Modules:
  0.0 52.2 jit_solution(3530423324926608223)
XLA Ops:
  0.6 0.0 copy-start
  0.6 0.0 copy-start.1
  0.7 0.0 copy-start.2
  0.7 0.0 copy-start.3
  0.7 0.0 copy-start.4
  0.7 0.0 copy-start.5
  0.7 0.0 copy-start.6
  0.7 40.2 %shard_map.130 = (bf16[16,2560]{1,0:T(8,128)(2,1)S(1)}, bf16[2,3,192,768]{3,2,1,0:T(8,128)(2,1)S(1)}, bf16[2,3,384,768]{3,2,1,0:T(8,128)(2,1)S(1)}, bf16[2,3,192...) custom-call(s32[8]{0:T(128)} %assign_hbm.3, s32[128,768]{1,0:T(8,128)} %layout_hbm.1, bf16[16,768]{1,0:T(8,128)(2,1)} %latents_hbm.1, ...), custom_call_target="tpu_custom_call" | custom-call | flops 3000000000 | bytes 13000000 | tf_op jit(solution)/shard_map/pallas_call | solution.py:323
  40.9 0.0 copy-done
  40.9 0.0 copy-done.1
  40.9 0.0 copy-done.2
  40.9 0.0 copy-done.3
  40.9 0.0 copy-done.4
  41.0 0.0 copy-done.5
  41.0 0.0 copy-done.6
  41.0 11.3 %shard_map.131 = (bf16[3,8,192,128]{3,2,1,0:T(8,128)(2,1)}, bf16[2,4,1024]{2,1,0:T(4,128)(2,1)}, bf16[2,256,384]{2,1,0:T(8,128)(2,1)}) custom-call(s32[8]{0:T(128)S(1)} %copy-done.5, s32[8]{0:T(128)S(1)} %copy-done.6, bf16[16,2560]{1,0:T(8,128)(2,1)S(1)} %get-tuple-element.11.window_ref, bf16[432,384]{1,0:T(8,128)(2,1)S(1)} %bitcast.9, f32[384]{0:T(512)S(1)} %copy-done.2, ...), custom_call_target="tpu_custom_call" | custom-call | flops 4499999744 | bytes 11000000 | tf_op jit(solution)/shard_map/pallas_call | solution.py:502
Async XLA Ops:
  0.6 40.3 %copy-start = (bf16[2,4,64,384]{3,2,1,0:T(8,128)(2,1)S(1)}, bf16[2,4,64,384]{3,2,1,0:T(8,128)(2,1)}, u32[]{:S(2)}) copy-start(bf16[2,4,64,384]{3,2,1,0:T(8,128)(2,1)} %param.16) | copy-start | bytes 1179652
  0.6 40.3 %copy-start.1 = (bf16[3,3,3,16,384]{4,3,2,1,0:T(8,128)(2,1)S(1)}, bf16[3,3,3,16,384]{4,3,2,1,0:T(8,128)(2,1)}, u32[]{:S(2)}) copy-start(bf16[3,3,3,16,384]{4,3,2,1,0:T(8,128)(2,1)} %param.17) | copy-start | bytes 995332
  0.7 40.3 %copy-start.2 = (f32[384]{0:T(512)S(1)}, f32[384]{0:T(512)}, u32[]{:S(2)}) copy-start(f32[384]{0:T(512)} %b1_hbm.1) | copy-start | bytes 4612
  0.7 40.3 %copy-start.3 = (f32[384]{0:T(512)S(1)}, f32[384]{0:T(512)}, u32[]{:S(2)}) copy-start(f32[384]{0:T(512)} %gain_hbm.1) | copy-start | bytes 4612
  0.7 40.3 %copy-start.4 = (f32[192]{0:T(256)S(1)}, f32[192]{0:T(256)}, u32[]{:S(2)}) copy-start(f32[192]{0:T(256)} %b2_hbm.1) | copy-start | bytes 2308
  0.7 40.3 %copy-start.5 = (s32[8]{0:T(128)S(1)}, s32[8]{0:T(128)}, u32[]{:S(2)}) copy-start(s32[8]{0:T(128)} %assign_hbm.3) | copy-start | bytes 100
  0.7 40.3 %copy-start.6 = (s32[8]{0:T(128)S(1)}, s32[8]{0:T(128)}, u32[]{:S(2)}) copy-start(s32[8]{0:T(128)} %counts_hbm.1) | copy-start | bytes 100

commit v6 on v5

--- a/solution.py
+++ b/solution.py
@@ -371,21 +371,18 @@
 
 
 def decode_kernel(
-    per_group, place_axis, assign_hbm, counts_hbm, window_ref, w1_hbm, b1_hbm, gain_hbm, fc_hbm, upper_ref, middle_ref, lower_ref,
-    part_ref, b2_hbm,
-    out_hbm, ln_ref, fn_ref,
-    assign_ref, counts_ref, w1_ref, b1_ref, gain_ref, fc_ref, sums_ref, b2_ref, xs_ref, pre_ref, h_ref, frames_ref,
-    load_sem, out_sem,
+    per_group, place_axis, assign_hbm, counts_hbm, window_ref, w1_ref, b1_ref, gain_ref, fc_ref, upper_ref, middle_ref, lower_ref,
+    part_ref, b2_ref,
+    out_hbm, ln_hbm, fn_hbm,
+    assign_ref, counts_ref, sums_ref, xs_ref, pre_ref, h_ref, frames_ref, ln_ref,
+    load_sem, out_sem, last_sem, keep_sem,
 ):
     f32, bf16 = jnp.float32, jnp.bfloat16
     place = (lax.axis_index(place_axis) + per_group // 2) % (per_group * REQS)
     position = place % per_group
     small = [
         pltpu.make_async_copy(source, target, load_sem.at[i])
-        for i, (source, target) in enumerate((
-            (w1_hbm, w1_ref), (b1_hbm, b1_ref), (gain_hbm, gain_ref), (b2_hbm, b2_ref), (fc_hbm, fc_ref),
-            (assign_hbm, assign_ref), (counts_hbm, counts_ref),
-        ))
+        for i, (source, target) in enumerate(((assign_hbm, assign_ref), (counts_hbm, counts_ref)))
     ]
     for copy in small:
         copy.start()
@@ -400,19 +397,18 @@
         xt,
         jnp.where(column == W - 1, 0.0, pltpu.roll(xt, lanes - 1, 1)),
     )
-    for e in range(3):
-        odd = pltpu.roll(shifted[e], lanes - W, 1).astype(bf16)
-        even = shifted[e].astype(bf16)
-        for b in range(3):
-            source, start = ((even, 0), (odd, 0), (even, 2 * W))[b]
-            for a in range(3):
-                k = ((a * 3 + b) * 3 + e) * LAT_CH
-                for t in range(FMAX):
+    evens = [one.astype(bf16) for one in shifted]
+    odds = [pltpu.roll(one, lanes - W, 1).astype(bf16) for one in shifted]
+
+    def patches(t):
+        for e in range(3):
+            for b in range(3):
+                source, start = ((evens[e], 0), (odds[e], 0), (evens[e], 2 * W))[b]
+                for a in range(3):
+                    k = ((a * 3 + b) * 3 + e) * LAT_CH
                     at = (t + a) * per_frame + start
                     xs_ref[k : k + LAT_CH, t * cells : (t + 1) * cells] = source[:, at : at + cells]
-    for copy in small:
-        copy.wait()
-    live = counts_ref[assign_ref[place // per_group]]
+
     bias = b1_ref[...].reshape(1, MID_CH)
     gain = gain_ref[...].reshape(1, MID_CH)
     row = lax.broadcasted_iota(jnp.int32, (W, MID_CH), 0)
@@ -423,43 +419,36 @@
         )
 
     def activate(t, y):
-        at = pl.ds(pl.multiple_of(y * W, W), W)
-        pre = pre_ref[t, at, :] + bias
+        pre = pre_ref[t, y * W : (y + 1) * W, :] + bias
         inverse = lax.rsqrt(jnp.mean(pre * pre, axis=1, keepdims=True) + 1e-06)
         half = 0.5 * (pre * inverse * gain)
-        above = jnp.logical_and(y == 0, position == 0)
-        below = jnp.logical_and(y == rows - 1, position == per_group - 1)
-        values = jnp.where(jnp.logical_or(above, below), 0.0, half + half * jnp.tanh(half))
+        values = half + half * jnp.tanh(half)
+        if y == 0:
+            values = jnp.where(position == 0, 0.0, values)
+        if y == rows - 1:
+            values = jnp.where(position == per_group - 1, 0.0, values)
+        at = slice(y * W, (y + 1) * W)
         here = values.astype(bf16)
         h_ref[0, t, at, 0:MID_CH] = jnp.where(row == 0, 0.0, pltpu.roll(values, 1, 0)).astype(bf16)
         h_ref[0, t, at, MID_CH : 2 * MID_CH] = here
         h_ref[1, t, at, 0:MID_CH] = here
         h_ref[1, t, at, MID_CH : 2 * MID_CH] = jnp.where(row == W - 1, 0.0, pltpu.roll(values, W - 1, 0)).astype(bf16)
 
-    def keep_last(j):
-        own = slice(W, W + tile)
-        fresh = h_ref[1, jnp.maximum(j + live - 2, 0), own, 0:MID_CH].astype(f32)
-        fn_ref[j] = jnp.where(j + live == 1, fc_ref[1].astype(f32), fresh).astype(bf16)
+    for t in range(FMAX):
+        patches(t)
+        linear(t)
+    for copy in small:
+        copy.wait()
+    live = counts_ref[assign_ref[place // per_group]]
+    fold, member = spread_of_cells()
+    for j in range(2):
         latest = window_ref[:, pl.ds(pl.multiple_of((j + live) * per_frame + 2 * W, 2 * W), tile)].astype(f32)
         latest = jnp.concatenate([latest[:, y * W : (y + 1) * W] for y in range(ROWS_DEV)], axis=0).astype(bf16)
         wide = lax.dot_general(latest, fold, (((1,), (1,)), ((), ())), preferred_element_type=f32)
         wide = jnp.where(member[None], wide.reshape(ROWS_DEV, LAT_CH, W * LAT_CH), 0.0)
         ln_ref[j] = jnp.sum(wide, axis=1).astype(bf16)
-
-    def finish(t, py):
-        ready = []
-        for px in range(2):
-            total = sums_ref[t, px, py] + (part_ref[t, px, py] if t < 2 else 0.0) + bias2
-            ready.append(jnp.where(t < live, total, 0.0).astype(bf16))
-        for pair in range(ROWS_DEV // 2):
-            part = slice(pair * 2 * W, (pair + 1) * 2 * W)
-            joined = jnp.concatenate([ready[0][:, part], ready[1][:, part]], axis=1)
-            woven = jnp.dot(joined, weave, preferred_element_type=f32).astype(bf16)
-            for line in range(2):
-                frames_ref[t, 2 * (2 * pair + line) + py] = woven[:, line * 2 * W : (line + 1) * 2 * W]
-
-    for t in range(FMAX):
-        linear(t)
+    kept = [pltpu.make_async_copy(ln_ref, ln_hbm, keep_sem.at[0])]
+    kept[0].start()
     for y in range(rows):
         activate(0, y)
     block = tile
@@ -468,28 +457,50 @@
     parity, line, cell = source // (2 * W), source // W % 2, source % W
     weave = (target == line * 2 * W + cell * 2 + parity).astype(bf16)
     bias2 = jnp.transpose(jnp.broadcast_to(b2_ref[...].reshape(1, OUT_CH), (8, OUT_CH)))[:, 0:1]
-    fold, member = spread_of_cells()
-    done = [pltpu.make_async_copy(frames_ref.at[t], out_hbm.at[t], out_sem.at[t]) for t in range(FMAX)]
+    started = set()
+    done = []
+    own = slice(W, W + tile)
     for frame in range(FMAX):
         times = tuple(range(2, frame - 1, -1))
-        started = set() if frame == 0 else {0, 1, 2}
-
-        @pl.loop(0, 2)
-        def _(i):
+        for px in range(2):
             for r in range(3):
-                add_products(sums_ref, h_ref, upper_ref, middle_ref, lower_ref, i, frame, frame, 3 - frame, times, started, (r,))
+                add_products(sums_ref, h_ref, upper_ref, middle_ref, lower_ref, px, frame, frame, 3 - frame, times, started, (r,))
                 if frame + 1 < FMAX:
-                    activate(frame + 1, i * 3 + r)
-            if frame > 0:
-                finish(frame - 1, i)
-            if frame == FMAX - 1:
-                keep_last(i)
-
-        if frame > 0:
-            done[frame - 1].start()
-    for py in range(2):
-        finish(FMAX - 1, py)
-    done[FMAX - 1].start()
+                    activate(frame + 1, px * 3 + r)
+        started = {0, 1, 2}
+        t = frame
+        for py in range(2):
+            ready = []
+            for px in range(2):
+                total = sums_ref[t, px, py] + (part_ref[t, px, py] if t < 2 else 0.0) + bias2
+                ready.append(jnp.where(t < live, total, 0.0).astype(bf16))
+            for pair in range(ROWS_DEV // 2):
+                part = slice(pair * 2 * W, (pair + 1) * 2 * W)
+                joined = jnp.concatenate([ready[0][:, part], ready[1][:, part]], axis=1)
+                woven = jnp.dot(joined, weave, preferred_element_type=f32).astype(bf16)
+                for line in range(2):
+                    at = 2 * (2 * pair + line) + py
+                    frames_ref[t, at] = woven[:, line * 2 * W : (line + 1) * 2 * W]
+                    if t == FMAX - 1:
+                        done.append(pltpu.make_async_copy(frames_ref.at[t, at], out_hbm.at[t, at], last_sem.at[at]))
+                        done[-1].start()
+        if t < FMAX - 1:
+            done.append(pltpu.make_async_copy(frames_ref.at[t], out_hbm.at[t], out_sem.at[t]))
+            done[-1].start()
+        if frame == FMAX - 2:
+            @pl.when(live == 1)
+            def _():
+                pltpu.make_async_copy(fc_ref.at[1], fn_hbm.at[0], keep_sem.at[1]).start()
+
+            @pl.when(live > 1)
+            def _():
+                pltpu.make_async_copy(h_ref.at[1, jnp.maximum(live - 2, 0), own, 0:MID_CH], fn_hbm.at[0], keep_sem.at[1]).start()
+
+            kept.append(pltpu.make_async_copy(fc_ref.at[1], fn_hbm.at[0], keep_sem.at[1]))
+            kept.append(pltpu.make_async_copy(h_ref.at[1, live - 1, own, 0:MID_CH], fn_hbm.at[1], keep_sem.at[2]))
+            kept[-1].start()
+    for copy in kept:
+        copy.wait()
     for copy in done:
         copy.wait()
 
@@ -506,23 +517,21 @@
             jax.ShapeDtypeStruct((2, ROWS_DEV, W * LAT_CH), bf16),
             jax.ShapeDtypeStruct((2, ROWS_DEV * W, MID_CH), bf16),
         ),
-        in_specs=[hbm, hbm, vm] + [hbm] * 4 + [vm] * 4 + [hbm],
-        out_specs=(hbm, vm, vm),
+        in_specs=[hbm, hbm] + [vm] * 10,
+        out_specs=(hbm, hbm, hbm),
         scratch_shapes=[
             pltpu.SMEM((REQS,), jnp.int32),
             pltpu.SMEM((REQS,), jnp.int32),
-            pltpu.VMEM((27 * LAT_CH, MID_CH), bf16),
-            pltpu.VMEM((MID_CH,), f32),
-            pltpu.VMEM((MID_CH,), f32),
-            pltpu.VMEM((2, ROWS_DEV * W, MID_CH), bf16),
             pltpu.VMEM((FMAX, 2, 2, OUT_CH, ROWS_DEV * W), f32),
-            pltpu.VMEM((OUT_CH,), f32),
             pltpu.VMEM((27 * LAT_CH, FMAX * cells), bf16),
             pltpu.VMEM((FMAX, cells, MID_CH), f32),
             pltpu.VMEM((2, FMAX, cells, 2 * MID_CH), bf16),
             pltpu.VMEM((FMAX, 2 * ROWS_DEV, OUT_CH, 2 * W), bf16),
-            pltpu.SemaphoreType.DMA((7,)),
+            pltpu.VMEM((2, ROWS_DEV, W * LAT_CH), bf16),
+            pltpu.SemaphoreType.DMA((2,)),
             pltpu.SemaphoreType.DMA((FMAX,)),
+            pltpu.SemaphoreType.DMA((2 * ROWS_DEV,)),
+            pltpu.SemaphoreType.DMA((3,)),
         ],
         compiler_params=pltpu.CompilerParams(vmem_limit_bytes=28 * 1024 * 1024),
         cost_estimate=pl.CostEstimate(flops=4_500_000_000, bytes_accessed=11_000_000, transcendentals=442368),

time: 52.3 us -> 48.9 us (0.935)
  Pallas kernels: 51.5 us -> 47.8 us
    pallas_call x1, Pallas kernels: 11.3 us -> 7.45 us  [decode(): pl.pallas_call(functools.partial(decode_kernel, per_group, 'seq'), out_sh...]
where the time goes in v6:
time: 48.9 us; the launch traced here: 48.8 us
  Pallas kernels  47.8 us (98%)
  between operations  0.91 us (2%)
    pallas_call x1, Pallas kernels, gather(): pl.pallas_call(functools.partial(gather_kernel, devices), out_shape=(jax....  40.4 us
    pallas_call x1, Pallas kernels, decode(): pl.pallas_call(functools.partial(decode_kernel, per_group, 'seq'), out_sh...  7.45 us

profile of v6, /device:TPU:40, one launch (start us, length us, event | category | flops | bytes accessed | tf_op | source)
XLA Modules:
  0.0 48.8 jit_solution(8822487715296718492)
XLA Ops:
  0.6 0.0 copy-start
  0.6 0.0 copy-start.1
  0.7 0.0 copy-start.2
  0.7 0.0 copy-start.3
  0.7 0.0 copy-start.4
  0.7 0.0 copy-start.5
  0.7 0.0 copy-start.6
  0.7 40.4 %shard_map.130 = (bf16[16,2560]{1,0:T(8,128)(2,1)S(1)}, bf16[2,3,192,768]{3,2,1,0:T(8,128)(2,1)S(1)}, bf16[2,3,384,768]{3,2,1,0:T(8,128)(2,1)S(1)}, bf16[2,3,192...) custom-call(s32[8]{0:T(128)} %assign_hbm.3, s32[128,768]{1,0:T(8,128)} %layout_hbm.1, bf16[16,768]{1,0:T(8,128)(2,1)} %latents_hbm.1, ...), custom_call_target="tpu_custom_call" | custom-call | flops 3000000000 | bytes 13000000 | tf_op jit(solution)/shard_map/pallas_call | solution.py:323
  41.1 0.0 copy-done
  41.1 0.0 copy-done.1
  41.1 0.0 copy-done.2
  41.1 0.0 copy-done.3
  41.1 0.0 copy-done.4
  41.1 0.0 copy-done.5
  41.2 0.0 copy-done.6
  41.2 7.4 %shard_map.131 = (bf16[3,8,192,128]{3,2,1,0:T(8,128)(2,1)}, bf16[2,4,1024]{2,1,0:T(4,128)(2,1)}, bf16[2,256,384]{2,1,0:T(8,128)(2,1)}) custom-call(s32[8]{0:T(128)S(1)} %copy-done.5, s32[8]{0:T(128)S(1)} %copy-done.6, bf16[16,2560]{1,0:T(8,128)(2,1)S(1)} %get-tuple-element.11.window_ref, bf16[432,384]{1,0:T(8,128)(2,1)S(1)} %bitcast.9, f32[384]{0:T(512)S(1)} %copy-done.2, ...), custom_call_target="tpu_custom_call" | custom-call | flops 4499999744 | bytes 11000000 | tf_op jit(solution)/shard_map/pallas_call | solution.py:513
Async XLA Ops:
  0.6 40.5 %copy-start = (bf16[2,4,64,384]{3,2,1,0:T(8,128)(2,1)S(1)}, bf16[2,4,64,384]{3,2,1,0:T(8,128)(2,1)}, u32[]{:S(2)}) copy-start(bf16[2,4,64,384]{3,2,1,0:T(8,128)(2,1)} %param.16) | copy-start | bytes 1179652
  0.6 40.5 %copy-start.1 = (bf16[3,3,3,16,384]{4,3,2,1,0:T(8,128)(2,1)S(1)}, bf16[3,3,3,16,384]{4,3,2,1,0:T(8,128)(2,1)}, u32[]{:S(2)}) copy-start(bf16[3,3,3,16,384]{4,3,2,1,0:T(8,128)(2,1)} %param.17) | copy-start | bytes 995332
  0.7 40.5 %copy-start.2 = (f32[384]{0:T(512)S(1)}, f32[384]{0:T(512)}, u32[]{:S(2)}) copy-start(f32[384]{0:T(512)} %b1_ref.1) | copy-start | bytes 4612
  0.7 40.5 %copy-start.3 = (f32[384]{0:T(512)S(1)}, f32[384]{0:T(512)}, u32[]{:S(2)}) copy-start(f32[384]{0:T(512)} %gain_ref.1) | copy-start | bytes 4612
  0.7 40.5 %copy-start.4 = (f32[192]{0:T(256)S(1)}, f32[192]{0:T(256)}, u32[]{:S(2)}) copy-start(f32[192]{0:T(256)} %b2_ref.1) | copy-start | bytes 2308
  0.7 40.5 %copy-start.5 = (s32[8]{0:T(128)S(1)}, s32[8]{0:T(128)}, u32[]{:S(2)}) copy-start(s32[8]{0:T(128)} %assign_hbm.3) | copy-start | bytes 100
  0.7 40.5 %copy-start.6 = (s32[8]{0:T(128)S(1)}, s32[8]{0:T(128)}, u32[]{:S(2)}) copy-start(s32[8]{0:T(128)} %counts_hbm.1) | copy-start | bytes 100

commit v7 on v6

--- a/solution.py
+++ b/solution.py
@@ -146,7 +146,7 @@
 
     @pl.when(first)
     def _():
-        signal(barrier, behind)
+        signal(barrier, (behind + devices - 1) % devices)
 
     row_of = lax.broadcasted_iota(i32, (tile_cells // 3, tile_cells // 3), 0)
     lane_of = lax.broadcasted_iota(i32, (tile_cells // 3, tile_cells // 3), 1)
@@ -179,7 +179,7 @@
 
     @pl.when(even)
     def _():
-        pl.semaphore_wait(barrier, plane - 1 + jnp.where(first, 1, 0))
+        pl.semaphore_wait(barrier, plane - 1 + jnp.where(jnp.logical_or(first, p == plane - 2), 1, 0))
         signal(plane_ok, me + 1)
 
     @pl.when(jnp.logical_not(even))
@@ -194,6 +194,16 @@
             device_id=(rep, z * plane + q), device_id_type=pl.DeviceIdType.MESH))
         near[-1].start()
     recv1_ref[p] = send1_ref[p]
+
+    loads[4].wait()
+    sides = []
+    for side in range(2):
+        sides.append(pltpu.make_async_remote_copy(
+            src_ref=features_ref.at[:, pl.ds((ROWS_DEV - 1) * W * (1 - side), W)],
+            dst_ref=(above_ref, below_ref)[side],
+            send_sem=sf.at[side], recv_sem=rf.at[side],
+            device_id=(rep, (ahead, behind)[side]), device_id_type=pl.DeviceIdType.MESH))
+        sides[-1].start()
 
     my_place = (me + per_group // 2) % devices
     my_group, position = my_place // per_group, my_place % per_group
@@ -230,7 +240,7 @@
 
     @pl.when(jnp.logical_not(even))
     def _():
-        pl.semaphore_wait(barrier, 2 * (planes - 1) + jnp.where(final, 1, 0))
+        pl.semaphore_wait(barrier, 2 * (planes - 1))
         signal(far_ok, me - 1)
 
     @pl.when(even)
@@ -245,16 +255,6 @@
             device_id=(rep, q * plane + p), device_id_type=pl.DeviceIdType.MESH))
         far[-1].start()
     recv2_ref[z] = send2_ref[z]
-    loads[4].wait()
-    sides = []
-    for side in range(2):
-        sides.append(pltpu.make_async_remote_copy(
-            src_ref=features_ref.at[:, pl.ds((ROWS_DEV - 1) * W * (1 - side), W)],
-            dst_ref=(above_ref, below_ref)[side],
-            send_sem=sf.at[side], recv_sem=rf.at[side],
-            device_id=(rep, (ahead, behind)[side]), device_id_type=pl.DeviceIdType.MESH))
-        sides[-1].start()
-
     loads[3].wait()
     wide = cache_ref[...].astype(f32).reshape(2 * ROWS_DEV, W * LAT_CH)
     fold, member = spread_of_cells()
@@ -410,7 +410,7 @@
                     xs_ref[k : k + LAT_CH, t * cells : (t + 1) * cells] = source[:, at : at + cells]
 
     bias = b1_ref[...].reshape(1, MID_CH)
-    gain = gain_ref[...].reshape(1, MID_CH)
+    half_gain = 0.5 * gain_ref[...].reshape(1, MID_CH)
     row = lax.broadcasted_iota(jnp.int32, (W, MID_CH), 0)
 
     def linear(t):
@@ -421,7 +421,7 @@
     def activate(t, y):
         pre = pre_ref[t, y * W : (y + 1) * W, :] + bias
         inverse = lax.rsqrt(jnp.mean(pre * pre, axis=1, keepdims=True) + 1e-06)
-        half = 0.5 * (pre * inverse * gain)
+        half = pre * inverse * half_gain
         values = half + half * jnp.tanh(half)
         if y == 0:
             values = jnp.where(position == 0, 0.0, values)
@@ -459,31 +459,34 @@
     bias2 = jnp.transpose(jnp.broadcast_to(b2_ref[...].reshape(1, OUT_CH), (8, OUT_CH)))[:, 0:1]
     started = set()
     done = []
+    def finish(t, py):
+        ready = []
+        for px in range(2):
+            total = sums_ref[t, px, py] + (part_ref[t, px, py] if t < 2 else 0.0) + bias2
+            ready.append(jnp.where(t < live, total, 0.0).astype(bf16))
+        for pair in range(ROWS_DEV // 2):
+            part = slice(pair * 2 * W, (pair + 1) * 2 * W)
+            joined = jnp.concatenate([ready[0][:, part], ready[1][:, part]], axis=1)
+            woven = jnp.dot(joined, weave, preferred_element_type=f32).astype(bf16)
+            for line in range(2):
+                at = 2 * (2 * pair + line) + py
+                frames_ref[t, at] = woven[:, line * 2 * W : (line + 1) * 2 * W]
+                if t == FMAX - 1:
+                    done.append(pltpu.make_async_copy(frames_ref.at[t, at], out_hbm.at[t, at], last_sem.at[at]))
+                    done[-1].start()
+
     own = slice(W, W + tile)
     for frame in range(FMAX):
         times = tuple(range(2, frame - 1, -1))
-        for px in range(2):
-            for r in range(3):
+        for r in range(3):
+            for px in range(2):
                 add_products(sums_ref, h_ref, upper_ref, middle_ref, lower_ref, px, frame, frame, 3 - frame, times, started, (r,))
                 if frame + 1 < FMAX:
-                    activate(frame + 1, px * 3 + r)
+                    activate(frame + 1, r * 2 + px)
+            if r > 0:
+                finish(frame, r - 1)
         started = {0, 1, 2}
         t = frame
-        for py in range(2):
-            ready = []
-            for px in range(2):
-                total = sums_ref[t, px, py] + (part_ref[t, px, py] if t < 2 else 0.0) + bias2
-                ready.append(jnp.where(t < live, total, 0.0).astype(bf16))
-            for pair in range(ROWS_DEV // 2):
-                part = slice(pair * 2 * W, (pair + 1) * 2 * W)
-                joined = jnp.concatenate([ready[0][:, part], ready[1][:, part]], axis=1)
-                woven = jnp.dot(joined, weave, preferred_element_type=f32).astype(bf16)
-                for line in range(2):
-                    at = 2 * (2 * pair + line) + py
-                    frames_ref[t, at] = woven[:, line * 2 * W : (line + 1) * 2 * W]
-                    if t == FMAX - 1:
-                        done.append(pltpu.make_async_copy(frames_ref.at[t, at], out_hbm.at[t, at], last_sem.at[at]))
-                        done[-1].start()
         if t < FMAX - 1:
             done.append(pltpu.make_async_copy(frames_ref.at[t], out_hbm.at[t], out_sem.at[t]))
             done[-1].start()

time: 48.9 us -> 48.5 us (level)
    pallas_call x1, Pallas kernels: 40.4 us -> 39.3 us  [gather(): pl.pallas_call(functools.partial(gather_kernel, devices), out_shape=(jax....]
    pallas_call x1, Pallas kernels: 7.45 us -> 8.12 us  [decode(): pl.pallas_call(functools.partial(decode_kernel, per_group, 'seq'), out_sh...]
where the time goes in v7:
time: 48.5 us; the launch traced here: 48.4 us
  Pallas kernels  47.4 us (98%)
  between operations  0.91 us (2%)
    pallas_call x1, Pallas kernels, gather(): pl.pallas_call(functools.partial(gather_kernel, devices), out_shape=(jax....  39.3 us
    pallas_call x1, Pallas kernels, decode(): pl.pallas_call(functools.partial(decode_kernel, per_group, 'seq'), out_sh...  8.12 us

profile of v7, /device:TPU:40, one launch (start us, length us, event | category | flops | bytes accessed | tf_op | source)
XLA Modules:
  0.0 48.4 jit_solution(13803733168968546484)
XLA Ops:
  0.6 0.0 copy-start
  0.6 0.0 copy-start.1
  0.7 0.0 copy-start.2
  0.7 0.0 copy-start.3
  0.7 0.0 copy-start.4
  0.7 0.0 copy-start.5
  0.7 0.0 copy-start.6
  0.7 39.3 %shard_map.130 = (bf16[16,2560]{1,0:T(8,128)(2,1)S(1)}, bf16[2,3,192,768]{3,2,1,0:T(8,128)(2,1)S(1)}, bf16[2,3,384,768]{3,2,1,0:T(8,128)(2,1)S(1)}, bf16[2,3,192...) custom-call(s32[8]{0:T(128)} %assign_hbm.3, s32[128,768]{1,0:T(8,128)} %layout_hbm.1, bf16[16,768]{1,0:T(8,128)(2,1)} %latents_hbm.1, ...), custom_call_target="tpu_custom_call" | custom-call | flops 3000000000 | bytes 13000000 | tf_op jit(solution)/shard_map/pallas_call | solution.py:323
  40.0 0.0 copy-done
  40.0 0.0 copy-done.1
  40.1 0.0 copy-done.2
  40.1 0.0 copy-done.3
  40.1 0.0 copy-done.4
  40.1 0.0 copy-done.5
  40.1 0.0 copy-done.6
  40.1 8.1 %shard_map.131 = (bf16[3,8,192,128]{3,2,1,0:T(8,128)(2,1)}, bf16[2,4,1024]{2,1,0:T(4,128)(2,1)}, bf16[2,256,384]{2,1,0:T(8,128)(2,1)}) custom-call(s32[8]{0:T(128)S(1)} %copy-done.5, s32[8]{0:T(128)S(1)} %copy-done.6, bf16[16,2560]{1,0:T(8,128)(2,1)S(1)} %get-tuple-element.11.window_ref, bf16[432,384]{1,0:T(8,128)(2,1)S(1)} %bitcast.9, f32[384]{0:T(512)S(1)} %copy-done.2, ...), custom_call_target="tpu_custom_call" | custom-call | flops 4499999744 | bytes 11000000 | tf_op jit(solution)/shard_map/pallas_call | solution.py:516
Async XLA Ops:
  0.6 39.4 %copy-start = (bf16[2,4,64,384]{3,2,1,0:T(8,128)(2,1)S(1)}, bf16[2,4,64,384]{3,2,1,0:T(8,128)(2,1)}, u32[]{:S(2)}) copy-start(bf16[2,4,64,384]{3,2,1,0:T(8,128)(2,1)} %param.16) | copy-start | bytes 1179652
  0.6 39.4 %copy-start.1 = (bf16[3,3,3,16,384]{4,3,2,1,0:T(8,128)(2,1)S(1)}, bf16[3,3,3,16,384]{4,3,2,1,0:T(8,128)(2,1)}, u32[]{:S(2)}) copy-start(bf16[3,3,3,16,384]{4,3,2,1,0:T(8,128)(2,1)} %param.17) | copy-start | bytes 995332
  0.7 39.4 %copy-start.2 = (f32[384]{0:T(512)S(1)}, f32[384]{0:T(512)}, u32[]{:S(2)}) copy-start(f32[384]{0:T(512)} %b1_ref.1) | copy-start | bytes 4612
  0.7 39.4 %copy-start.3 = (f32[384]{0:T(512)S(1)}, f32[384]{0:T(512)}, u32[]{:S(2)}) copy-start(f32[384]{0:T(512)} %gain_ref.1) | copy-start | bytes 4612
  0.7 39.4 %copy-start.4 = (f32[192]{0:T(256)S(1)}, f32[192]{0:T(256)}, u32[]{:S(2)}) copy-start(f32[192]{0:T(256)} %b2_ref.1) | copy-start | bytes 2308
  0.7 39.4 %copy-start.5 = (s32[8]{0:T(128)S(1)}, s32[8]{0:T(128)}, u32[]{:S(2)}) copy-start(s32[8]{0:T(128)} %assign_hbm.3) | copy-start | bytes 100
  0.7 39.4 %copy-start.6 = (s32[8]{0:T(128)S(1)}, s32[8]{0:T(128)}, u32[]{:S(2)}) copy-start(s32[8]{0:T(128)} %counts_hbm.1) | copy-start | bytes 100

commit v8 on v6

--- a/solution.py
+++ b/solution.py
@@ -146,7 +146,7 @@
 
     @pl.when(first)
     def _():
-        signal(barrier, behind)
+        signal(barrier, (behind + devices - 1) % devices)
 
     row_of = lax.broadcasted_iota(i32, (tile_cells // 3, tile_cells // 3), 0)
     lane_of = lax.broadcasted_iota(i32, (tile_cells // 3, tile_cells // 3), 1)
@@ -179,7 +179,7 @@
 
     @pl.when(even)
     def _():
-        pl.semaphore_wait(barrier, plane - 1 + jnp.where(first, 1, 0))
+        pl.semaphore_wait(barrier, plane - 1 + jnp.where(jnp.logical_or(first, p == plane - 2), 1, 0))
         signal(plane_ok, me + 1)
 
     @pl.when(jnp.logical_not(even))
@@ -194,6 +194,16 @@
             device_id=(rep, z * plane + q), device_id_type=pl.DeviceIdType.MESH))
         near[-1].start()
     recv1_ref[p] = send1_ref[p]
+
+    loads[4].wait()
+    sides = []
+    for side in range(2):
+        sides.append(pltpu.make_async_remote_copy(
+            src_ref=features_ref.at[:, pl.ds((ROWS_DEV - 1) * W * (1 - side), W)],
+            dst_ref=(above_ref, below_ref)[side],
+            send_sem=sf.at[side], recv_sem=rf.at[side],
+            device_id=(rep, (ahead, behind)[side]), device_id_type=pl.DeviceIdType.MESH))
+        sides[-1].start()
 
     my_place = (me + per_group // 2) % devices
     my_group, position = my_place // per_group, my_place % per_group
@@ -230,7 +240,7 @@
 
     @pl.when(jnp.logical_not(even))
     def _():
-        pl.semaphore_wait(barrier, 2 * (planes - 1) + jnp.where(final, 1, 0))
+        pl.semaphore_wait(barrier, 2 * (planes - 1))
         signal(far_ok, me - 1)
 
     @pl.when(even)
@@ -245,16 +255,6 @@
             device_id=(rep, q * plane + p), device_id_type=pl.DeviceIdType.MESH))
         far[-1].start()
     recv2_ref[z] = send2_ref[z]
-    loads[4].wait()
-    sides = []
-    for side in range(2):
-        sides.append(pltpu.make_async_remote_copy(
-            src_ref=features_ref.at[:, pl.ds((ROWS_DEV - 1) * W * (1 - side), W)],
-            dst_ref=(above_ref, below_ref)[side],
-            send_sem=sf.at[side], recv_sem=rf.at[side],
-            device_id=(rep, (ahead, behind)[side]), device_id_type=pl.DeviceIdType.MESH))
-        sides[-1].start()
-
     loads[3].wait()
     wide = cache_ref[...].astype(f32).reshape(2 * ROWS_DEV, W * LAT_CH)
     fold, member = spread_of_cells()

time: 48.9 us -> 47.8 us (0.978)
  Pallas kernels: 47.8 us -> 46.8 us
    pallas_call x1, Pallas kernels: 40.4 us -> 39.3 us  [gather(): pl.pallas_call(functools.partial(gather_kernel, devices), out_shape=(jax....]
where the time goes in v8:
time: 47.8 us; the launch traced here: 47.7 us
  Pallas kernels  46.8 us (98%)
  between operations  0.91 us (2%)
    pallas_call x1, Pallas kernels, gather(): pl.pallas_call(functools.partial(gather_kernel, devices), out_shape=(jax....  39.3 us
    pallas_call x1, Pallas kernels, decode(): pl.pallas_call(functools.partial(decode_kernel, per_group, 'seq'), out_sh...  7.45 us

profile of v8, /device:TPU:40, one launch (start us, length us, event | category | flops | bytes accessed | tf_op | source)
XLA Modules:
  0.0 47.7 jit_solution(16790061820621310082)
XLA Ops:
  0.6 0.0 copy-start
  0.6 0.0 copy-start.1
  0.7 0.0 copy-start.2
  0.7 0.0 copy-start.3
  0.7 0.0 copy-start.4
  0.7 0.0 copy-start.5
  0.7 0.0 copy-start.6
  0.7 39.3 %shard_map.130 = (bf16[16,2560]{1,0:T(8,128)(2,1)S(1)}, bf16[2,3,192,768]{3,2,1,0:T(8,128)(2,1)S(1)}, bf16[2,3,384,768]{3,2,1,0:T(8,128)(2,1)S(1)}, bf16[2,3,192...) custom-call(s32[8]{0:T(128)} %assign_hbm.3, s32[128,768]{1,0:T(8,128)} %layout_hbm.1, bf16[16,768]{1,0:T(8,128)(2,1)} %latents_hbm.1, ...), custom_call_target="tpu_custom_call" | custom-call | flops 3000000000 | bytes 13000000 | tf_op jit(solution)/shard_map/pallas_call | solution.py:323
  40.0 0.0 copy-done
  40.0 0.0 copy-done.1
  40.1 0.0 copy-done.2
  40.1 0.0 copy-done.3
  40.1 0.0 copy-done.4
  40.1 0.0 copy-done.5
  40.1 0.0 copy-done.6
  40.1 7.5 %shard_map.131 = (bf16[3,8,192,128]{3,2,1,0:T(8,128)(2,1)}, bf16[2,4,1024]{2,1,0:T(4,128)(2,1)}, bf16[2,256,384]{2,1,0:T(8,128)(2,1)}) custom-call(s32[8]{0:T(128)S(1)} %copy-done.5, s32[8]{0:T(128)S(1)} %copy-done.6, bf16[16,2560]{1,0:T(8,128)(2,1)S(1)} %get-tuple-element.11.window_ref, bf16[432,384]{1,0:T(8,128)(2,1)S(1)} %bitcast.9, f32[384]{0:T(512)S(1)} %copy-done.2, ...), custom_call_target="tpu_custom_call" | custom-call | flops 4499999744 | bytes 11000000 | tf_op jit(solution)/shard_map/pallas_call | solution.py:513
Async XLA Ops:
  0.6 39.4 %copy-start = (bf16[2,4,64,384]{3,2,1,0:T(8,128)(2,1)S(1)}, bf16[2,4,64,384]{3,2,1,0:T(8,128)(2,1)}, u32[]{:S(2)}) copy-start(bf16[2,4,64,384]{3,2,1,0:T(8,128)(2,1)} %param.16) | copy-start | bytes 1179652
  0.6 39.4 %copy-start.1 = (bf16[3,3,3,16,384]{4,3,2,1,0:T(8,128)(2,1)S(1)}, bf16[3,3,3,16,384]{4,3,2,1,0:T(8,128)(2,1)}, u32[]{:S(2)}) copy-start(bf16[3,3,3,16,384]{4,3,2,1,0:T(8,128)(2,1)} %param.17) | copy-start | bytes 995332
  0.7 39.4 %copy-start.2 = (f32[384]{0:T(512)S(1)}, f32[384]{0:T(512)}, u32[]{:S(2)}) copy-start(f32[384]{0:T(512)} %b1_ref.1) | copy-start | bytes 4612
  0.7 39.4 %copy-start.3 = (f32[384]{0:T(512)S(1)}, f32[384]{0:T(512)}, u32[]{:S(2)}) copy-start(f32[384]{0:T(512)} %gain_ref.1) | copy-start | bytes 4612
  0.7 39.4 %copy-start.4 = (f32[192]{0:T(256)S(1)}, f32[192]{0:T(256)}, u32[]{:S(2)}) copy-start(f32[192]{0:T(256)} %b2_ref.1) | copy-start | bytes 2308
  0.7 39.4 %copy-start.5 = (s32[8]{0:T(128)S(1)}, s32[8]{0:T(128)}, u32[]{:S(2)}) copy-start(s32[8]{0:T(128)} %assign_hbm.3) | copy-start | bytes 100
  0.7 39.4 %copy-start.6 = (s32[8]{0:T(128)S(1)}, s32[8]{0:T(128)}, u32[]{:S(2)}) copy-start(s32[8]{0:T(128)} %counts_hbm.1) | copy-start | bytes 100
